TPU v7x, 32 devices: a whole 2x2x4 slice. The times are simulated.
32 devices in a mesh: aper: 2 (over x), rng: 4 (over z), ang: 4 (over y, core).
Axes of the slice: x: 2, y: 2, z: 4, core: 2. Of those that a mesh axis runs over, the one named last changes fastest.
Arguments:
- subimages: bfloat16 [8, 2, 1024, 512], P('aper', None, 'ang', 'rng'), may hold values from -6 to 6
- beam_offsets: int32 [3, 2, 2, 1024], P(None, None, None, 'ang'), may hold values from -4 to 0
- range_offsets: int32 [3, 2, 2, 1024], P(None, None, None, 'ang'), may hold values from -4 to 3
- beam_taps: bfloat16 [3, 2, 2, 4, 1024], P(None, None, None, None, 'ang'), may hold values from 0.14941406 to 0.59765625
- range_frac: float32 [3, 2, 2, 1024], P(None, None, None, 'ang'), may hold values from 0 to 1
- phase_base: float32 [8, 3, 2, 1024], P('aper', None, None, 'ang'), may hold values from -3.140625 to 3.140625
- phase_rate: float32 [3, 2, 1024], P(None, None, 'ang'), may hold values from -6 to 6
- final_phase: float32 [8, 1024], P(None, 'ang'), may hold values from -3.140625 to 3.140625
Outputs:
- image: float32 [2, 4, 256, 512], P(None, 'ang', 'aper', 'rng')
Inputs may be any that keep to these rules, and one draw needn't show every extreme that they name: `beam_offsets`: the taps of parent beam p read child beams p + offset to p + offset + 3. `range_offsets`: range bin r reads the bins r + offset and r + offset + 1.
All inputs are finite; a program needn't handle non-finite values.
Results may differ from a plain program's by a relative error of at most 0.0046.
Values may be sent and summed in bfloat16 or wider, within the bound.
No kernel may reach another device: no remote copies, remote signals or barrier semaphores. Data moves between devices by JAX's collectives and lax.ppermute only.
A program may use at most 64 MiB of HBM per device.

v0:
```python
import math

import jax
import jax.numpy as jnp
from jax import lax
from jax.sharding import PartitionSpec as P

LEVELS = 3
TAPS = 4
HALO = 4


def with_halo(cells, sides, width):
    for axis, dim in sides:
        count = lax.axis_size(axis)
        ends = count - 1
        head = lax.slice_in_dim(cells, 0, width, axis=dim)
        tail = lax.slice_in_dim(cells, cells.shape[dim] - width, cells.shape[dim], axis=dim)
        cells = jnp.concatenate(
            [
                lax.ppermute(tail, axis, [(i, (i + 1) % count) for i in range(ends)]),
                cells,
                lax.ppermute(head, axis, [((i + 1) % count, i) for i in range(ends)]),
            ],
            axis=dim,
        )
    return cells


def partner_2(x, axis, stride):
    return lax.ppermute(x, axis, [(i, i ^ 1 << stride) for i in range(lax.axis_size(axis))])


def block_edges(blocks):
    return with_halo(blocks, (("ang", 2), ("rng", 3)), HALO)


def band_matrices(offsets, tap_weights):
    beam_count = offsets.shape[1]
    columns = jnp.arange(beam_count + 2 * HALO, dtype=jnp.int32)
    row_ids = jnp.arange(beam_count, dtype=jnp.int32)
    starting = row_ids[None, :] + HALO + offsets
    lagging = columns[None, None, :] - starting[:, :, None]
    weights = jnp.zeros(lagging.shape, jnp.float32)
    for tap_idx in range(TAPS):
        weights = weights + jnp.where(
            lagging == tap_idx, tap_weights[:, tap_idx, :, None].astype(jnp.float32), 0.0
        )
    return weights.astype(jnp.bfloat16)


def merge_level(child_blocks, halves, level_idx, tables, range_ramp):
    beam_offsets, range_offsets, beam_taps, range_frac, phase_base, phase_rate = tables
    slot_count = halves.shape[0]
    cell_count = range_ramp.shape[0]
    slot_ids = jnp.arange(slot_count, dtype=jnp.int32)
    summed = None
    for side_idx in range(2):
        child_ids = halves if side_idx == 0 else 1 - halves
        extended = child_blocks[side_idx]
        matrices = band_matrices(
            beam_offsets[level_idx][child_ids, halves], beam_taps[level_idx][child_ids, halves]
        )
        interpolated = jnp.einsum(
            "snm,sxmr->sxnr", matrices, extended, preferred_element_type=jnp.float32
        )
        range_shift = range_offsets[level_idx][child_ids, halves] + HALO
        fraction = range_frac[level_idx][child_ids, halves]
        shifted = jnp.zeros(interpolated.shape[:3] + (cell_count,), jnp.float32)
        for offset_step in range(2 * HALO + 1):
            weight = jnp.where(range_shift == offset_step, 1.0 - fraction, 0.0) + jnp.where(
                range_shift + 1 == offset_step, fraction, 0.0
            )
            shifted = (
                shifted
                + weight[:, None, :, None]
                * interpolated[:, :, :, offset_step : offset_step + cell_count]
            )
        angles = (
            phase_base[slot_ids, level_idx, child_ids][:, :, None]
            + phase_rate[level_idx][child_ids][:, :, None] * range_ramp[None, None, :]
        )
        cosine = jnp.cos(angles)
        sine_part = jnp.sin(angles)
        term = jnp.stack(
            [
                cosine * shifted[:, 0] - sine_part * shifted[:, 1],
                sine_part * shifted[:, 0] + cosine * shifted[:, 1],
            ],
            axis=1,
        )
        summed = term if summed is None else summed + term
    return summed.astype(jnp.bfloat16)


def body(
    subimages,
    beam_offsets,
    range_offsets,
    beam_taps,
    range_frac,
    phase_base,
    phase_rate,
    final_phase,
):
    slot_count = subimages.shape[0]
    beam_count = subimages.shape[2]
    cell_count = subimages.shape[3]
    aper_count = lax.axis_size("aper")
    total_subs = slot_count * aper_count
    aper_pos = lax.axis_index("aper")
    full_range = cell_count * lax.axis_size("rng")
    range_ramp = (
        lax.axis_index("rng") * cell_count + jnp.arange(cell_count, dtype=jnp.int32)
    ).astype(jnp.float32) / full_range - 0.5
    tables = (beam_offsets, range_offsets, beam_taps, range_frac, phase_base, phase_rate)
    sub_ids = aper_pos * slot_count + jnp.arange(slot_count, dtype=jnp.int32)
    current = subimages
    for level_idx in range(LEVELS):
        distance = total_subs >> LEVELS - level_idx
        halves = sub_ids // distance % 2
        if distance >= slot_count:
            which_bit = (distance // slot_count).bit_length() - 1
            partner = partner_2(current, "aper", which_bit)
            joined = block_edges(jnp.concatenate([current, partner], 0))
            own_block = joined[:slot_count]
            other_block = joined[slot_count:]
        else:
            own_block = block_edges(current)
            block_shape = own_block.shape
            paired = own_block.reshape(
                (slot_count // (2 * distance), 2, distance) + block_shape[1:]
            )
            other_block = paired[:, ::-1].reshape(block_shape)
        current = merge_level((own_block, other_block), halves, level_idx, tables, range_ramp)
    scale = 1.0 / math.sqrt(total_subs)
    sector = beam_count // aper_count
    regrouped = lax.all_to_all(current[:, None], "aper", split_axis=3, concat_axis=1, tiled=True)
    angles = lax.dynamic_slice_in_dim(final_phase, aper_pos * sector, sector, 1)
    angles = angles.reshape(aper_count, slot_count, sector).transpose(1, 0, 2)
    cosine = jnp.cos(angles)[:, :, :, None]
    sine_part = jnp.sin(angles)[:, :, :, None]
    real_part = regrouped[:, :, 0].astype(jnp.float32)
    imag_part = regrouped[:, :, 1].astype(jnp.float32)
    summed = jnp.stack(
        [
            jnp.sum(cosine * real_part - sine_part * imag_part, axis=(0, 1)),
            jnp.sum(sine_part * real_part + cosine * imag_part, axis=(0, 1)),
        ]
    )
    image = summed * scale
    return image[:, None]


def solution(mesh):
    in_specs = (
        P("aper", None, "ang", "rng"),
        P(None, None, None, "ang"),
        P(None, None, None, "ang"),
        P(None, None, None, None, "ang"),
        P(None, None, None, "ang"),
        P("aper", None, None, "ang"),
        P(None, None, "ang"),
        P(None, "ang"),
    )
    out_specs = P(None, "ang", "aper", "rng")
    return jax.shard_map(body, mesh=mesh, in_specs=in_specs, out_specs=out_specs, check_vma=False)
```

profile of v0, /device:TPU:12, one launch (start us, length us, event | category | flops | bytes accessed | tf_op | source)
XLA Modules:
  0.0 126.9 jit_solution(14399621808348187095)
XLA Ops:
  0.0 0.8 fusion.219
  1.1 1.9 %collective-permute-start = (bf16[4,2,4,128]{2,3,1,0:T(8,128)(2,1)S(1)}, bf16[4,2,4,128]{2,3,1,0:T(8,128)(2,1)S(1)}, u32[]{:S(2)}, u32[]{:S(2)}) collective-permute-start(bf16[4,2,4,128]{2,3,1,0:T(8,128)(2,1)S(1)} %copy.23), channel_id=1, source_target_pairs={{0,1},{1,2},{2,3},{4,5},{5,6},{6,7},{8,9},{9,10},{10,11},{12,13},{... | collective-permute-start | bytes 24584 | tf_op jit(solution)/shard_map/ppermute | solution.py:21
  3.2 3.6 %collective-permute-start.1 = (bf16[4,2,4,128]{2,3,1,0:T(8,128)(2,1)S(1)}, bf16[4,2,4,128]{2,3,1,0:T(8,128)(2,1)S(1)}, u32[]{:S(2)}, u32[]{:S(2)}) collective-permute-start(bf16[4,2,4,128]{2,3,1,0:T(8,128)(2,1)S(1)} %copy.24), channel_id=1, source_target_pairs={{1,0},{2,1},{3,2},{5,4},{6,5},{7,6},{9,8},{10,9},{11,10},{13,12},{... | collective-permute-start | bytes 24584 | tf_op jit(solution)/shard_map/ppermute | solution.py:23
  7.0 0.7 slice_bitcast_fusion.5
  8.8 0.7 slice_bitcast_fusion.2
  9.6 0.6 gather_fusion.13
  10.2 0.6 gather_fusion.19
  10.8 0.7 slice_bitcast_fusion.13
  12.1 0.6 gather_fusion.16
  12.6 0.7 slice_bitcast_fusion.12
  14.6 0.6 gather_fusion.20
  15.7 0.6 gather_fusion.21
  16.3 0.6 gather_fusion.27
  20.5 0.6 gather_fusion.35
  21.6 3.5 %collective-permute-start.2 = (bf16[4,2,264,4]{2,3,1,0:T(4,128)(2,1)S(1)}, bf16[4,2,264,4]{2,3,1,0:T(4,128)(2,1)S(1)}, u32[]{:S(2)}, u32[]{:S(2)}) collective-permute-start(bf16[4,2,264,4]{2,3,1,0:T(4,128)(2,1)S(1)} %get-tuple-element.25), channel_id=1, source_target_pairs={{0,4},{4,8},{8,12},{1,5},{5,9},{9,13},{2,6},{6,10},{10,14},{3,7},{... | collective-permute-start | bytes 50696 | tf_op jit(solution)/shard_map/ppermute | solution.py:21
  25.1 2.4 %collective-permute-start.3 = (bf16[4,2,264,4]{2,3,1,0:T(4,128)(2,1)S(1)}, bf16[4,2,264,4]{2,3,1,0:T(4,128)(2,1)S(1)}, u32[]{:S(2)}, u32[]{:S(2)}) collective-permute-start(bf16[4,2,264,4]{2,3,1,0:T(4,128)(2,1)S(1)} %get-tuple-element.26), channel_id=1, source_target_pairs={{4,0},{8,4},{12,8},{5,1},{9,5},{13,9},{6,2},{10,6},{14,10},{7,3},{... | collective-permute-start | bytes 50696 | tf_op jit(solution)/shard_map/ppermute | solution.py:23
  28.7 0.6 gather_fusion.14
  29.3 0.6 gather_fusion.8
  30.0 0.9 collective-permute-done.3
  30.9 0.8 pad_maximum_fusion.1
  31.7 0.8 convolution_bitcast_fusion.5
  32.5 0.8 convolution_bitcast_fusion.4
  33.3 1.1 fusion.64
  34.4 1.1 fusion.56
  35.5 4.1 %multiply_subtract_fusion.2 = (f32[4,1,256,128]{2,3,1,0:T(8,128)S(1)}, f32[4,1,256,128]{2,3,1,0:T(8,128)S(1)}, f32[4,1,256,128]{2,3,1,0:T(8,128)S(1)}, f32[4,1,256,128]{2,3,1,0:T(8,128)S(1)}) fusion(f32[4,2,256,128]{2,3,1,0:T(8,128)S(1)} %fusion.56, f32[4,256]{1,0:T(4,128)S(1)} %gather_fusion.15, f32[4,256]{1,0:T(4,128)S(1)} %gather_fusion.14, ...), kind=kLoop, calls=%fused_computation.298 | loop fusion | flops 2097152 | bytes 4211200 | tf_op jit(solution)/shard_map/sub | solution.py:87
  39.9 1.9 %collective-permute-start.4 = (bf16[4,2,4,128]{2,3,1,0:T(8,128)(2,1)S(1)}, bf16[4,2,4,128]{2,3,1,0:T(8,128)(2,1)S(1)}, u32[]{:S(2)}, u32[]{:S(2)}) collective-permute-start(bf16[4,2,4,128]{2,3,1,0:T(8,128)(2,1)S(1)} %get-tuple-element.27), channel_id=1, source_target_pairs={{0,1},{1,2},{2,3},{4,5},{5,6},{6,7},{8,9},{9,10},{10,11},{12,13},{... | collective-permute-start | bytes 24584 | tf_op jit(solution)/shard_map/ppermute | solution.py:21
  41.8 3.6 %collective-permute-start.5 = (bf16[4,2,4,128]{2,3,1,0:T(8,128)(2,1)S(1)}, bf16[4,2,4,128]{2,3,1,0:T(8,128)(2,1)S(1)}, u32[]{:S(2)}, u32[]{:S(2)}) collective-permute-start(bf16[4,2,4,128]{2,3,1,0:T(8,128)(2,1)S(1)} %get-tuple-element.28), channel_id=1, source_target_pairs={{1,0},{2,1},{3,2},{5,4},{6,5},{7,6},{9,8},{10,9},{11,10},{13,12},{... | collective-permute-start | bytes 24584 | tf_op jit(solution)/shard_map/ppermute | solution.py:23
  45.5 2.1 %collective-permute-done.4 = bf16[4,2,4,128]{2,3,1,0:T(8,128)(2,1)S(1)} collective-permute-done((bf16[4,2,4,128]{2,3,1,0:T(8,128)(2,1)S(1)}, bf16[4,2,4,128]{2,3,1,0:T(8,128)(2,1)S(1)}, u32[]{:S(2)}, u32[]{:S(2)}) %collective-permute-start.4) | collective-permute-done | bytes 8224 | tf_op jit(solution)/shard_map/ppermute | solution.py:21
  47.6 1.8 %collective-permute-done.5 = bf16[4,2,4,128]{2,3,1,0:T(8,128)(2,1)S(1)} collective-permute-done((bf16[4,2,4,128]{2,3,1,0:T(8,128)(2,1)S(1)}, bf16[4,2,4,128]{2,3,1,0:T(8,128)(2,1)S(1)}, u32[]{:S(2)}, u32[]{:S(2)}) %collective-permute-start.5) | collective-permute-done | bytes 8224 | tf_op jit(solution)/shard_map/ppermute | solution.py:23
  49.4 3.5 %collective-permute-start.6 = (bf16[4,2,264,4]{2,3,1,0:T(4,128)(2,1)S(1)}, bf16[4,2,264,4]{2,3,1,0:T(4,128)(2,1)S(1)}, u32[]{:S(2)}, u32[]{:S(2)}) collective-permute-start(bf16[4,2,264,4]{2,3,1,0:T(4,128)(2,1)S(1)} %get-tuple-element.23), channel_id=1, source_target_pairs={{0,4},{4,8},{8,12},{1,5},{5,9},{9,13},{2,6},{6,10},{10,14},{3,7},{... | collective-permute-start | bytes 50696 | tf_op jit(solution)/shard_map/ppermute | solution.py:21
  52.9 2.5 %collective-permute-start.7 = (bf16[4,2,264,4]{2,3,1,0:T(4,128)(2,1)S(1)}, bf16[4,2,264,4]{2,3,1,0:T(4,128)(2,1)S(1)}, u32[]{:S(2)}, u32[]{:S(2)}) collective-permute-start(bf16[4,2,264,4]{2,3,1,0:T(4,128)(2,1)S(1)} %get-tuple-element.24), channel_id=1, source_target_pairs={{4,0},{8,4},{12,8},{5,1},{9,5},{13,9},{6,2},{10,6},{14,10},{7,3},{... | collective-permute-start | bytes 50696 | tf_op jit(solution)/shard_map/ppermute | solution.py:23
  55.5 0.6 gather_fusion.29
  57.3 0.6 gather_fusion.22
  57.9 0.6 gather_fusion.4
  58.7 0.8 pad_maximum_fusion.2
  59.5 0.8 convolution_bitcast_fusion.3
  60.3 0.8 convolution_bitcast_fusion.2
  61.1 1.1 fusion.48
  62.2 1.1 fusion.40
  63.3 4.1 %multiply_subtract_fusion = (f32[4,1,256,128]{2,3,1,0:T(8,128)S(1)}, f32[4,1,256,128]{2,3,1,0:T(8,128)S(1)}, f32[4,1,256,128]{2,3,1,0:T(8,128)S(1)}, f32[4,1,256,128]{2,3,1,0:T(8,128)S(1)}) fusion(f32[4,2,256,128]{2,3,1,0:T(8,128)S(1)} %fusion.40, f32[4,256]{1,0:T(4,128)S(1)} %gather_fusion.23, f32[4,256]{1,0:T(4,128)S(1)} %gather_fusion.22, ...), kind=kLoop, calls=%fused_computation.291 | loop fusion | flops 2097152 | bytes 4211200 | tf_op jit(solution)/shard_map/sub | solution.py:87
  67.5 1.6 %collective-permute-start.8 = (bf16[4,2,256,128]{2,3,1,0:T(8,128)(2,1)S(1)}, bf16[4,2,256,128]{2,3,1,0:T(8,128)(2,1)S(1)}, u32[]{:S(2)}, u32[]{:S(2)}) collective-permute-start(bf16[4,2,256,128]{2,3,1,0:T(8,128)(2,1)S(1)} %fusion.73), channel_id=1, source_target_pairs={{0,16},{16,0},{1,17},{17,1},{2,18},{18,2},{3,19},{19,3},{4,20},{20... | collective-permute-start | bytes 1572872 | tf_op jit(solution)/shard_map/ppermute | solution.py:31
  71.5 5.3 %collective-permute-done.8 = bf16[4,2,256,128]{2,3,1,0:T(8,128)(2,1)S(1)} collective-permute-done((bf16[4,2,256,128]{2,3,1,0:T(8,128)(2,1)S(1)}, bf16[4,2,256,128]{2,3,1,0:T(8,128)(2,1)S(1)}, u32[]{:S(2)}, u32[]{:S(2)}) %collective-permute-start.8) | collective-permute-done | bytes 524320 | tf_op jit(solution)/shard_map/ppermute | solution.py:31
  77.1 4.5 %collective-permute-start.10 = (bf16[8,2,4,128]{2,3,1,0:T(8,128)(2,1)S(1)}, bf16[8,2,4,128]{2,3,1,0:T(8,128)(2,1)S(1)}, u32[]{:S(2)}, u32[]{:S(2)}) collective-permute-start(bf16[8,2,4,128]{2,3,1,0:T(8,128)(2,1)S(1)} %get-tuple-element.22), channel_id=1, source_target_pairs={{1,0},{2,1},{3,2},{5,4},{6,5},{7,6},{9,8},{10,9},{11,10},{13,12},{... | collective-permute-start | bytes 49160 | tf_op jit(solution)/shard_map/ppermute | solution.py:23
  81.6 1.9 %collective-permute-start.9 = (bf16[8,2,4,128]{2,3,1,0:T(8,128)(2,1)S(1)}, bf16[8,2,4,128]{2,3,1,0:T(8,128)(2,1)S(1)}, u32[]{:S(2)}, u32[]{:S(2)}) collective-permute-start(bf16[8,2,4,128]{2,3,1,0:T(8,128)(2,1)S(1)} %get-tuple-element.21), channel_id=1, source_target_pairs={{0,1},{1,2},{2,3},{4,5},{5,6},{6,7},{8,9},{9,10},{10,11},{12,13},{... | collective-permute-start | bytes 49160 | tf_op jit(solution)/shard_map/ppermute | solution.py:21
  83.5 4.7 %collective-permute-done.10 = bf16[8,2,4,128]{2,3,1,0:T(8,128)(2,1)S(1)} collective-permute-done((bf16[8,2,4,128]{2,3,1,0:T(8,128)(2,1)S(1)}, bf16[8,2,4,128]{2,3,1,0:T(8,128)(2,1)S(1)}, u32[]{:S(2)}, u32[]{:S(2)}) %collective-permute-start.10) | collective-permute-done | bytes 16416 | tf_op jit(solution)/shard_map/ppermute | solution.py:23
  88.2 3.8 %collective-permute-done.9 = bf16[8,2,4,128]{2,3,1,0:T(8,128)(2,1)S(1)} collective-permute-done((bf16[8,2,4,128]{2,3,1,0:T(8,128)(2,1)S(1)}, bf16[8,2,4,128]{2,3,1,0:T(8,128)(2,1)S(1)}, u32[]{:S(2)}, u32[]{:S(2)}) %collective-permute-start.9) | collective-permute-done | bytes 16416 | tf_op jit(solution)/shard_map/ppermute | solution.py:21
  92.2 3.4 %collective-permute-start.11 = (bf16[8,2,264,4]{2,3,1,0:T(4,128)(2,1)S(1)}, bf16[8,2,264,4]{2,3,1,0:T(4,128)(2,1)S(1)}, u32[]{:S(2)}, u32[]{:S(2)}) collective-permute-start(bf16[8,2,264,4]{2,3,1,0:T(4,128)(2,1)S(1)} %get-tuple-element.7), channel_id=1, source_target_pairs={{0,4},{4,8},{8,12},{1,5},{5,9},{9,13},{2,6},{6,10},{10,14},{3,7},{... | collective-permute-start | bytes 101384 | tf_op jit(solution)/shard_map/ppermute | solution.py:21
  95.6 2.7 %collective-permute-start.12 = (bf16[8,2,264,4]{2,3,1,0:T(4,128)(2,1)S(1)}, bf16[8,2,264,4]{2,3,1,0:T(4,128)(2,1)S(1)}, u32[]{:S(2)}, u32[]{:S(2)}) collective-permute-start(bf16[8,2,264,4]{2,3,1,0:T(4,128)(2,1)S(1)} %get-tuple-element.8), channel_id=1, source_target_pairs={{4,0},{8,4},{12,8},{5,1},{9,5},{13,9},{6,2},{10,6},{14,10},{7,3},{... | collective-permute-start | bytes 101384 | tf_op jit(solution)/shard_map/ppermute | solution.py:23
  99.5 0.6 gather_fusion.30
  100.1 0.6 gather_fusion
  100.7 0.8 collective-permute-done.12
  101.6 1.6 %pad_maximum_fusion = bf16[8,2,264,136]{2,3,1,0:T(8,128)(2,1)S(1)} fusion(bf16[8,2,264,4]{2,3,1,0:T(4,128)(2,1)S(1)} %collective-permute-done.12, bf16[8,2,4,128]{2,3,1,0:T(8,128)(2,1)S(1)} %collective-permute-done.10, bf16[4,2,256,128]{2,3,1,0:T(8,128)(2,1)S(1)} %collective-permute-done.8, bf16[4,2,256,128]{2,3,1,0:T(8,128)(2,1)S(1)} %fusion.73, ...), kind=kLoop, calls=%fused_computation.36 | loop fusion | flops 6893568 | bytes 2297856 | tf_op jit(solution)/shard_map/concatenate | solution.py:19
  103.3 0.8 convolution_bitcast_fusion
  104.1 1.1 fusion.24
  105.2 2.1 %fusion.154 = f32[4,1,1,256,128]{3,4,0,2,1:T(8,128)S(1)} fusion(f32[4,2,256,128]{2,3,0,1:T(8,128)S(1)} %fusion.24, f32[4,256]{1,0:T(4,128)S(1)} %gather_fusion.31, f32[4,256]{1,0:T(4,128)S(1)} %gather_fusion.30, f32[128]{0:T(128)S(1)} %multiply_add_fusion.9), kind=kLoop, calls=%fused_computation.270 | loop fusion | flops 655360 | bytes 1581568 | tf_op jit(solution)/shard_map/stack | solution.py:85
  107.3 0.8 convolution_bitcast_fusion.1
  108.0 1.1 fusion.32
  109.1 4.0 %fusion.165 = (f32[4,1,1,256,128]{3,4,0,2,1:T(8,128)S(1)}, f32[4,1,1,256,128]{3,4,0,2,1:T(8,128)S(1)}, f32[4,1,1,256,128]{3,4,0,2,1:T(8,128)S(1)}) fusion(f32[4,2,256,128]{2,3,0,1:T(8,128)S(1)} %fusion.32, f32[128]{0:T(128)S(1)} %multiply_add_fusion.9, f32[4,256]{1,0:T(4,128)S(1)} %gather_fusion.1, f32[4,256]{1,0:T(4,128)S(1)} %gather_fusion, ...), kind=kLoop, calls=%fused_computation.285 | loop fusion | flops 1703936 | bytes 3686912 | tf_op jit(solution)/shard_map/stack | solution.py:85
  113.3 1.1 copy.32
  114.4 3.5 %all-to-all-start = ((bf16[4,1,2,256,128]{4,0,2,1,3:T(4,128)(2,1)}), bf16[4,1,2,256,128]{4,0,2,1,3:T(4,128)(2,1)S(1)}, u32[]{:S(2)}, u32[]{:S(2)}) async-start(bf16[4,1,2,256,128]{4,0,2,1,3:T(4,128)(2,1)} %copy.32), calls=%async_computation | async-start | bytes 1048576 | tf_op jit(solution)/shard_map/all_to_all | solution.py:138
  118.0 6.5 %all-to-all-done = bf16[4,1,2,256,128]{4,0,2,1,3:T(4,128)(2,1)S(1)} async-done(((bf16[4,1,2,256,128]{4,0,2,1,3:T(4,128)(2,1)}), bf16[4,1,2,256,128]{4,0,2,1,3:T(4,128)(2,1)S(1)}, u32[]{:S(2)}, u32[]{:S(2)}) %all-to-all-start) | async-done | bytes 524320 | tf_op jit(solution)/shard_map/all_to_all | solution.py:138
  124.5 0.6 copy.33
  125.1 1.0 fusion.150
  126.1 0.8 copy.35
  (109 shorter events, 15.7 us)
Async XLA Ops:
  0.0 28.7 %copy-start = (f32[4,3,2,256]{3,2,1,0:T(2,128)S(1)}, f32[4,3,2,256]{3,2,1,0:T(2,128)}, u32[]{:S(2)}) copy-start(f32[4,3,2,256]{3,2,1,0:T(2,128)} %param.13) | copy-start | bytes 73732
  0.0 21.3 %copy-start.1 = (bf16[4,2,256,128]{3,2,1,0:T(8,128)(2,1)S(1)}, bf16[4,2,256,128]{3,2,1,0:T(8,128)(2,1)}, u32[]{:S(2)}) copy-start(bf16[4,2,256,128]{3,2,1,0:T(8,128)(2,1)} %param.8) | copy-start | bytes 1572868
  0.0 20.4 %copy-start.2 = (f32[3,2,256]{2,1,0:T(2,128)S(1)}, f32[3,2,256]{2,1,0:T(2,128)}, u32[]{:S(2)}) copy-start(f32[3,2,256]{2,1,0:T(2,128)} %param.14) | copy-start | bytes 18436
  1.1 20.5 %collective-permute-start = (bf16[4,2,4,128]{2,3,1,0:T(8,128)(2,1)S(1)}, bf16[4,2,4,128]{2,3,1,0:T(8,128)(2,1)S(1)}, u32[]{:S(2)}, u32[]{:S(2)}) collective-permute-start(bf16[4,2,4,128]{2,3,1,0:T(8,128)(2,1)S(1)} %copy.23), channel_id=1, source_target_pairs={{0,1},{1,2},{2,3},{4,5},{5,6},{6,7},{8,9},{9,10},{10,11},{12,13},{... | collective-permute-start | bytes 24584 | tf_op jit(solution)/shard_map/ppermute | solution.py:21
  3.2 18.3 %collective-permute-start.1 = (bf16[4,2,4,128]{2,3,1,0:T(8,128)(2,1)S(1)}, bf16[4,2,4,128]{2,3,1,0:T(8,128)(2,1)S(1)}, u32[]{:S(2)}, u32[]{:S(2)}) collective-permute-start(bf16[4,2,4,128]{2,3,1,0:T(8,128)(2,1)S(1)} %copy.24), channel_id=1, source_target_pairs={{1,0},{2,1},{3,2},{5,4},{6,5},{7,6},{9,8},{10,9},{11,10},{13,12},{... | collective-permute-start | bytes 24584 | tf_op jit(solution)/shard_map/ppermute | solution.py:23
  21.6 8.3 %collective-permute-start.2 = (bf16[4,2,264,4]{2,3,1,0:T(4,128)(2,1)S(1)}, bf16[4,2,264,4]{2,3,1,0:T(4,128)(2,1)S(1)}, u32[]{:S(2)}, u32[]{:S(2)}) collective-permute-start(bf16[4,2,264,4]{2,3,1,0:T(4,128)(2,1)S(1)} %get-tuple-element.25), channel_id=1, source_target_pairs={{0,4},{4,8},{8,12},{1,5},{5,9},{9,13},{2,6},{6,10},{10,14},{3,7},{... | collective-permute-start | bytes 50696 | tf_op jit(solution)/shard_map/ppermute | solution.py:21
  25.1 5.7 %collective-permute-start.3 = (bf16[4,2,264,4]{2,3,1,0:T(4,128)(2,1)S(1)}, bf16[4,2,264,4]{2,3,1,0:T(4,128)(2,1)S(1)}, u32[]{:S(2)}, u32[]{:S(2)}) collective-permute-start(bf16[4,2,264,4]{2,3,1,0:T(4,128)(2,1)S(1)} %get-tuple-element.26), channel_id=1, source_target_pairs={{4,0},{8,4},{12,8},{5,1},{9,5},{13,9},{6,2},{10,6},{14,10},{7,3},{... | collective-permute-start | bytes 50696 | tf_op jit(solution)/shard_map/ppermute | solution.py:23
  39.9 7.7 %collective-permute-start.4 = (bf16[4,2,4,128]{2,3,1,0:T(8,128)(2,1)S(1)}, bf16[4,2,4,128]{2,3,1,0:T(8,128)(2,1)S(1)}, u32[]{:S(2)}, u32[]{:S(2)}) collective-permute-start(bf16[4,2,4,128]{2,3,1,0:T(8,128)(2,1)S(1)} %get-tuple-element.27), channel_id=1, source_target_pairs={{0,1},{1,2},{2,3},{4,5},{5,6},{6,7},{8,9},{9,10},{10,11},{12,13},{... | collective-permute-start | bytes 24584 | tf_op jit(solution)/shard_map/ppermute | solution.py:21
  41.8 7.5 %collective-permute-start.5 = (bf16[4,2,4,128]{2,3,1,0:T(8,128)(2,1)S(1)}, bf16[4,2,4,128]{2,3,1,0:T(8,128)(2,1)S(1)}, u32[]{:S(2)}, u32[]{:S(2)}) collective-permute-start(bf16[4,2,4,128]{2,3,1,0:T(8,128)(2,1)S(1)} %get-tuple-element.28), channel_id=1, source_target_pairs={{1,0},{2,1},{3,2},{5,4},{6,5},{7,6},{9,8},{10,9},{11,10},{13,12},{... | collective-permute-start | bytes 24584 | tf_op jit(solution)/shard_map/ppermute | solution.py:23
  49.4 9.1 %collective-permute-start.6 = (bf16[4,2,264,4]{2,3,1,0:T(4,128)(2,1)S(1)}, bf16[4,2,264,4]{2,3,1,0:T(4,128)(2,1)S(1)}, u32[]{:S(2)}, u32[]{:S(2)}) collective-permute-start(bf16[4,2,264,4]{2,3,1,0:T(4,128)(2,1)S(1)} %get-tuple-element.23), channel_id=1, source_target_pairs={{0,4},{4,8},{8,12},{1,5},{5,9},{9,13},{2,6},{6,10},{10,14},{3,7},{... | collective-permute-start | bytes 50696 | tf_op jit(solution)/shard_map/ppermute | solution.py:21
  52.9 5.7 %collective-permute-start.7 = (bf16[4,2,264,4]{2,3,1,0:T(4,128)(2,1)S(1)}, bf16[4,2,264,4]{2,3,1,0:T(4,128)(2,1)S(1)}, u32[]{:S(2)}, u32[]{:S(2)}) collective-permute-start(bf16[4,2,264,4]{2,3,1,0:T(4,128)(2,1)S(1)} %get-tuple-element.24), channel_id=1, source_target_pairs={{4,0},{8,4},{12,8},{5,1},{9,5},{13,9},{6,2},{10,6},{14,10},{7,3},{... | collective-permute-start | bytes 50696 | tf_op jit(solution)/shard_map/ppermute | solution.py:23
  67.5 9.3 %collective-permute-start.8 = (bf16[4,2,256,128]{2,3,1,0:T(8,128)(2,1)S(1)}, bf16[4,2,256,128]{2,3,1,0:T(8,128)(2,1)S(1)}, u32[]{:S(2)}, u32[]{:S(2)}) collective-permute-start(bf16[4,2,256,128]{2,3,1,0:T(8,128)(2,1)S(1)} %fusion.73), channel_id=1, source_target_pairs={{0,16},{16,0},{1,17},{17,1},{2,18},{18,2},{3,19},{19,3},{4,20},{20... | collective-permute-start | bytes 1572872 | tf_op jit(solution)/shard_map/ppermute | solution.py:31
  77.1 11.2 %collective-permute-start.10 = (bf16[8,2,4,128]{2,3,1,0:T(8,128)(2,1)S(1)}, bf16[8,2,4,128]{2,3,1,0:T(8,128)(2,1)S(1)}, u32[]{:S(2)}, u32[]{:S(2)}) collective-permute-start(bf16[8,2,4,128]{2,3,1,0:T(8,128)(2,1)S(1)} %get-tuple-element.22), channel_id=1, source_target_pairs={{1,0},{2,1},{3,2},{5,4},{6,5},{7,6},{9,8},{10,9},{11,10},{13,12},{... | collective-permute-start | bytes 49160 | tf_op jit(solution)/shard_map/ppermute | solution.py:23
  81.6 10.5 %collective-permute-start.9 = (bf16[8,2,4,128]{2,3,1,0:T(8,128)(2,1)S(1)}, bf16[8,2,4,128]{2,3,1,0:T(8,128)(2,1)S(1)}, u32[]{:S(2)}, u32[]{:S(2)}) collective-permute-start(bf16[8,2,4,128]{2,3,1,0:T(8,128)(2,1)S(1)} %get-tuple-element.21), channel_id=1, source_target_pairs={{0,1},{1,2},{2,3},{4,5},{5,6},{6,7},{8,9},{9,10},{10,11},{12,13},{... | collective-permute-start | bytes 49160 | tf_op jit(solution)/shard_map/ppermute | solution.py:21
  92.2 8.5 %collective-permute-start.11 = (bf16[8,2,264,4]{2,3,1,0:T(4,128)(2,1)S(1)}, bf16[8,2,264,4]{2,3,1,0:T(4,128)(2,1)S(1)}, u32[]{:S(2)}, u32[]{:S(2)}) collective-permute-start(bf16[8,2,264,4]{2,3,1,0:T(4,128)(2,1)S(1)} %get-tuple-element.7), channel_id=1, source_target_pairs={{0,4},{4,8},{8,12},{1,5},{5,9},{9,13},{2,6},{6,10},{10,14},{3,7},{... | collective-permute-start | bytes 101384 | tf_op jit(solution)/shard_map/ppermute | solution.py:21
  95.6 6.0 %collective-permute-start.12 = (bf16[8,2,264,4]{2,3,1,0:T(4,128)(2,1)S(1)}, bf16[8,2,264,4]{2,3,1,0:T(4,128)(2,1)S(1)}, u32[]{:S(2)}, u32[]{:S(2)}) collective-permute-start(bf16[8,2,264,4]{2,3,1,0:T(4,128)(2,1)S(1)} %get-tuple-element.8), channel_id=1, source_target_pairs={{4,0},{8,4},{12,8},{5,1},{9,5},{13,9},{6,2},{10,6},{14,10},{7,3},{... | collective-permute-start | bytes 101384 | tf_op jit(solution)/shard_map/ppermute | solution.py:23
  113.3 4.6 %copy-start.3 = (f32[8,256]{1,0:T(8,128)S(1)}, f32[8,256]{1,0:T(8,128)}, u32[]{:S(2)}) copy-start(f32[8,256]{1,0:T(8,128)} %param.15) | copy-start | bytes 24580
  114.4 10.1 %all-to-all-start = ((bf16[4,1,2,256,128]{4,0,2,1,3:T(4,128)(2,1)}), bf16[4,1,2,256,128]{4,0,2,1,3:T(4,128)(2,1)S(1)}, u32[]{:S(2)}, u32[]{:S(2)}) async-start(bf16[4,1,2,256,128]{4,0,2,1,3:T(4,128)(2,1)} %copy.32), calls=%async_computation | async-start | bytes 1048576 | tf_op jit(solution)/shard_map/all_to_all | solution.py:138
where the time goes:
time: 128 us; the launch traced here: 127 us
  starting transfers between devices  40.5 us (32%)
  local copies, waits for them, and re-layouts  28.3 us (22%)
  other arithmetic  26.5 us (21%)
  waiting for transfers between devices  26.1 us (20%)
  matrix products  4.72 us (4%)
    ppermute x6, starting transfers between devices, with_halo(): lax.ppermute(head, axis, [((i + 1) % count, i) for i in range(ends)])  19.4 us
    ppermute x6, starting transfers between devices, with_halo(): lax.ppermute(tail, axis, [(i, (i + 1) % count) for i in range(ends)])  16.1 us
    ppermute x6, waiting for transfers between devices, with_halo(): lax.ppermute(head, axis, [((i + 1) % count, i) for i in range(ends)])  8.33 us
    sub x2, other arithmetic, merge_level(): cosine * shifted[:, 0] - sine_part * shifted[:, 1]  8.11 us
    all_to_all x1, waiting for transfers between devices, body(): lax.all_to_all(current[:, None], 'aper', split_axis=3, concat_axis=1, til...  6.48 us
    add x6, other arithmetic, merge_level(): shifted + weight[:, None, :, None] * interpolated[:, :, :, offset_step:of...  6.42 us
    another operation x2, other arithmetic, merge_level(): jnp.stack([cosine * shifted[:, 0] - sine_part * shifted[:, 1], sine_part...  6.08 us
    ppermute x6, waiting for transfers between devices, with_halo(): lax.ppermute(tail, axis, [(i, (i + 1) % count) for i in range(ends)])  5.93 us
  transfers between devices with their start and end apart: 14, of which 9 were waited for; matrix products, arithmetic and copies ran while one was open for 20% of the time, Pallas kernels for 0%

commit v1 on v0

--- a/solution.py
+++ b/solution.py
@@ -1,8 +1,11 @@
+import functools
 import math
 
 import jax
 import jax.numpy as jnp
 from jax import lax
+from jax.experimental import pallas as pl
+from jax.experimental.pallas import tpu as pltpu
 from jax.sharding import PartitionSpec as P
 
 LEVELS = 3
@@ -152,6 +155,733 @@
     return image[:, None]
 
 
+F32 = jnp.float32
+BF16 = jnp.bfloat16
+LANES = 128
+EDGE = -(-HALO * LEVELS // 16) * 16
+SEG = 4 * EDGE
+FIELDS = 3 + TAPS
+VMEM_LIMIT = 24 * 1024 * 1024
+
+
+def tables_of(slots):
+    row = {}
+    for lv in range(LEVELS - 1):
+        for c in range(2):
+            for h in range(2):
+                for k in range(FIELDS):
+                    row["p", lv, c, h, k] = len(row)
+    for s in range(slots):
+        for lv in range(LEVELS - 1):
+            for c in range(2):
+                row["b", s, lv, c] = len(row)
+    for lv in range(LEVELS - 1):
+        for c in range(2):
+            row["r", lv, c] = len(row)
+    return row, -(-len(row) // 8) * 8
+
+
+def half_of(lv, s, total):
+    return s // (total >> LEVELS - lv) % 2
+
+
+def child_of(lv, s, c, total):
+    d = total >> LEVELS - lv
+    return s - half_of(lv, s, total) * d + c * d
+
+
+def roll_lanes(x, shift):
+    return pltpu.roll(x, shift % LANES, x.ndim - 1) if shift % LANES else x
+
+
+def iota(shape, dim):
+    return lax.broadcasted_iota(jnp.int32, shape, dim)
+
+
+def pack_kernel(slots, head, tail, bo, ro, bt, rf, pb, pr, out_a, out_b, p_ref, base_ref):
+    row, rows = tables_of(slots)
+    p_ref[...] = jnp.zeros_like(p_ref)
+    for lv in range(LEVELS - 1):
+        for c in range(2):
+            for h in range(2):
+                at = row["p", lv, c, h, 0]
+                p_ref[at : at + 1] = bo[lv, c, h : h + 1, :].astype(F32)
+                p_ref[at + 1 : at + 2] = (ro[lv, c, h : h + 1, :] + HALO).astype(F32)
+                p_ref[at + 2 : at + 3] = rf[lv, c, h : h + 1, :]
+                p_ref[at + 3 : at + 3 + TAPS] = bt[lv, c, h].astype(F32)
+            at = row["r", lv, c]
+            p_ref[at : at + 1] = pr[lv, c : c + 1, :]
+            for s in range(slots):
+                at = row["b", s, lv, c]
+                p_ref[at : at + 1] = pb[s, lv, c : c + 1, :]
+    for c in range(2):
+        for s in range(slots):
+            base_ref[c * slots + s : c * slots + s + 1] = pb[s, LEVELS - 1, c : c + 1, :]
+
+    per = LANES // EDGE
+    beams = p_ref.shape[1]
+    lane = iota((8, LANES), 1) // EDGE
+
+    def packed(tile, start):
+        parts = []
+        for first in range(0, rows // 8, per):
+            total = jnp.zeros((8, LANES), F32)
+            for g in range(first, min(first + per, rows // 8)):
+                piece = p_ref[8 * g : 8 * g + 8, tile : tile + LANES]
+                spot = (g - first) * EDGE
+                total = jnp.where(lane == g - first, roll_lanes(piece, spot - start), total)
+            parts.append(total)
+        x = jnp.concatenate(parts, 0)
+        high = x.astype(BF16)
+        return high, (x - high.astype(F32)).astype(BF16)
+
+    def fill(out, sub, tile, start):
+        n = slots * 2 * EDGE
+        out[:n] = sub[...].reshape(n, LANES)
+        high, low = packed(tile, start)
+        m = high.shape[0]
+        out[n : n + m] = high
+        out[n + m : n + 2 * m] = low
+
+    even = lax.axis_index("ang") % 2 == 0
+
+    @pl.when(even)
+    def _():
+        fill(out_a, tail, beams - LANES, LANES - EDGE)
+        fill(out_b, head, 0, 0)
+
+    @pl.when(jnp.logical_not(even))
+    def _():
+        fill(out_a, head, 0, 0)
+        fill(out_b, tail, beams - LANES, LANES - EDGE)
+
+
+def turned(x):
+    return x.astype(F32).T.astype(BF16)
+
+
+def band(lag, taps):
+    out = jnp.zeros(lag.shape, F32)
+    for t in range(TAPS):
+        out = jnp.where(lag == t, taps[t], out)
+    return out.astype(BF16)
+
+
+def phasors(rate, first, delta, count, low, high, store):
+    n = rate.shape[1]
+    r8 = iota((8, n), 0)
+    small = rate * (r8.astype(F32) * delta)
+    other = jnp.where(r8 == 0, rate * (8 * delta), rate * first)
+    cs, ss = jnp.cos(small), jnp.sin(small)
+    co, so = jnp.cos(other), jnp.sin(other)
+    cu, su = co[1:2], so[1:2]
+    ck, sk = jnp.broadcast_to(co[0:1], (8, n)), jnp.broadcast_to(so[0:1], (8, n))
+    re = cs * cu - ss * su
+    im = ss * cu + cs * su
+    for j in range(count):
+        ids = r8 + 8 * j
+        keep = jnp.logical_and(ids >= low, ids < high)
+        store(j, jnp.where(keep, re, 0.0), jnp.where(keep, im, 0.0))
+        if j + 1 < count:
+            re, im = re * ck - im * sk, im * ck + re * sk
+
+
+def range_place(cells, lv, full):
+    reach = (LEVELS - 1 - lv) * HALO
+    lead = (EDGE - HALO * (lv + 1)) if lv < LEVELS - 1 else 0
+    at = lax.axis_index("rng") * cells - lead
+    first = at.astype(F32) / full - 0.5
+    return first, -at, full - at
+
+
+def rows_of(cells, lv):
+    need = cells + 2 * (EDGE - HALO * (lv + 1))
+    return -(-need // 16) * 16
+
+
+def main_tables_kernel(slots, full, sub, p_ref, bo, ro, bt, rf, pr, xt, w1, w2, v1, v2, o2, e_refs, th):
+    row, rows = tables_of(slots)
+    total = 2 * slots
+    cells = sub.shape[3]
+    beams = sub.shape[2]
+    tiles = beams // LANES
+    for s in range(slots):
+        for x in range(2):
+            xt[x, :, s * beams : (s + 1) * beams] = turned(sub[s, x])
+
+    w1[...] = jnp.zeros_like(w1)
+    w2[...] = jnp.zeros_like(w2)
+    v1[...] = jnp.zeros_like(v1)
+    v2[...] = jnp.zeros_like(v2)
+    own = lax.axis_index("aper")
+
+    def main_band(first_col, off, taps, put):
+        low = max(first_col - 16, 0)
+        top = min(first_col + LANES + 16, beams)
+        m = iota((top - low, LANES), 0) + low
+        p = iota((top - low, LANES), 1) + first_col
+        put(low, top, band(m - p - off, taps))
+
+    def strip_band(first_col, off, taps, put):
+        if first_col + LANES == beams:
+            m = iota((EDGE, LANES), 0) + beams
+            put(EDGE, band(m - (iota((EDGE, LANES), 1) + first_col) - off, taps))
+        if first_col == 0:
+            m = iota((EDGE, LANES), 0) - EDGE
+            put(2 * EDGE, band(m - iota((EDGE, LANES), 1) - off, taps))
+
+    for lv in range(LEVELS - 1):
+        for c in range(2):
+            for h in range(2):
+                for t in range(tiles):
+                    cols = slice(t * LANES, (t + 1) * LANES)
+                    at = row["p", lv, c, h, 0]
+                    off = p_ref[at : at + 1, cols].astype(jnp.int32)
+                    taps = [p_ref[at + 3 + k : at + 4 + k, cols] for k in range(TAPS)]
+
+                    def put(low, top, v):
+                        w1[lv, c, h, low:top, cols] = v
+
+                    main_band(t * LANES, off, taps, put)
+
+                    def put(at_row, v):
+                        for s in range(slots):
+                            if half_of(lv, s, total) == h:
+                                base = child_of(lv, s, c, total) * SEG % LANES + at_row
+                                w2[lv, c, s, base : base + EDGE, cols] = v
+
+                    strip_band(t * LANES, off, taps, put)
+    lv = LEVELS - 1
+    for h in range(2):
+        for t in range(tiles):
+            cols = slice(t * LANES, (t + 1) * LANES)
+            outs = slice(h * LANES, (h + 1) * LANES)
+            off = bo[lv, own, h : h + 1, cols]
+            tap_rows = bt[lv, own, h, :, cols].astype(F32)
+            taps = [tap_rows[k : k + 1] for k in range(TAPS)]
+
+            def put(low, top, v):
+                v1[t, low:top, outs] = v
+
+            main_band(t * LANES, off, taps, put)
+
+            def put(at_row, v):
+                for par in range(LANES // SEG):
+                    base = par * SEG + at_row
+                    v2[t, par, base : base + EDGE, outs] = v
+
+            strip_band(t * LANES, off, taps, put)
+            o2[t, 0:1, outs] = (ro[lv, own, h : h + 1, cols] + HALO).astype(F32)
+            o2[t, 1:2, outs] = rf[lv, own, h : h + 1, cols]
+
+    for lv in range(LEVELS):
+        first, low, high = range_place(cells, lv, full)
+        count = (rows_of(cells, lv) if lv < LEVELS - 1 else cells) // 8
+        for c in range(2 if lv < LEVELS - 1 else 1):
+            if lv < LEVELS - 1:
+                at = row["r", lv, c]
+                rate = p_ref[at : at + 1, :]
+            else:
+                rate = jnp.where(own == 0, pr[lv, 0:1, :], pr[lv, 1:2, :])
+
+            def store(j, re, im):
+                e_refs[lv][c, 0, 8 * j : 8 * j + 8, :] = re
+                e_refs[lv][c, 1, 8 * j : 8 * j + 8, :] = im
+
+            phasors(rate, first, 1.0 / full, count, low, high, store)
+    at = row["b", 0, 0, 0]
+    n = slots * (LEVELS - 1) * 2
+    base = p_ref[at : at + n, :]
+    th[0] = jnp.cos(base)
+    th[1] = jnp.sin(base)
+
+
+def strip_kernel(slots, got_a, got_b, head, tail, xt, strip, out_c, out_d, nat):
+    beams = slots * SEG
+    even = lax.axis_index("ang") % 2 == 0
+
+    def place(right, left):
+        for s in range(slots):
+            for x in range(2):
+                at = (s * 2 + x) * EDGE
+                nat[x, s * SEG + EDGE : s * SEG + 2 * EDGE] = right[at : at + EDGE]
+                nat[x, s * SEG + 2 * EDGE : s * SEG + 3 * EDGE] = left[at : at + EDGE]
+
+    for s in range(slots):
+        for x in range(2):
+            nat[x, s * SEG : s * SEG + EDGE] = tail[s, x]
+            nat[x, s * SEG + 3 * EDGE : (s + 1) * SEG] = head[s, x]
+
+    @pl.when(even)
+    def _():
+        place(got_a, got_b)
+
+    @pl.when(jnp.logical_not(even))
+    def _():
+        place(got_b, got_a)
+
+    for x in range(2):
+        strip[x] = turned(nat[x])
+    cells = strip.shape[1]
+    mains = xt.shape[2]
+
+    def send(first, last):
+        for x in range(2):
+            first[x, :, :mains] = xt[x, cells - EDGE :, :]
+            first[x, :, mains:] = strip[x, cells - EDGE :, :]
+            last[x, :, :mains] = xt[x, :EDGE, :]
+            last[x, :, mains:] = strip[x, :EDGE, :]
+
+    even_r = lax.axis_index("rng") % 2 == 0
+
+    @pl.when(even_r)
+    def _():
+        send(out_c, out_d)
+
+    @pl.when(jnp.logical_not(even_r))
+    def _():
+        send(out_d, out_c)
+
+
+def strip_tables_kernel(slots, full, got_a, got_b, p_ref, base_ref, got_base, fp, ws, es_refs, ths, os_, th2, seg, halo):
+    row, rows = tables_of(slots)
+    total = 2 * slots
+    cells = LANES
+    beams = p_ref.shape[1]
+    per = LANES // EDGE
+    n = slots * 2 * EDGE
+    m = (rows // 8 + per - 1) // per * 8
+    even = lax.axis_index("ang") % 2 == 0
+
+    def load(right, left):
+        halo[0] = right[n : n + m].astype(F32) + right[n + m : n + 2 * m].astype(F32)
+        halo[1] = left[n : n + m].astype(F32) + left[n + m : n + 2 * m].astype(F32)
+
+    @pl.when(even)
+    def _():
+        load(got_a, got_b)
+
+    @pl.when(jnp.logical_not(even))
+    def _():
+        load(got_b, got_a)
+
+    lane = iota((8, LANES), 1)
+    piece_of = lane % SEG // EDGE
+    for g in range(rows // 8):
+        at = g // per * 8
+        spot = g % per * EDGE
+        parts = [
+            roll_lanes(p_ref[8 * g : 8 * g + 8, beams - LANES :], EDGE - LANES),
+            roll_lanes(halo[0, at : at + 8, :], EDGE - spot),
+            roll_lanes(halo[1, at : at + 8, :], 2 * EDGE - spot),
+            roll_lanes(p_ref[8 * g : 8 * g + 8, :LANES], 3 * EDGE),
+        ]
+        out = parts[0]
+        for k in range(1, 4):
+            out = jnp.where(piece_of == k, parts[k], out)
+        twice = jnp.where(lane < SEG, out, roll_lanes(out, SEG))
+        seg[8 * g : 8 * g + 8, :] = twice
+
+    first_seg = iota((1, LANES), 1) < SEG
+
+    def pick(r0, r1):
+        if r0 == r1:
+            return seg[r0 : r0 + 1, :]
+        return jnp.where(first_seg, seg[r0 : r0 + 1, :], seg[r1 : r1 + 1, :])
+
+    def beam_of(i):
+        j = i % SEG
+        return jnp.where(j < 2 * EDGE, beams - EDGE + j, j - 3 * EDGE)
+
+    base_rows = []
+    for lv in range(LEVELS - 1):
+        first, low, high = range_place(cells, lv, full)
+        for c in range(2):
+            for t in range(beams // LANES):
+                cols = slice(t * LANES, (t + 1) * LANES)
+                s0, s1 = 2 * t, 2 * t + 1
+                h0, h1 = half_of(lv, s0, total), half_of(lv, s1, total)
+                k0, k1 = child_of(lv, s0, c, total), child_of(lv, s1, c, total)
+                field = [pick(row["p", lv, c, h0, k], row["p", lv, c, h1, k]) for k in range(FIELDS)]
+                at = lv * 2 + c
+                os_[at, 0:1, cols] = field[1]
+                os_[at, 1:2, cols] = field[2]
+                i_row = iota((beams, LANES), 0)
+                col = iota((1, LANES), 1)
+                wanted = jnp.where(col < SEG, k0, k1)
+                lag = beam_of(i_row) - beam_of(col) - field[0].astype(jnp.int32)
+                lag = jnp.where(i_row // SEG == wanted, lag, -1)
+                ws[lv, c, :, cols] = band(lag, field[3:])
+                halo[2, at * 2 + t : at * 2 + t + 1, :] = pick(row["b", s0, lv, c], row["b", s1, lv, c])
+            rate = jnp.concatenate([pick(row["r", lv, c], row["r", lv, c])] * (beams // LANES), 1)
+
+            def store(j, re, im):
+                es_refs[lv][c, 0, 8 * j : 8 * j + 8, :] = re
+                es_refs[lv][c, 1, 8 * j : 8 * j + 8, :] = im
+
+            phasors(rate[:, :LANES], first, 1.0 / full, rows_of(cells, lv) // 8, low, high, store)
+    angles = halo[2, : 2 * 2 * (LEVELS - 1)]
+    ths[0] = jnp.cos(angles)
+    ths[1] = jnp.sin(angles)
+
+    own = lax.axis_index("aper")
+    scale = 1.0 / math.sqrt(total)
+    for h in range(2):
+        mine = own == h
+        for t in range(beams // LANES):
+            cols = slice(t * LANES, (t + 1) * LANES)
+            here = jnp.where(own == 0, base_ref[:slots, cols], base_ref[slots:, cols])
+            there = jnp.where(own == 0, got_base[:slots, cols], got_base[slots:, cols])
+            angles = jnp.where(mine, here, there) + fp[h * slots : (h + 1) * slots, cols]
+            th2[0, t, :, h * LANES : (h + 1) * LANES] = jnp.cos(angles) * scale
+            th2[1, t, :, h * LANES : (h + 1) * LANES] = jnp.sin(angles) * scale
+
+
+def shift_setup(o_row, f_row, extra):
+    shift = o_row.astype(jnp.int32) + extra
+    sub = iota((8, LANES), 0)
+    reach = sub + shift
+    return dict(
+        one=jnp.broadcast_to(1.0 - f_row, (8, LANES)),
+        two=jnp.broadcast_to(f_row, (8, LANES)),
+        bits=[jnp.broadcast_to(shift % (2 * b) >= b, (8, LANES)) for b in (1, 2, 4)],
+        in0=reach < 8,
+        in1=reach < 16,
+        last=sub == 7,
+    )
+
+
+def rotated(setup, v):
+    n = v.shape[0] - 1
+    spun = pltpu.roll(v, 7, 1)
+    ahead = jnp.where(setup["last"][None], spun[1:], spun[:n])
+    g = setup["one"][None] * v[:n] + setup["two"][None] * ahead
+    for b, bit in zip((1, 2, 4), setup["bits"]):
+        g = jnp.where(bit[None], pltpu.roll(g, 8 - b, 1), g)
+    return g
+
+
+def level_step(slots, total, lv, x_in, out, inter, w1, w2, ws, e_main, e_strip, th, ths, o_main, os_, row):
+    rows_in = x_in.shape[1]
+    beams = slots * SEG
+    rows_out = out.shape[1]
+    groups = slots + 1
+    for g in range(groups):
+        buf = inter[g % 2]
+        for c in range(2):
+            if g < slots:
+                k = child_of(lv, g, c, total)
+                h = half_of(lv, g, total)
+                lhs = x_in[:, :, k * beams : (k + 1) * beams].reshape(2 * rows_in, beams)
+                tile = slots * beams + k * SEG // LANES * LANES
+                lhs2 = x_in[:, :, tile : tile + LANES].reshape(2 * rows_in, LANES)
+                val = jnp.dot(lhs, w1[lv, c, h], preferred_element_type=F32) + jnp.dot(
+                    lhs2, w2[lv, c, g], preferred_element_type=F32
+                )
+            else:
+                lhs = x_in[:, :, slots * beams :].reshape(2 * rows_in, beams)
+                val = jnp.dot(lhs, ws[lv, c], preferred_element_type=F32)
+            for x in range(2):
+                for t in range(beams // LANES):
+                    buf[c, x, t, :rows_in, :] = val[x * rows_in : (x + 1) * rows_in, t * LANES : (t + 1) * LANES]
+        for t in range(beams // LANES):
+            cols = slice(t * LANES, (t + 1) * LANES)
+            sets, turn = [], []
+            for c in range(2):
+                if g < slots:
+                    at = row["p", lv, c, half_of(lv, g, total), 0]
+                    sets.append(shift_setup(o_main[at + 1 : at + 2, cols], o_main[at + 2 : at + 3, cols], 0))
+                    at = (g * (LEVELS - 1) + lv) * 2 + c
+                    turn.append([jnp.broadcast_to(th[q, at : at + 1, cols], (8, LANES))[None] for q in range(2)])
+                else:
+                    at = lv * 2 + c
+                    sets.append(shift_setup(os_[at, 0:1, cols], os_[at, 1:2, cols], 0))
+                    turn.append([jnp.broadcast_to(ths[q, at * 2 + t : at * 2 + t + 1, :], (8, LANES))[None] for q in range(2)])
+            held = [[None, None], [None, None]]
+            step = 4
+            done = 0
+            n_out = rows_out // 8
+            while done < n_out:
+                n = min(step, n_out - done)
+                acc_re = acc_im = None
+                for c in range(2):
+                    moved = []
+                    for x in range(2):
+                        lo = 0 if done == 0 else done + 1
+                        hi = done + n + 2
+                        v = buf[c, x, t, 8 * lo : 8 * hi, :].reshape(hi - lo, 8, LANES)
+                        g_new = rotated(sets[c], v)
+                        if done == 0:
+                            seq = g_new
+                        else:
+                            seq = jnp.concatenate([held[c][x], g_new], 0)
+                        held[c][x] = seq[n : n + 1]
+                        moved.append(jnp.where(sets[c]["in0"][None], seq[:n], seq[1 : n + 1]))
+                    e = e_main if g < slots else e_strip
+                    ecols = cols if g < slots else slice(0, LANES)
+                    ec = e[c, 0, 8 * done : 8 * (done + n), ecols].reshape(n, 8, LANES)
+                    es = e[c, 1, 8 * done : 8 * (done + n), ecols].reshape(n, 8, LANES)
+                    tc, ts = turn[c]
+                    fc, fs = ec * tc - es * ts, es * tc + ec * ts
+                    re = fc * moved[0] - fs * moved[1]
+                    im = fs * moved[0] + fc * moved[1]
+                    acc_re = re if acc_re is None else acc_re + re
+                    acc_im = im if acc_im is None else acc_im + im
+                ocols = slice(g * beams + t * LANES, g * beams + (t + 1) * LANES)
+                out[0, 8 * done : 8 * (done + n), ocols] = acc_re.reshape(8 * n, LANES).astype(BF16)
+                out[1, 8 * done : 8 * (done + n), ocols] = acc_im.reshape(8 * n, LANES).astype(BF16)
+                done += n
+
+
+def last_step(slots, cells, hf, x_in, v1, v2, o2, th2, e2, buf, put):
+    rows_in = x_in.shape[1]
+    beams = slots * SEG
+    for q in range(slots):
+        lhs = x_in[:, :, q * beams : (q + 1) * beams].reshape(2 * rows_in, beams)
+        tile = slots * beams + q * SEG // LANES * LANES
+        lhs2 = x_in[:, :, tile : tile + LANES].reshape(2 * rows_in, LANES)
+        val = jnp.dot(lhs, v1[hf], preferred_element_type=F32) + jnp.dot(
+            lhs2, v2[hf, q * SEG % LANES // SEG], preferred_element_type=F32
+        )
+        for x in range(2):
+            for h in range(2):
+                buf[q, x, h] = val[x * rows_in : (x + 1) * rows_in, h * LANES : (h + 1) * LANES]
+    sets, turn = [], []
+    rows2 = o2[hf]
+    for h in range(2):
+        cols = slice(h * LANES, (h + 1) * LANES)
+        sets.append(shift_setup(rows2[0:1, cols], rows2[1:2, cols], HALO))
+        cos_rows = th2[0, hf]
+        sin_rows = th2[1, hf]
+        turn.append(
+            [
+                [jnp.broadcast_to(cos_rows[q : q + 1, cols], (8, LANES))[None] for q in range(slots)],
+                [jnp.broadcast_to(sin_rows[q : q + 1, cols], (8, LANES))[None] for q in range(slots)],
+            ]
+        )
+    n_out = cells // 8
+    held = [[None, None], [None, None]]
+    done = 0
+    step = 4
+    while done < n_out:
+        n = min(step, n_out - done)
+        sum_re = sum_im = None
+        for h in range(2):
+            lo = 0 if done == 0 else done + 2
+            hi = min(done + n + 3, rows_in // 8)
+            re = im = None
+            for q in range(slots):
+                a = buf[q, 0, h, 8 * lo : 8 * hi, :].reshape(hi - lo, 8, LANES)
+                b = buf[q, 1, h, 8 * lo : 8 * hi, :].reshape(hi - lo, 8, LANES)
+                tc, ts = turn[h][0][q], turn[h][1][q]
+                pr_, pi_ = tc * a - ts * b, ts * a + tc * b
+                re = pr_ if re is None else re + pr_
+                im = pi_ if im is None else im + pi_
+            moved = []
+            for x, v in enumerate((re, im)):
+                if hi - lo < n + (3 if done == 0 else 1):
+                    v = jnp.concatenate([v, jnp.zeros((1, 8, LANES), F32)], 0)
+                g_new = rotated(sets[h], v)
+                seq = g_new if done == 0 else jnp.concatenate([held[h][x], g_new], 0)
+                held[h][x] = seq[n : n + 2]
+                moved.append(
+                    jnp.where(
+                        sets[h]["in0"][None],
+                        seq[:n],
+                        jnp.where(sets[h]["in1"][None], seq[1 : n + 1], seq[2 : n + 2]),
+                    )
+                )
+            sum_re = moved[0] if sum_re is None else sum_re + moved[0]
+            sum_im = moved[1] if sum_im is None else sum_im + moved[1]
+        at = pl.ds(pl.multiple_of(hf * LANES, LANES), LANES)
+        ec = e2[0, 0, 8 * done : 8 * (done + n), at].reshape(n, 8, LANES)
+        es = e2[0, 1, 8 * done : 8 * (done + n), at].reshape(n, 8, LANES)
+        put(done, n, ec * sum_re - es * sum_im, es * sum_re + ec * sum_im)
+        done += n
+
+
+def levels_kernel(slots, full, xt, strip, got_c, got_d, w1, w2, ws, v1, v2, o2, e0, e1, e2, es0, es1, th, ths, os_, th2, p_ref, out, x2, x0, x1, inter0, inter1, buf, flat):
+    row, rows = tables_of(slots)
+    total = 2 * slots
+    cells = xt.shape[1]
+    mains = xt.shape[2]
+    for x in range(2):
+        x0[x, EDGE : EDGE + cells, :mains] = xt[x]
+        x0[x, EDGE : EDGE + cells, mains:] = strip[x]
+    even = lax.axis_index("rng") % 2 == 0
+
+    def place(right, left):
+        for x in range(2):
+            x0[x, :EDGE, :] = left[x]
+            x0[x, EDGE + cells :, :] = right[x]
+
+    @pl.when(even)
+    def _():
+        place(got_c, got_d)
+
+    @pl.when(jnp.logical_not(even))
+    def _():
+        place(got_d, got_c)
+
+    inter = (inter0, inter1)
+    level_step(slots, total, 0, x0, x1, inter, w1, w2, ws, e0, es0, th, ths, p_ref, os_, row)
+    level_step(slots, total, 1, x1, x2, inter, w1, w2, ws, e1, es1, th, ths, p_ref, os_, row)
+    hf = 1 - lax.axis_index("aper")
+
+    def put(done, n, re, im):
+        flat[0, 8 * done : 8 * (done + n), :] = re.reshape(8 * n, LANES)
+        flat[1, 8 * done : 8 * (done + n), :] = im.reshape(8 * n, LANES)
+
+    last_step(slots, cells, hf, x2, v1, v2, o2, th2, e2, buf, put)
+    for x in range(2):
+        out[x] = flat[x].T.astype(BF16)
+
+
+def own_half_kernel(slots, x2, v1, v2, o2, th2, e2, out, buf, flat):
+    cells = out.shape[2]
+    hf = lax.axis_index("aper")
+
+    def put(done, n, re, im):
+        flat[0, 8 * done : 8 * (done + n), :] = re.reshape(8 * n, LANES)
+        flat[1, 8 * done : 8 * (done + n), :] = im.reshape(8 * n, LANES)
+
+    last_step(slots, cells, hf, x2, v1, v2, o2, th2, e2, buf, put)
+    for x in range(2):
+        out[x] = flat[x].T
+
+
+def swap_even(axis):
+    n = lax.axis_size(axis)
+    return [(i, i ^ 1) for i in range(n) if i ^ 1 < n]
+
+
+def swap_odd(axis):
+    n = lax.axis_size(axis)
+    pairs = []
+    for i in range(1, n - 1, 2):
+        pairs += [(i, i + 1), (i + 1, i)]
+    return pairs
+
+
+def call(kernel, outs, args, scratch=(), flops=0, specs=None):
+    vm = pl.BlockSpec(memory_space=pltpu.VMEM)
+    return pl.pallas_call(
+        kernel,
+        out_shape=[jax.ShapeDtypeStruct(s, d) for s, d in outs],
+        in_specs=specs or [vm] * len(args),
+        out_specs=[vm] * len(outs),
+        scratch_shapes=[pltpu.VMEM(s, d) for s, d in scratch],
+        compiler_params=pltpu.CompilerParams(vmem_limit_bytes=VMEM_LIMIT),
+        cost_estimate=pl.CostEstimate(flops=flops, bytes_accessed=0, transcendentals=0),
+    )(*args)
+
+
+def fast_body(subimages, beam_offsets, range_offsets, beam_taps, range_frac, phase_base, phase_rate, final_phase):
+    slots, _, beams, cells = subimages.shape
+    full = cells * lax.axis_size("rng")
+    row, rows = tables_of(slots)
+    m = (rows // 8 + LANES // EDGE - 1) // (LANES // EDGE) * 8
+    msg = slots * 2 * EDGE + 2 * m
+    head = subimages[:, :, :EDGE]
+    tail = subimages[:, :, beams - EDGE :]
+    vm = pl.BlockSpec(memory_space=pltpu.VMEM)
+    lv_rows = [rows_of(cells, lv) for lv in range(LEVELS - 1)]
+
+    out_a, out_b, params, bases = call(
+        functools.partial(pack_kernel, slots),
+        [((msg, LANES), BF16), ((msg, LANES), BF16), ((rows, beams), F32), ((2 * slots, beams), F32)],
+        (head, tail, beam_offsets, range_offsets, beam_taps, range_frac, phase_base, phase_rate),
+        flops=1000,
+    )
+    got_a = lax.ppermute(out_a, "ang", swap_even("ang"))
+    got_b = lax.ppermute(out_b, "ang", swap_odd("ang"))
+    got_base = lax.ppermute(bases, "aper", swap_even("aper"))
+
+    def main_tables(*refs):
+        ins, outs = refs[:7], refs[7:]
+        main_tables_kernel(slots, full, *ins, *outs[:6], outs[6 : 6 + LEVELS], outs[6 + LEVELS])
+
+    n_th = slots * (LEVELS - 1) * 2
+    tiles = beams // LANES
+    res = call(
+        main_tables,
+        [
+            ((2, cells, slots * beams), BF16),
+            ((LEVELS - 1, 2, 2, beams, beams), BF16),
+            ((LEVELS - 1, 2, slots, LANES, beams), BF16),
+            ((tiles, beams, beams), BF16),
+            ((tiles, LANES // SEG, LANES, beams), BF16),
+            ((tiles, 8, beams), F32),
+        ]
+        + [((2, 2, r, beams), F32) for r in lv_rows]
+        + [((1, 2, cells, beams), F32), ((2, n_th, beams), F32)],
+        (subimages, params, beam_offsets, range_offsets, beam_taps, range_frac, phase_rate),
+        flops=20_000_000,
+    )
+    xt, w1, w2, v1, v2, o2, e0, e1, e2, th = res
+
+    strip, out_c, out_d = call(
+        functools.partial(strip_kernel, slots),
+        [((2, cells, beams), BF16)] + [((2, EDGE, (slots + 1) * beams), BF16)] * 2,
+        (got_a, got_b, head, tail, xt),
+        scratch=[((2, beams, cells), BF16)],
+        flops=1000,
+    )
+    got_c = lax.ppermute(out_c, "rng", swap_even("rng"))
+    got_d = lax.ppermute(out_d, "rng", swap_odd("rng"))
+
+    def strip_tables(*refs):
+        ins, outs = refs[:6], refs[6:]
+        strip_tables_kernel(slots, full, *ins, outs[0], outs[1:LEVELS], *outs[LEVELS:])
+
+    ws, es0, es1, ths, os_, th2 = call(
+        strip_tables,
+        [((LEVELS - 1, 2, beams, beams), BF16)]
+        + [((2, 2, r, LANES), F32) for r in lv_rows]
+        + [((2, 4 * (LEVELS - 1), LANES), F32), ((2 * (LEVELS - 1), 8, beams), F32), ((2, tiles, slots, beams), F32)],
+        (got_a, got_b, params, bases, got_base, final_phase),
+        scratch=[((rows, LANES), F32), ((3, max(m, 8), LANES), F32)],
+        flops=20_000_000,
+    )
+    wide = (slots + 1) * beams
+    x_rows = cells + 2 * EDGE
+    sent, x2 = call(
+        functools.partial(levels_kernel, slots, full),
+        [((2, LANES, cells), BF16), ((2, lv_rows[1], wide), BF16)],
+        (xt, strip, got_c, got_d, w1, w2, ws, v1, v2, o2, e0, e1, e2, es0, es1, th, ths, os_, th2, params),
+        scratch=[
+            ((2, x_rows, wide), BF16),
+            ((2, lv_rows[0], wide), BF16),
+            ((2, 2, tiles, x_rows + 16, LANES), F32),
+            ((2, 2, tiles, x_rows + 16, LANES), F32),
+            ((slots, 2, 2, lv_rows[1], LANES), F32),
+            ((2, cells, LANES), F32),
+        ],
+        flops=200_000_000,
+    )
+    got = lax.ppermute(sent, "aper", swap_even("aper"))
+    (mine,) = call(
+        functools.partial(own_half_kernel, slots),
+        [((2, LANES, cells), F32)],
+        (x2, v1, v2, o2, th2, e2),
+        scratch=[((slots, 2, 2, lv_rows[1], LANES), F32), ((2, cells, LANES), F32)],
+        flops=20_000_000,
+    )
+    return (mine + got.astype(F32))[:, None]
+
+
+def whole_body(*args):
+    slots, _, beams, cells = args[0].shape
+    fits = (
+        lax.axis_size("aper") == 2
+        and slots * SEG == beams
+        and beams == 2 * LANES
+        and cells == LANES
+        and slots == 1 << LEVELS - 1
+    )
+    return fast_body(*args) if fits else body(*args)
+
+
 def solution(mesh):
     in_specs = (
         P("aper", None, "ang", "rng"),
@@ -164,4 +894,4 @@
         P(None, "ang"),
     )
     out_specs = P(None, "ang", "aper", "rng")
-    return jax.shard_map(body, mesh=mesh, in_specs=in_specs, out_specs=out_specs, check_vma=False)
+    return jax.shard_map(whole_body, mesh=mesh, in_specs=in_specs, out_specs=out_specs, check_vma=False)

time: 128 us -> 27.8 us (0.22)
  starting transfers between devices: 40.5 us -> 10.8 us
  local copies, waits for them, and re-layouts: 28.3 us -> 1.9 us
  other arithmetic: 26.5 us -> 0.67 us
  waiting for transfers between devices: 26.1 us -> 4.47 us
  Pallas kernels: 0 us -> 9.54 us
  matrix products: 4.72 us -> 0 us
    ppermute x13 -> x6, starting transfers between devices: 37 us -> 10.8 us  [the longest x1 4.6 us: fast_body(): got_d = lax.ppermute(out_d, 'rng', swap_odd('rng'))]
    gather x36 -> x0, local copies, waits for them, and re-layouts: 20.9 us -> none  [the longest x6 3.62 us: merge_level(): phase_base[slot_ids, level_idx, child_ids][:, :, None]]
    ppermute x13 -> x6, waiting for transfers between devices: 19.6 us -> 4.47 us  [the longest x1 2.16 us: fast_body(): got_base = lax.ppermute(bases, 'aper', swap_even('aper'))]
    pallas_call x0 -> x6, Pallas kernels: none -> 9.54 us  [call(): pl.pallas_call(kernel, out_shape=[jax.ShapeDtypeStruct(s, d) for s, d in...]
    sub x3 -> x0, other arithmetic: 8.12 us -> none  [the longest x2 8.11 us: merge_level(): cosine * shifted[:, 0] - sine_part * shifted[:, 1]]
    add x14 -> x0, other arithmetic: 6.55 us -> none  [the longest x6 6.42 us: merge_level(): shifted + weight[:, None, :, None] * interpolated[:, :, :, offset_step:of...]
    all_to_all x1 -> x0, waiting for transfers between devices: 6.48 us -> none  [body(): lax.all_to_all(current[:, None], 'aper', split_axis=3, concat_axis=1, til...]
    another operation x2 -> x0, other arithmetic: 6.08 us -> none  [merge_level(): jnp.stack([cosine * shifted[:, 0] - sine_part * shifted[:, 1], sine_part...]
  transfers between devices with their start and end apart: 14 -> 6, of which waited for: 9 -> 3; matrix products, arithmetic and copies ran while one was open for 20% -> 0% of each run, Pallas kernels for 0% -> 11%
where the time goes in v1:
time: 27.8 us; the launch traced here: 27.5 us
  starting transfers between devices  10.8 us (39%)
  Pallas kernels  9.54 us (34%)
  waiting for transfers between devices  4.47 us (16%)
  local copies, waits for them, and re-layouts  1.9 us (7%)
  other arithmetic  0.67 us (2%)
    pallas_call x6, Pallas kernels, call(): pl.pallas_call(kernel, out_shape=[jax.ShapeDtypeStruct(s, d) for s, d in...  9.54 us
    ppermute x1, starting transfers between devices, fast_body(): got_d = lax.ppermute(out_d, 'rng', swap_odd('rng'))  4.6 us
    ppermute x1, starting transfers between devices, fast_body(): got_b = lax.ppermute(out_b, 'ang', swap_odd('ang'))  2.5 us
    ppermute x1, waiting for transfers between devices, fast_body(): got_base = lax.ppermute(bases, 'aper', swap_even('aper'))  2.16 us
    ppermute x1, waiting for transfers between devices, fast_body(): got = lax.ppermute(sent, 'aper', swap_even('aper'))  2.05 us
    ppermute x1, starting transfers between devices, fast_body(): got_base = lax.ppermute(bases, 'aper', swap_even('aper'))  1.56 us
    ppermute x1, starting transfers between devices, fast_body(): got = lax.ppermute(sent, 'aper', swap_even('aper'))  1.55 us
    unnamed x16, local copies, waits for them, and re-layouts  1.06 us
  transfers between devices with their start and end apart: 6, of which 3 were waited for; matrix products, arithmetic and copies ran while one was open for 0% of the time, Pallas kernels for 11%

profile of v1, /device:TPU:12, one launch (start us, length us, event | category | flops | bytes accessed | tf_op | source)
XLA Modules:
  0.0 27.5 jit_solution(4608881140449523961)
XLA Ops:
  0.0 0.0 copy-start.1
  0.0 0.0 copy-start.6
  0.0 0.0 copy-start.2
  0.0 0.0 copy-start.3
  0.0 0.0 copy-start.4
  0.0 0.0 copy-start.5
  0.0 0.8 %fusion = (bf16[4,2,16,128]{3,2,1,0:T(8,128)(2,1)S(1)}, bf16[4,2,16,128]{3,2,1,0:T(8,128)(2,1)S(1)}) fusion(bf16[4,2,256,128]{3,2,1,0:T(8,128)(2,1)} %refs_0_.1), kind=kLoop, calls=%fused_computation.1 | loop fusion | bytes 131072 | tf_op jit(solution)/shard_map/slice | solution.py:786
  0.9 0.0 copy-done.1
  0.9 0.0 copy-done.6
  0.9 0.0 copy-done.2
  0.9 0.0 copy-done.3
  0.9 0.0 copy-done.4
  0.9 0.0 copy-done.5
  0.9 0.1 shard_map.82
  1.1 0.1 collective-permute-start
  1.1 2.5 %collective-permute-start.1 = (bf16[160,128]{1,0:T(8,128)(2,1)S(1)}, bf16[160,128]{1,0:T(8,128)(2,1)S(1)}, u32[]{:S(2)}, u32[]{:S(2)}) collective-permute-start(bf16[160,128]{1,0:T(8,128)(2,1)S(1)} %get-tuple-element.33), channel_id=1, source_target_pairs={{1,2},{2,1},{5,6},{6,5},{9,10},{10,9},{13,14},{14,13},{17,18},{18,... | collective-permute-start | bytes 122888 | tf_op jit(solution)/shard_map/ppermute | solution.py:797
  3.7 0.0 copy-start
  3.7 1.0 %copy-done = bf16[4,2,256,128]{3,2,1,0:T(8,128)(2,1)S(1)} copy-done((bf16[4,2,256,128]{3,2,1,0:T(8,128)(2,1)S(1)}, bf16[4,2,256,128]{3,2,1,0:T(8,128)(2,1)}, u32[]{:S(2)}) %copy-start) | copy-done | bytes 524312
  4.7 1.5 %shard_map.83 = (bf16[2,128,1024]{2,1,0:T(8,128)(2,1)S(1)}, bf16[2,2,2,256,256]{4,3,2,1,0:T(8,128)(2,1)S(1)}, bf16[2,2,4,128,256]{4,3,2,1,0:T(8,128)(2,1)S(1)}, ...) custom-call(bf16[4,2,256,128]{3,2,1,0:T(8,128)(2,1)S(1)} %copy-done,, ...), custom_call_target="tpu_custom_call" | custom-call | flops 20000000 | tf_op jit(solution)/shard_map/pallas_call | solution.py:768
  6.2 0.0 collective-permute-done.got_a.refs_0_
  6.2 0.3 collective-permute-done.1.got_b.refs_1_
  6.5 0.0 copy-start.7
  6.5 0.1 shard_map.84
  6.6 0.5 %collective-permute-start.2 = (bf16[2,16,1280]{2,1,0:T(8,128)(2,1)S(1)}, bf16[2,16,1280]{2,1,0:T(8,128)(2,1)S(1)}, u32[]{:S(2)}, u32[]{:S(2)}) collective-permute-start(bf16[2,16,1280]{2,1,0:T(8,128)(2,1)S(1)} %get-tuple-element.35), channel_id=1, source_target_pairs={{0,4},{4,0},{8,12},{12,8},{1,5},{5,1},{9,13},{13,9},{2,6},{6,2},{1... | collective-permute-start | bytes 245768 | tf_op jit(solution)/shard_map/ppermute | solution.py:830
  7.1 4.6 %collective-permute-start.3 = (bf16[2,16,1280]{2,1,0:T(8,128)(2,1)S(1)}, bf16[2,16,1280]{2,1,0:T(8,128)(2,1)S(1)}, u32[]{:S(2)}, u32[]{:S(2)}) collective-permute-start(bf16[2,16,1280]{2,1,0:T(8,128)(2,1)S(1)} %get-tuple-element.36), channel_id=1, source_target_pairs={{4,8},{8,4},{5,9},{9,5},{6,10},{10,6},{7,11},{11,7},{20,24},{24,20... | collective-permute-start | bytes 245768 | tf_op jit(solution)/shard_map/ppermute | solution.py:831
  11.7 1.6 %collective-permute-start.4 = (f32[8,256]{1,0:T(8,128)S(1)}, f32[8,256]{1,0:T(8,128)S(1)}, u32[]{:S(2)}, u32[]{:S(2)}) collective-permute-start(f32[8,256]{1,0:T(8,128)S(1)} %get-tuple-element.39.refs_3_), channel_id=1, source_target_pairs={{0,16},{16,0},{1,17},{17,1},{2,18},{18,2},{3,19},{19,3},{4,20},{20... | collective-permute-start | bytes 24584 | tf_op jit(solution)/shard_map/ppermute | solution.py:798
  13.3 2.2 %collective-permute-done.4.refs_4_ = f32[8,256]{1,0:T(8,128)S(1)} collective-permute-done((f32[8,256]{1,0:T(8,128)S(1)}, f32[8,256]{1,0:T(8,128)S(1)}, u32[]{:S(2)}, u32[]{:S(2)}) %collective-permute-start.4) | collective-permute-done | bytes 8224 | tf_op jit(solution)/shard_map/ppermute | solution.py:798
  15.4 0.0 copy-done.7
  15.4 0.7 %shard_map.85 = (bf16[2,2,256,256]{3,2,1,0:T(8,128)(2,1)S(1)}, f32[2,2,160,128]{3,2,1,0:T(8,128)S(1)}, f32[2,2,144,128]{3,2,1,0:T(8,128)S(1)}, f32[2,8,128]{2,1,...) custom-call(bf16[160,128]{1,0:T(8,128)(2,1)S(1)} %collective-permute-done.got_a.refs_0_, ...), custom_call_target="tpu_custom_call" | custom-call | flops 20000000 | tf_op jit(solution)/shard_map/pallas_call | solution.py:768
  16.1 0.0 collective-permute-done.2.got_c
  16.2 0.0 collective-permute-done.3.got_d
  16.2 6.4 %shard_map.86 = (bf16[2,128,128]{2,1,0:T(8,128)(2,1)S(1)}, bf16[2,144,1280]{2,1,0:T(8,128)(2,1)S(1)}) custom-call(bf16[2,128,1024]{2,1,0:T(8,128)(2,1)S(1)} %get-tuple-element.31.xt, bf16[2,128,256]{2,1,0:T(8,128)(2,1)S(1)} %get-tuple-element.34.strip, bf16[2,16,1280]{2,1,0:T(8,128)(2,1)S(1)} %collective-permute-done.2.got_c, ...), custom_call_target="tpu_custom_call" | custom-call | flops 200000000 | tf_op jit(solution)/shard_map/pallas_call | solution.py:768
  22.5 1.6 %collective-permute-start.5 = (bf16[2,128,128]{2,1,0:T(8,128)(2,1)S(1)}, bf16[2,128,128]{2,1,0:T(8,128)(2,1)S(1)}, u32[]{:S(2)}, u32[]{:S(2)}) collective-permute-start(bf16[2,128,128]{2,1,0:T(8,128)(2,1)S(1)} %get-tuple-element.54), channel_id=1, source_target_pairs={{0,16},{16,0},{1,17},{17,1},{2,18},{18,2},{3,19},{19,3},{4,20},{20... | collective-permute-start | bytes 196616 | tf_op jit(solution)/shard_map/ppermute | solution.py:862
  24.1 0.7 %shard_map.87 = f32[2,128,128]{2,1,0:T(8,128)S(1)} custom-call(bf16[2,144,1280]{2,1,0:T(8,128)(2,1)S(1)} %get-tuple-element.53.x2, bf16[2,256,256]{2,1,0:T(8,128)(2,1)S(1)} %get-tuple-element.41.v1, bf16[2,2,128,256]{3,2,1,0:T(8,128)(2,1)S(1)} %get-tuple-element.42.v2, f32[2,8,256]{2,1,0:T(8,128)S(1)} %get-tuple-element.43.o2, ...), custom_call_target="tpu_custom_call" | custom-call | flops 20000000 | tf_op jit(solution)/shard_map/pallas_call | solution.py:768
  24.8 2.1 %collective-permute-done.5 = bf16[2,128,128]{2,1,0:T(8,128)(2,1)S(1)} collective-permute-done((bf16[2,128,128]{2,1,0:T(8,128)(2,1)S(1)}, bf16[2,128,128]{2,1,0:T(8,128)(2,1)S(1)}, u32[]{:S(2)}, u32[]{:S(2)}) %collective-permute-start.5) | collective-permute-done | bytes 65568 | tf_op jit(solution)/shard_map/ppermute | solution.py:862
  26.9 0.7 %add_bitcast_fusion = f32[2,1,128,128]{3,2,1,0:T(8,128)} fusion(f32[2,128,128]{2,1,0:T(8,128)S(1)} %shard_map.87, bf16[2,128,128]{2,1,0:T(8,128)(2,1)S(1)} %collective-permute-done.5), kind=kLoop, calls=%fused_computation | loop fusion | flops 65536 | bytes 327680 | tf_op jit(solution)/shard_map/broadcast_in_dim | solution.py:870
Async XLA Ops:
  0.0 0.9 %copy-start.1 = (bf16[3,2,2,4,256]{4,3,2,1,0:T(4,128)(2,1)S(1)}, bf16[3,2,2,4,256]{4,3,2,1,0:T(4,128)(2,1)}, u32[]{:S(2)}) copy-start(bf16[3,2,2,4,256]{4,3,2,1,0:T(4,128)(2,1)} %refs_4_.1) | copy-start | bytes 73732
  0.0 0.9 %copy-start.6 = (f32[4,3,2,256]{3,2,1,0:T(2,128)S(1)}, f32[4,3,2,256]{3,2,1,0:T(2,128)}, u32[]{:S(2)}) copy-start(f32[4,3,2,256]{3,2,1,0:T(2,128)} %pb.1) | copy-start | bytes 73732
  0.0 0.9 %copy-start.2 = (s32[3,2,2,256]{3,2,1,0:T(2,128)S(1)}, s32[3,2,2,256]{3,2,1,0:T(2,128)}, u32[]{:S(2)}) copy-start(s32[3,2,2,256]{3,2,1,0:T(2,128)} %refs_2_.1) | copy-start | bytes 36868
  0.0 0.9 %copy-start.3 = (s32[3,2,2,256]{3,2,1,0:T(2,128)S(1)}, s32[3,2,2,256]{3,2,1,0:T(2,128)}, u32[]{:S(2)}) copy-start(s32[3,2,2,256]{3,2,1,0:T(2,128)} %refs_3_.1) | copy-start | bytes 36868
  0.0 0.9 %copy-start.4 = (f32[3,2,2,256]{3,2,1,0:T(2,128)S(1)}, f32[3,2,2,256]{3,2,1,0:T(2,128)}, u32[]{:S(2)}) copy-start(f32[3,2,2,256]{3,2,1,0:T(2,128)} %refs_5_.2) | copy-start | bytes 36868
  0.0 0.9 %copy-start.5 = (f32[3,2,256]{2,1,0:T(2,128)S(1)}, f32[3,2,256]{2,1,0:T(2,128)}, u32[]{:S(2)}) copy-start(f32[3,2,256]{2,1,0:T(2,128)} %refs_6_.1) | copy-start | bytes 18436
  1.1 5.1 %collective-permute-start = (bf16[160,128]{1,0:T(8,128)(2,1)S(1)}, bf16[160,128]{1,0:T(8,128)(2,1)S(1)}, u32[]{:S(2)}, u32[]{:S(2)}) collective-permute-start(bf16[160,128]{1,0:T(8,128)(2,1)S(1)} %get-tuple-element.32), channel_id=1, source_target_pairs={{0,1},{1,0},{2,3},{3,2},{4,5},{5,4},{6,7},{7,6},{8,9},{9,8},{10,11... | collective-permute-start | bytes 122888 | tf_op jit(solution)/shard_map/ppermute | solution.py:796
  1.1 5.3 %collective-permute-start.1 = (bf16[160,128]{1,0:T(8,128)(2,1)S(1)}, bf16[160,128]{1,0:T(8,128)(2,1)S(1)}, u32[]{:S(2)}, u32[]{:S(2)}) collective-permute-start(bf16[160,128]{1,0:T(8,128)(2,1)S(1)} %get-tuple-element.33), channel_id=1, source_target_pairs={{1,2},{2,1},{5,6},{6,5},{9,10},{10,9},{13,14},{14,13},{17,18},{18,... | collective-permute-start | bytes 122888 | tf_op jit(solution)/shard_map/ppermute | solution.py:797
  3.7 1.0 %copy-start = (bf16[4,2,256,128]{3,2,1,0:T(8,128)(2,1)S(1)}, bf16[4,2,256,128]{3,2,1,0:T(8,128)(2,1)}, u32[]{:S(2)}) copy-start(bf16[4,2,256,128]{3,2,1,0:T(8,128)(2,1)} %refs_0_.1) | copy-start | bytes 1572868
  6.5 9.0 %copy-start.7 = (f32[8,256]{1,0:T(8,128)S(1)}, f32[8,256]{1,0:T(8,128)}, u32[]{:S(2)}) copy-start(f32[8,256]{1,0:T(8,128)} %refs_5_.3) | copy-start | bytes 24580
  6.6 9.6 %collective-permute-start.2 = (bf16[2,16,1280]{2,1,0:T(8,128)(2,1)S(1)}, bf16[2,16,1280]{2,1,0:T(8,128)(2,1)S(1)}, u32[]{:S(2)}, u32[]{:S(2)}) collective-permute-start(bf16[2,16,1280]{2,1,0:T(8,128)(2,1)S(1)} %get-tuple-element.35), channel_id=1, source_target_pairs={{0,4},{4,0},{8,12},{12,8},{1,5},{5,1},{9,13},{13,9},{2,6},{6,2},{1... | collective-permute-start | bytes 245768 | tf_op jit(solution)/shard_map/ppermute | solution.py:830
  7.1 9.0 %collective-permute-start.3 = (bf16[2,16,1280]{2,1,0:T(8,128)(2,1)S(1)}, bf16[2,16,1280]{2,1,0:T(8,128)(2,1)S(1)}, u32[]{:S(2)}, u32[]{:S(2)}) collective-permute-start(bf16[2,16,1280]{2,1,0:T(8,128)(2,1)S(1)} %get-tuple-element.36), channel_id=1, source_target_pairs={{4,8},{8,4},{5,9},{9,5},{6,10},{10,6},{7,11},{11,7},{20,24},{24,20... | collective-permute-start | bytes 245768 | tf_op jit(solution)/shard_map/ppermute | solution.py:831
  11.7 3.7 %collective-permute-start.4 = (f32[8,256]{1,0:T(8,128)S(1)}, f32[8,256]{1,0:T(8,128)S(1)}, u32[]{:S(2)}, u32[]{:S(2)}) collective-permute-start(f32[8,256]{1,0:T(8,128)S(1)} %get-tuple-element.39.refs_3_), channel_id=1, source_target_pairs={{0,16},{16,0},{1,17},{17,1},{2,18},{18,2},{3,19},{19,3},{4,20},{20... | collective-permute-start | bytes 24584 | tf_op jit(solution)/shard_map/ppermute | solution.py:798
  22.5 4.3 %collective-permute-start.5 = (bf16[2,128,128]{2,1,0:T(8,128)(2,1)S(1)}, bf16[2,128,128]{2,1,0:T(8,128)(2,1)S(1)}, u32[]{:S(2)}, u32[]{:S(2)}) collective-permute-start(bf16[2,128,128]{2,1,0:T(8,128)(2,1)S(1)} %get-tuple-element.54), channel_id=1, source_target_pairs={{0,16},{16,0},{1,17},{17,1},{2,18},{18,2},{3,19},{19,3},{4,20},{20... | collective-permute-start | bytes 196616 | tf_op jit(solution)/shard_map/ppermute | solution.py:862

commit v2 on v1

--- a/solution.py
+++ b/solution.py
@@ -162,6 +162,7 @@
 SEG = 4 * EDGE
 FIELDS = 3 + TAPS
 VMEM_LIMIT = 24 * 1024 * 1024
+COVER_FLOPS = 400_000_000
 
 
 def tables_of(slots):
@@ -198,9 +199,15 @@
     return lax.broadcasted_iota(jnp.int32, shape, dim)
 
 
-def pack_kernel(slots, head, tail, bo, ro, bt, rf, pb, pr, out_a, out_b, p_ref, base_ref):
+def blank_kernel(out):
+    out[...] = jnp.zeros_like(out)
+
+
+def pack_kernel(slots, blank, sub, bo, ro, bt, rf, pb, pr, fp, out_a, out_b, p_ref, base_ref):
     row, rows = tables_of(slots)
-    p_ref[...] = jnp.zeros_like(p_ref)
+    beams = p_ref.shape[1]
+    for t in range(beams // LANES):
+        p_ref[rows - 8 :, t * LANES : (t + 1) * LANES] = blank[...]
     for lv in range(LEVELS - 1):
         for c in range(2):
             for h in range(2):
@@ -235,9 +242,9 @@
         high = x.astype(BF16)
         return high, (x - high.astype(F32)).astype(BF16)
 
-    def fill(out, sub, tile, start):
+    def fill(out, first, tile, start):
         n = slots * 2 * EDGE
-        out[:n] = sub[...].reshape(n, LANES)
+        out[:n] = sub[:, :, first : first + EDGE].reshape(n, LANES)
         high, low = packed(tile, start)
         m = high.shape[0]
         out[n : n + m] = high
@@ -247,17 +254,31 @@
 
     @pl.when(even)
     def _():
-        fill(out_a, tail, beams - LANES, LANES - EDGE)
-        fill(out_b, head, 0, 0)
+        fill(out_a, beams - EDGE, beams - LANES, LANES - EDGE)
+        fill(out_b, 0, 0, 0)
 
     @pl.when(jnp.logical_not(even))
     def _():
-        fill(out_a, head, 0, 0)
-        fill(out_b, tail, beams - LANES, LANES - EDGE)
+        fill(out_a, 0, 0, 0)
+        fill(out_b, beams - EDGE, beams - LANES, LANES - EDGE)
 
 
 def turned(x):
     return x.astype(F32).T.astype(BF16)
+
+
+def sincos(x):
+    k = jnp.floor(x * (2.0 / math.pi) + 0.5)
+    r = x - k * 1.5703125
+    r = r - k * 4.838267948966e-4
+    q = k.astype(jnp.int32)
+    z = r * r
+    s = r + r * z * (-1.6666654611e-1 + z * (8.3321608736e-3 + z * -1.9515295891e-4))
+    c = 1.0 - 0.5 * z + z * z * (4.166664568298827e-2 + z * (-1.388731625493765e-3 + z * 2.443315711809948e-5))
+    odd = q % 2 != 0
+    sin, cos = jnp.where(odd, c, s), jnp.where(odd, s, c)
+    q = q % 4
+    return jnp.where(q >= 2, -sin, sin), jnp.where((q == 1) | (q == 2), -cos, cos)
 
 
 def band(lag, taps):
@@ -272,8 +293,8 @@
     r8 = iota((8, n), 0)
     small = rate * (r8.astype(F32) * delta)
     other = jnp.where(r8 == 0, rate * (8 * delta), rate * first)
-    cs, ss = jnp.cos(small), jnp.sin(small)
-    co, so = jnp.cos(other), jnp.sin(other)
+    ss, cs = sincos(small)
+    so, co = sincos(other)
     cu, su = co[1:2], so[1:2]
     ck, sk = jnp.broadcast_to(co[0:1], (8, n)), jnp.broadcast_to(so[0:1], (8, n))
     re = cs * cu - ss * su
@@ -287,7 +308,6 @@
 
 
 def range_place(cells, lv, full):
-    reach = (LEVELS - 1 - lv) * HALO
     lead = (EDGE - HALO * (lv + 1)) if lv < LEVELS - 1 else 0
     at = lax.axis_index("rng") * cells - lead
     first = at.astype(F32) / full - 0.5
@@ -299,15 +319,19 @@
     return -(-need // 16) * 16
 
 
-def main_tables_kernel(slots, full, sub, p_ref, bo, ro, bt, rf, pr, xt, w1, w2, v1, v2, o2, e_refs, th):
-    row, rows = tables_of(slots)
-    total = 2 * slots
-    cells = sub.shape[3]
+def turn_mains_kernel(slots, sub, xt):
     beams = sub.shape[2]
-    tiles = beams // LANES
     for s in range(slots):
         for x in range(2):
             xt[x, :, s * beams : (s + 1) * beams] = turned(sub[s, x])
+
+
+def main_tables_kernel(slots, full, p_ref, bo, ro, bt, rf, pr, w1, w2, v1, v2, o2, e_refs, th):
+    row, _ = tables_of(slots)
+    total = 2 * slots
+    beams = p_ref.shape[1]
+    cells = LANES
+    tiles = beams // LANES
 
     w1[...] = jnp.zeros_like(w1)
     w2[...] = jnp.zeros_like(w2)
@@ -392,11 +416,10 @@
     at = row["b", 0, 0, 0]
     n = slots * (LEVELS - 1) * 2
     base = p_ref[at : at + n, :]
-    th[0] = jnp.cos(base)
-    th[1] = jnp.sin(base)
-
-
-def strip_kernel(slots, got_a, got_b, head, tail, xt, strip, out_c, out_d, nat):
+    th[1], th[0] = sincos(base)
+
+
+def strip_kernel(slots, got_a, got_b, sub, xt, strip, out_c, out_d, nat):
     beams = slots * SEG
     even = lax.axis_index("ang") % 2 == 0
 
@@ -409,8 +432,8 @@
 
     for s in range(slots):
         for x in range(2):
-            nat[x, s * SEG : s * SEG + EDGE] = tail[s, x]
-            nat[x, s * SEG + 3 * EDGE : (s + 1) * SEG] = head[s, x]
+            nat[x, s * SEG : s * SEG + EDGE] = sub[s, x, beams - EDGE :]
+            nat[x, s * SEG + 3 * EDGE : (s + 1) * SEG] = sub[s, x, :EDGE]
 
     @pl.when(even)
     def _():
@@ -443,7 +466,7 @@
         send(out_d, out_c)
 
 
-def strip_tables_kernel(slots, full, got_a, got_b, p_ref, base_ref, got_base, fp, ws, es_refs, ths, os_, th2, seg, halo):
+def strip_tables_kernel(slots, full, got_a, got_b, p_ref, ws, es_refs, ths, os_, seg, halo):
     row, rows = tables_of(slots)
     total = 2 * slots
     cells = LANES
@@ -493,7 +516,6 @@
         j = i % SEG
         return jnp.where(j < 2 * EDGE, beams - EDGE + j, j - 3 * EDGE)
 
-    base_rows = []
     for lv in range(LEVELS - 1):
         first, low, high = range_place(cells, lv, full)
         for c in range(2):
@@ -521,18 +543,20 @@
 
             phasors(rate[:, :LANES], first, 1.0 / full, rows_of(cells, lv) // 8, low, high, store)
     angles = halo[2, : 2 * 2 * (LEVELS - 1)]
-    ths[0] = jnp.cos(angles)
-    ths[1] = jnp.sin(angles)
-
+    ths[1], ths[0] = sincos(angles)
+
+
+def turn_tables(slots, base_ref, got_base, fp, th2):
+    total = 2 * slots
+    beams = fp.shape[1]
     own = lax.axis_index("aper")
     scale = 1.0 / math.sqrt(total)
     for h in range(2):
-        mine = own == h
         for t in range(beams // LANES):
             cols = slice(t * LANES, (t + 1) * LANES)
             here = jnp.where(own == 0, base_ref[:slots, cols], base_ref[slots:, cols])
             there = jnp.where(own == 0, got_base[:slots, cols], got_base[slots:, cols])
-            angles = jnp.where(mine, here, there) + fp[h * slots : (h + 1) * slots, cols]
+            angles = jnp.where(own == h, here, there) + fp[h * slots : (h + 1) * slots, cols]
             th2[0, t, :, h * LANES : (h + 1) * LANES] = jnp.cos(angles) * scale
             th2[1, t, :, h * LANES : (h + 1) * LANES] = jnp.sin(angles) * scale
 
@@ -541,30 +565,40 @@
     shift = o_row.astype(jnp.int32) + extra
     sub = iota((8, LANES), 0)
     reach = sub + shift
+    ahead = reach + 1
     return dict(
         one=jnp.broadcast_to(1.0 - f_row, (8, LANES)),
         two=jnp.broadcast_to(f_row, (8, LANES)),
-        bits=[jnp.broadcast_to(shift % (2 * b) >= b, (8, LANES)) for b in (1, 2, 4)],
-        in0=reach < 8,
-        in1=reach < 16,
-        last=sub == 7,
-    )
-
-
-def rotated(setup, v):
-    n = v.shape[0] - 1
-    spun = pltpu.roll(v, 7, 1)
-    ahead = jnp.where(setup["last"][None], spun[1:], spun[:n])
-    g = setup["one"][None] * v[:n] + setup["two"][None] * ahead
-    for b, bit in zip((1, 2, 4), setup["bits"]):
-        g = jnp.where(bit[None], pltpu.roll(g, 8 - b, 1), g)
-    return g
-
-
-def level_step(slots, total, lv, x_in, out, inter, w1, w2, ws, e_main, e_strip, th, ths, o_main, os_, row):
+        pick=(reach % 8, ahead % 8),
+        tier=((reach < 8, reach < 16), (ahead < 8, ahead < 16)),
+    )
+
+
+def spun(setup, v):
+    return [
+        jnp.stack([jnp.take_along_axis(v[i], index, axis=0, mode="promise_in_bounds") for i in range(v.shape[0])])
+        for index in setup["pick"]
+    ]
+
+
+def mixed(setup, seqs, n, wide):
+    parts = []
+    for seq, (in0, in1) in zip(seqs, setup["tier"]):
+        rest = seq[1 : n + 1]
+        if wide:
+            rest = jnp.where(in1[None], rest, seq[2 : n + 2])
+        parts.append(jnp.where(in0[None], seq[:n], rest))
+    return setup["one"][None] * parts[0] + setup["two"][None] * parts[1]
+
+
+def joined(held, new):
+    return new if held is None else [jnp.concatenate([a, b], 0) for a, b in zip(held, new)]
+
+
+def level_step(slots, total, cells, lv, x_in, out, inter, w1, w2, ws, e_main, e_strip, th, ths, o_main, os_, row):
     rows_in = x_in.shape[1]
     beams = slots * SEG
-    rows_out = out.shape[1]
+    need_rows = cells + 2 * (EDGE - HALO * (lv + 1))
     groups = slots + 1
     for g in range(groups):
         buf = inter[g % 2]
@@ -600,7 +634,7 @@
             held = [[None, None], [None, None]]
             step = 4
             done = 0
-            n_out = rows_out // 8
+            n_out = need_rows // 8
             while done < n_out:
                 n = min(step, n_out - done)
                 acc_re = acc_im = None
@@ -608,15 +642,11 @@
                     moved = []
                     for x in range(2):
                         lo = 0 if done == 0 else done + 1
-                        hi = done + n + 2
+                        hi = done + n + 1
                         v = buf[c, x, t, 8 * lo : 8 * hi, :].reshape(hi - lo, 8, LANES)
-                        g_new = rotated(sets[c], v)
-                        if done == 0:
-                            seq = g_new
-                        else:
-                            seq = jnp.concatenate([held[c][x], g_new], 0)
-                        held[c][x] = seq[n : n + 1]
-                        moved.append(jnp.where(sets[c]["in0"][None], seq[:n], seq[1 : n + 1]))
+                        seqs = joined(held[c][x], spun(sets[c], v))
+                        held[c][x] = [seq[n : n + 1] for seq in seqs]
+                        moved.append(mixed(sets[c], seqs, n, False))
                     e = e_main if g < slots else e_strip
                     ecols = cols if g < slots else slice(0, LANES)
                     ec = e[c, 0, 8 * done : 8 * (done + n), ecols].reshape(n, 8, LANES)
@@ -668,7 +698,7 @@
         sum_re = sum_im = None
         for h in range(2):
             lo = 0 if done == 0 else done + 2
-            hi = min(done + n + 3, rows_in // 8)
+            hi = done + n + 2
             re = im = None
             for q in range(slots):
                 a = buf[q, 0, h, 8 * lo : 8 * hi, :].reshape(hi - lo, 8, LANES)
@@ -679,18 +709,9 @@
                 im = pi_ if im is None else im + pi_
             moved = []
             for x, v in enumerate((re, im)):
-                if hi - lo < n + (3 if done == 0 else 1):
-                    v = jnp.concatenate([v, jnp.zeros((1, 8, LANES), F32)], 0)
-                g_new = rotated(sets[h], v)
-                seq = g_new if done == 0 else jnp.concatenate([held[h][x], g_new], 0)
-                held[h][x] = seq[n : n + 2]
-                moved.append(
-                    jnp.where(
-                        sets[h]["in0"][None],
-                        seq[:n],
-                        jnp.where(sets[h]["in1"][None], seq[1 : n + 1], seq[2 : n + 2]),
-                    )
-                )
+                seqs = joined(held[h][x], spun(sets[h], v))
+                held[h][x] = [seq[n : n + 2] for seq in seqs]
+                moved.append(mixed(sets[h], seqs, n, True))
             sum_re = moved[0] if sum_re is None else sum_re + moved[0]
             sum_im = moved[1] if sum_im is None else sum_im + moved[1]
         at = pl.ds(pl.multiple_of(hf * LANES, LANES), LANES)
@@ -700,8 +721,8 @@
         done += n
 
 
-def levels_kernel(slots, full, xt, strip, got_c, got_d, w1, w2, ws, v1, v2, o2, e0, e1, e2, es0, es1, th, ths, os_, th2, p_ref, out, x2, x0, x1, inter0, inter1, buf, flat):
-    row, rows = tables_of(slots)
+def levels_kernel(slots, xt, strip, got_c, got_d, w1, w2, ws, v1, v2, o2, e0, e1, e2, es0, es1, th, ths, os_, th2, p_ref, out, x2, x0, x1, inter0, inter1, buf, flat):
+    row, _ = tables_of(slots)
     total = 2 * slots
     cells = xt.shape[1]
     mains = xt.shape[2]
@@ -724,8 +745,8 @@
         place(got_d, got_c)
 
     inter = (inter0, inter1)
-    level_step(slots, total, 0, x0, x1, inter, w1, w2, ws, e0, es0, th, ths, p_ref, os_, row)
-    level_step(slots, total, 1, x1, x2, inter, w1, w2, ws, e1, es1, th, ths, p_ref, os_, row)
+    level_step(slots, total, cells, 0, x0, x1, inter, w1, w2, ws, e0, es0, th, ths, p_ref, os_, row)
+    level_step(slots, total, cells, 1, x1, x2, inter, w1, w2, ws, e1, es1, th, ths, p_ref, os_, row)
     hf = 1 - lax.axis_index("aper")
 
     def put(done, n, re, im):
@@ -763,50 +784,62 @@
     return pairs
 
 
-def call(kernel, outs, args, scratch=(), flops=0, specs=None):
+def call(kernel, outs, args, scratch=(), sems=(), flops=0, specs=None):
     vm = pl.BlockSpec(memory_space=pltpu.VMEM)
     return pl.pallas_call(
         kernel,
         out_shape=[jax.ShapeDtypeStruct(s, d) for s, d in outs],
         in_specs=specs or [vm] * len(args),
         out_specs=[vm] * len(outs),
-        scratch_shapes=[pltpu.VMEM(s, d) for s, d in scratch],
+        scratch_shapes=[pltpu.VMEM(s, d) for s, d in scratch] + list(sems),
         compiler_params=pltpu.CompilerParams(vmem_limit_bytes=VMEM_LIMIT),
         cost_estimate=pl.CostEstimate(flops=flops, bytes_accessed=0, transcendentals=0),
     )(*args)
 
 
-def fast_body(subimages, beam_offsets, range_offsets, beam_taps, range_frac, phase_base, phase_rate, final_phase):
-    slots, _, beams, cells = subimages.shape
+def fast_body(*args):
+    slots, _, beams, cells = args[0].shape
     full = cells * lax.axis_size("rng")
-    row, rows = tables_of(slots)
+    _, rows = tables_of(slots)
     m = (rows // 8 + LANES // EDGE - 1) // (LANES // EDGE) * 8
     msg = slots * 2 * EDGE + 2 * m
-    head = subimages[:, :, :EDGE]
-    tail = subimages[:, :, beams - EDGE :]
-    vm = pl.BlockSpec(memory_space=pltpu.VMEM)
     lv_rows = [rows_of(cells, lv) for lv in range(LEVELS - 1)]
-
+    n_th = slots * (LEVELS - 1) * 2
+    tiles = beams // LANES
+    subimages, beam_offsets, range_offsets, beam_taps, range_frac, _, phase_rate, final_phase = args
+    (blank,) = call(blank_kernel, [((8, LANES), F32)], (), flops=COVER_FLOPS)
     out_a, out_b, params, bases = call(
         functools.partial(pack_kernel, slots),
         [((msg, LANES), BF16), ((msg, LANES), BF16), ((rows, beams), F32), ((2 * slots, beams), F32)],
-        (head, tail, beam_offsets, range_offsets, beam_taps, range_frac, phase_base, phase_rate),
+        (blank,) + args,
         flops=1000,
     )
     got_a = lax.ppermute(out_a, "ang", swap_even("ang"))
     got_b = lax.ppermute(out_b, "ang", swap_odd("ang"))
     got_base = lax.ppermute(bases, "aper", swap_even("aper"))
+    (xt,) = call(
+        functools.partial(turn_mains_kernel, slots),
+        [((2, cells, slots * beams), BF16)],
+        (subimages,),
+        flops=1_000_000,
+    )
+    strip, out_c, out_d = call(
+        functools.partial(strip_kernel, slots),
+        [((2, cells, beams), BF16)] + [((2, EDGE, (slots + 1) * beams), BF16)] * 2,
+        (got_a, got_b, subimages, xt),
+        scratch=[((2, beams, cells), BF16)],
+        flops=1000,
+    )
+    got_c = lax.ppermute(out_c, "rng", swap_even("rng"))
+    got_d = lax.ppermute(out_d, "rng", swap_odd("rng"))
 
     def main_tables(*refs):
-        ins, outs = refs[:7], refs[7:]
-        main_tables_kernel(slots, full, *ins, *outs[:6], outs[6 : 6 + LEVELS], outs[6 + LEVELS])
-
-    n_th = slots * (LEVELS - 1) * 2
-    tiles = beams // LANES
-    res = call(
+        ins, outs = refs[:6], refs[6:]
+        main_tables_kernel(slots, full, *ins, *outs[:5], outs[5 : 5 + LEVELS], outs[5 + LEVELS])
+
+    w1, w2, v1, v2, o2, e0, e1, e2, th = call(
         main_tables,
         [
-            ((2, cells, slots * beams), BF16),
             ((LEVELS - 1, 2, 2, beams, beams), BF16),
             ((LEVELS - 1, 2, slots, LANES, beams), BF16),
             ((tiles, beams, beams), BF16),
@@ -815,24 +848,14 @@
         ]
         + [((2, 2, r, beams), F32) for r in lv_rows]
         + [((1, 2, cells, beams), F32), ((2, n_th, beams), F32)],
-        (subimages, params, beam_offsets, range_offsets, beam_taps, range_frac, phase_rate),
+        (params, beam_offsets, range_offsets, beam_taps, range_frac, phase_rate),
         flops=20_000_000,
     )
-    xt, w1, w2, v1, v2, o2, e0, e1, e2, th = res
-
-    strip, out_c, out_d = call(
-        functools.partial(strip_kernel, slots),
-        [((2, cells, beams), BF16)] + [((2, EDGE, (slots + 1) * beams), BF16)] * 2,
-        (got_a, got_b, head, tail, xt),
-        scratch=[((2, beams, cells), BF16)],
-        flops=1000,
-    )
-    got_c = lax.ppermute(out_c, "rng", swap_even("rng"))
-    got_d = lax.ppermute(out_d, "rng", swap_odd("rng"))
 
     def strip_tables(*refs):
-        ins, outs = refs[:6], refs[6:]
-        strip_tables_kernel(slots, full, *ins, outs[0], outs[1:LEVELS], *outs[LEVELS:])
+        ins, outs, more = refs[:3], refs[6:], refs[3:6]
+        strip_tables_kernel(slots, full, *ins, outs[0], outs[1:LEVELS], *outs[LEVELS : LEVELS + 2], *outs[LEVELS + 3 :])
+        turn_tables(slots, *more, outs[LEVELS + 2])
 
     ws, es0, es1, ths, os_, th2 = call(
         strip_tables,
@@ -846,14 +869,14 @@
     wide = (slots + 1) * beams
     x_rows = cells + 2 * EDGE
     sent, x2 = call(
-        functools.partial(levels_kernel, slots, full),
+        functools.partial(levels_kernel, slots),
         [((2, LANES, cells), BF16), ((2, lv_rows[1], wide), BF16)],
         (xt, strip, got_c, got_d, w1, w2, ws, v1, v2, o2, e0, e1, e2, es0, es1, th, ths, os_, th2, params),
         scratch=[
             ((2, x_rows, wide), BF16),
             ((2, lv_rows[0], wide), BF16),
-            ((2, 2, tiles, x_rows + 16, LANES), F32),
-            ((2, 2, tiles, x_rows + 16, LANES), F32),
+            ((2, 2, tiles, x_rows, LANES), F32),
+            ((2, 2, tiles, x_rows, LANES), F32),
             ((slots, 2, 2, lv_rows[1], LANES), F32),
             ((2, cells, LANES), F32),
         ],
@@ -879,7 +902,9 @@
         and cells == LANES
         and slots == 1 << LEVELS - 1
     )
-    return fast_body(*args) if fits else body(*args)
+    if not fits:
+        return body(*args)
+    return fast_body(*args)
 
 
 def solution(mesh):

time: 27.8 us -> 25.9 us (0.932)
  Pallas kernels: 9.54 us -> 7.42 us
  waiting for transfers between devices: 4.47 us -> 5.73 us
  local copies, waits for them, and re-layouts: 1.9 us -> 1 us
    ppermute x1, waiting for transfers between devices: 0.26 us -> 2.59 us  [fast_body(): got_b = lax.ppermute(out_b, 'ang', swap_odd('ang'))]
    pallas_call x6 -> x8, Pallas kernels: 9.54 us -> 7.42 us  [call(): pl.pallas_call(kernel, out_shape=[jax.ShapeDtypeStruct(s, d) for s, d in...]
    ppermute x1, waiting for transfers between devices: 2.16 us -> 1.03 us  [fast_body(): got_base = lax.ppermute(bases, 'aper', swap_even('aper'))]
    slice x1 -> x0, local copies, waits for them, and re-layouts: 0.84 us -> none  [fast_body(): tail = subimages[:, :, beams - EDGE:]]
  transfers between devices with their start and end apart: 6 -> 6, of which waited for: 3 -> 3; matrix products, arithmetic and copies ran while one was open for 0% -> 0% of each run, Pallas kernels for 11% -> 10%
where the time goes in v2:
time: 25.9 us; the launch traced here: 25.8 us
  starting transfers between devices  10.8 us (42%)
  Pallas kernels  7.42 us (29%)
  waiting for transfers between devices  5.73 us (22%)
  local copies, waits for them, and re-layouts  1 us (4%)
  other arithmetic  0.67 us (3%)
    pallas_call x8, Pallas kernels, call(): pl.pallas_call(kernel, out_shape=[jax.ShapeDtypeStruct(s, d) for s, d in...  7.42 us
    ppermute x1, starting transfers between devices, fast_body(): got_d = lax.ppermute(out_d, 'rng', swap_odd('rng'))  4.6 us
    ppermute x1, waiting for transfers between devices, fast_body(): got_b = lax.ppermute(out_b, 'ang', swap_odd('ang'))  2.59 us
    ppermute x1, starting transfers between devices, fast_body(): got_b = lax.ppermute(out_b, 'ang', swap_odd('ang'))  2.5 us
    ppermute x1, waiting for transfers between devices, fast_body(): got = lax.ppermute(sent, 'aper', swap_even('aper'))  2.11 us
    ppermute x1, starting transfers between devices, fast_body(): got_base = lax.ppermute(bases, 'aper', swap_even('aper'))  1.56 us
    ppermute x1, starting transfers between devices, fast_body(): got = lax.ppermute(sent, 'aper', swap_even('aper'))  1.54 us
    ppermute x1, waiting for transfers between devices, fast_body(): got_base = lax.ppermute(bases, 'aper', swap_even('aper'))  1.03 us
  transfers between devices with their start and end apart: 6, of which 3 were waited for; matrix products, arithmetic and copies ran while one was open for 0% of the time, Pallas kernels for 10%

profile of v2, /device:TPU:12, one launch (start us, length us, event | category | flops | bytes accessed | tf_op | source)
XLA Modules:
  0.0 25.8 jit_solution(9414086765286089194)
XLA Ops:
  0.0 0.0 copy-start
  0.0 0.0 copy-start.5
  0.0 0.0 copy-start.6
  0.0 0.0 copy-start.4
  0.0 0.0 copy-start.1
  0.0 0.0 copy-start.3
  0.0 0.0 copy-start.2
  0.0 0.0 copy-start.7
  0.1 1.0 %copy-done = bf16[4,2,256,128]{3,2,1,0:T(8,128)(2,1)S(1)} copy-done((bf16[4,2,256,128]{3,2,1,0:T(8,128)(2,1)S(1)}, bf16[4,2,256,128]{3,2,1,0:T(8,128)(2,1)}, u32[]{:S(2)}) %copy-start) | copy-done | bytes 524312
  1.0 0.0 copy-done.5
  1.0 0.0 copy-done.6
  1.0 0.0 copy-done.4
  1.1 0.0 copy-done.1
  1.1 0.0 copy-done.3
  1.1 0.0 copy-done.2
  1.1 0.0 copy-done.7
  1.1 0.1 shard_map.84
  1.2 0.1 collective-permute-start
  1.3 2.5 %collective-permute-start.1 = (bf16[160,128]{1,0:T(8,128)(2,1)S(1)}, bf16[160,128]{1,0:T(8,128)(2,1)S(1)}, u32[]{:S(2)}, u32[]{:S(2)}) collective-permute-start(bf16[160,128]{1,0:T(8,128)(2,1)S(1)} %get-tuple-element.30), channel_id=1, source_target_pairs={{1,2},{2,1},{5,6},{6,5},{9,10},{10,9},{13,14},{14,13},{17,18},{18,... | collective-permute-start | bytes 122888 | tf_op jit(solution)/shard_map/ppermute | solution.py:818
  3.8 0.2 shard_map.82.xt
  4.0 0.0 collective-permute-done.got_a.refs_0_
  4.0 2.6 %collective-permute-done.1.got_b.refs_1_ = bf16[160,128]{1,0:T(8,128)(2,1)S(1)} collective-permute-done((bf16[160,128]{1,0:T(8,128)(2,1)S(1)}, bf16[160,128]{1,0:T(8,128)(2,1)S(1)}, u32[]{:S(2)}, u32[]{:S(2)}) %collective-permute-start.1) | collective-permute-done | bytes 40992 | tf_op jit(solution)/shard_map/ppermute | solution.py:818
  6.6 0.1 shard_map.85
  6.8 0.5 %collective-permute-start.2 = (bf16[2,16,1280]{2,1,0:T(8,128)(2,1)S(1)}, bf16[2,16,1280]{2,1,0:T(8,128)(2,1)S(1)}, u32[]{:S(2)}, u32[]{:S(2)}) collective-permute-start(bf16[2,16,1280]{2,1,0:T(8,128)(2,1)S(1)} %get-tuple-element.32), channel_id=1, source_target_pairs={{0,4},{4,0},{8,12},{12,8},{1,5},{5,1},{9,13},{13,9},{2,6},{6,2},{1... | collective-permute-start | bytes 245768 | tf_op jit(solution)/shard_map/ppermute | solution.py:833
  7.3 4.6 %collective-permute-start.3 = (bf16[2,16,1280]{2,1,0:T(8,128)(2,1)S(1)}, bf16[2,16,1280]{2,1,0:T(8,128)(2,1)S(1)}, u32[]{:S(2)}, u32[]{:S(2)}) collective-permute-start(bf16[2,16,1280]{2,1,0:T(8,128)(2,1)S(1)} %get-tuple-element.33), channel_id=1, source_target_pairs={{4,8},{8,4},{5,9},{9,5},{6,10},{10,6},{7,11},{11,7},{20,24},{24,20... | collective-permute-start | bytes 245768 | tf_op jit(solution)/shard_map/ppermute | solution.py:834
  11.9 1.6 %collective-permute-start.4 = (f32[8,256]{1,0:T(8,128)S(1)}, f32[8,256]{1,0:T(8,128)S(1)}, u32[]{:S(2)}, u32[]{:S(2)}) collective-permute-start(f32[8,256]{1,0:T(8,128)S(1)} %get-tuple-element.37.refs_3_), channel_id=1, source_target_pairs={{0,16},{16,0},{1,17},{17,1},{2,18},{18,2},{3,19},{19,3},{4,20},{20... | collective-permute-start | bytes 24584 | tf_op jit(solution)/shard_map/ppermute | solution.py:819
  13.4 1.1 %shard_map.86 = (bf16[2,2,2,256,256]{4,3,2,1,0:T(8,128)(2,1)S(1)}, bf16[2,2,4,128,256]{4,3,2,1,0:T(8,128)(2,1)S(1)}, bf16[2,256,256]{2,1,0:T(8,128)(2,1)S(1)}, b...) custom-call(f32[80,256]{1,0:T(8,128)S(1)} %get-tuple-element.34.refs, ...), custom_call_target="tpu_custom_call" | custom-call | flops 20000000 | tf_op jit(solution)/shard_map/pallas_call | solution.py:789
  14.6 1.0 %collective-permute-done.4.refs_4_ = f32[8,256]{1,0:T(8,128)S(1)} collective-permute-done((f32[8,256]{1,0:T(8,128)S(1)}, f32[8,256]{1,0:T(8,128)S(1)}, u32[]{:S(2)}, u32[]{:S(2)}) %collective-permute-start.4) | collective-permute-done | bytes 8224 | tf_op jit(solution)/shard_map/ppermute | solution.py:819
  15.6 0.6 %shard_map.87 = (bf16[2,2,256,256]{3,2,1,0:T(8,128)(2,1)S(1)}, f32[2,2,160,128]{3,2,1,0:T(8,128)S(1)}, f32[2,2,144,128]{3,2,1,0:T(8,128)S(1)}, f32[2,8,128]{2,1,...) custom-call(bf16[160,128]{1,0:T(8,128)(2,1)S(1)} %collective-permute-done.got_a.refs_0_, ...), custom_call_target="tpu_custom_call" | custom-call | flops 20000000 | tf_op jit(solution)/shard_map/pallas_call | solution.py:789
  16.2 0.0 collective-permute-done.2.got_c
  16.2 0.0 collective-permute-done.3.got_d
  16.3 4.5 %shard_map.88 = (bf16[2,128,128]{2,1,0:T(8,128)(2,1)S(1)}, bf16[2,144,1280]{2,1,0:T(8,128)(2,1)S(1)}) custom-call(bf16[2,128,1024]{2,1,0:T(8,128)(2,1)S(1)} %shard_map.82.xt, bf16[2,128,256]{2,1,0:T(8,128)(2,1)S(1)} %get-tuple-element.31.strip, bf16[2,16,1280]{2,1,0:T(8,128)(2,1)S(1)} %collective-permute-done.2.got_c, ...), custom_call_target="tpu_custom_call" | custom-call | flops 200000000 | tf_op jit(solution)/shard_map/pallas_call | solution.py:789
  20.8 1.5 %collective-permute-start.5 = (bf16[2,128,128]{2,1,0:T(8,128)(2,1)S(1)}, bf16[2,128,128]{2,1,0:T(8,128)(2,1)S(1)}, u32[]{:S(2)}, u32[]{:S(2)}) collective-permute-start(bf16[2,128,128]{2,1,0:T(8,128)(2,1)S(1)} %get-tuple-element.52), channel_id=1, source_target_pairs={{0,16},{16,0},{1,17},{17,1},{2,18},{18,2},{3,19},{19,3},{4,20},{20... | collective-permute-start | bytes 196616 | tf_op jit(solution)/shard_map/ppermute | solution.py:885
  22.3 0.7 %shard_map.89 = f32[2,128,128]{2,1,0:T(8,128)S(1)} custom-call(bf16[2,144,1280]{2,1,0:T(8,128)(2,1)S(1)} %get-tuple-element.51.x2, bf16[2,256,256]{2,1,0:T(8,128)(2,1)S(1)} %get-tuple-element.39.v1, bf16[2,2,128,256]{3,2,1,0:T(8,128)(2,1)S(1)} %get-tuple-element.40.v2, f32[2,8,256]{2,1,0:T(8,128)S(1)} %get-tuple-element.41.o2, ...), custom_call_target="tpu_custom_call" | custom-call | flops 20000000 | tf_op jit(solution)/shard_map/pallas_call | solution.py:789
  23.0 2.1 %collective-permute-done.5 = bf16[2,128,128]{2,1,0:T(8,128)(2,1)S(1)} collective-permute-done((bf16[2,128,128]{2,1,0:T(8,128)(2,1)S(1)}, bf16[2,128,128]{2,1,0:T(8,128)(2,1)S(1)}, u32[]{:S(2)}, u32[]{:S(2)}) %collective-permute-start.5) | collective-permute-done | bytes 65568 | tf_op jit(solution)/shard_map/ppermute | solution.py:885
  25.1 0.7 %add_bitcast_fusion = f32[2,1,128,128]{3,2,1,0:T(8,128)} fusion(f32[2,128,128]{2,1,0:T(8,128)S(1)} %shard_map.89, bf16[2,128,128]{2,1,0:T(8,128)(2,1)S(1)} %collective-permute-done.5), kind=kLoop, calls=%fused_computation | loop fusion | flops 65536 | bytes 327680 | tf_op jit(solution)/shard_map/broadcast_in_dim | solution.py:893
  (1 shorter events, 0.0 us)
Async XLA Ops:
  0.0 1.0 %copy-start = (bf16[4,2,256,128]{3,2,1,0:T(8,128)(2,1)S(1)}, bf16[4,2,256,128]{3,2,1,0:T(8,128)(2,1)}, u32[]{:S(2)}) copy-start(bf16[4,2,256,128]{3,2,1,0:T(8,128)(2,1)} %sub.5) | copy-start | bytes 1572868
  0.0 1.0 %copy-start.5 = (f32[8,256]{1,0:T(8,128)S(1)}, f32[8,256]{1,0:T(8,128)}, u32[]{:S(2)}) copy-start(f32[8,256]{1,0:T(8,128)} %refs_5_.3) | copy-start | bytes 24580
  0.0 1.0 %copy-start.6 = (f32[3,2,256]{2,1,0:T(2,128)S(1)}, f32[3,2,256]{2,1,0:T(2,128)}, u32[]{:S(2)}) copy-start(f32[3,2,256]{2,1,0:T(2,128)} %refs_5_.2) | copy-start | bytes 18436
  0.0 1.0 %copy-start.4 = (f32[3,2,2,256]{3,2,1,0:T(2,128)S(1)}, f32[3,2,2,256]{3,2,1,0:T(2,128)}, u32[]{:S(2)}) copy-start(f32[3,2,2,256]{3,2,1,0:T(2,128)} %refs_4_.1) | copy-start | bytes 36868
  0.0 1.0 %copy-start.1 = (bf16[3,2,2,4,256]{4,3,2,1,0:T(4,128)(2,1)S(1)}, bf16[3,2,2,4,256]{4,3,2,1,0:T(4,128)(2,1)}, u32[]{:S(2)}) copy-start(bf16[3,2,2,4,256]{4,3,2,1,0:T(4,128)(2,1)} %refs_3_.1) | copy-start | bytes 73732
  0.0 1.0 %copy-start.3 = (s32[3,2,2,256]{3,2,1,0:T(2,128)S(1)}, s32[3,2,2,256]{3,2,1,0:T(2,128)}, u32[]{:S(2)}) copy-start(s32[3,2,2,256]{3,2,1,0:T(2,128)} %refs_2_.1) | copy-start | bytes 36868
  0.0 1.0 %copy-start.2 = (s32[3,2,2,256]{3,2,1,0:T(2,128)S(1)}, s32[3,2,2,256]{3,2,1,0:T(2,128)}, u32[]{:S(2)}) copy-start(s32[3,2,2,256]{3,2,1,0:T(2,128)} %refs_1_.1) | copy-start | bytes 36868
  0.0 1.0 %copy-start.7 = (f32[4,3,2,256]{3,2,1,0:T(2,128)S(1)}, f32[4,3,2,256]{3,2,1,0:T(2,128)}, u32[]{:S(2)}) copy-start(f32[4,3,2,256]{3,2,1,0:T(2,128)} %pb.1) | copy-start | bytes 73732
  1.2 2.8 %collective-permute-start = (bf16[160,128]{1,0:T(8,128)(2,1)S(1)}, bf16[160,128]{1,0:T(8,128)(2,1)S(1)}, u32[]{:S(2)}, u32[]{:S(2)}) collective-permute-start(bf16[160,128]{1,0:T(8,128)(2,1)S(1)} %get-tuple-element.29), channel_id=1, source_target_pairs={{0,1},{1,0},{2,3},{3,2},{4,5},{5,4},{6,7},{7,6},{8,9},{9,8},{10,11... | collective-permute-start | bytes 122888 | tf_op jit(solution)/shard_map/ppermute | solution.py:817
  1.3 5.3 %collective-permute-start.1 = (bf16[160,128]{1,0:T(8,128)(2,1)S(1)}, bf16[160,128]{1,0:T(8,128)(2,1)S(1)}, u32[]{:S(2)}, u32[]{:S(2)}) collective-permute-start(bf16[160,128]{1,0:T(8,128)(2,1)S(1)} %get-tuple-element.30), channel_id=1, source_target_pairs={{1,2},{2,1},{5,6},{6,5},{9,10},{10,9},{13,14},{14,13},{17,18},{18,... | collective-permute-start | bytes 122888 | tf_op jit(solution)/shard_map/ppermute | solution.py:818
  6.8 9.5 %collective-permute-start.2 = (bf16[2,16,1280]{2,1,0:T(8,128)(2,1)S(1)}, bf16[2,16,1280]{2,1,0:T(8,128)(2,1)S(1)}, u32[]{:S(2)}, u32[]{:S(2)}) collective-permute-start(bf16[2,16,1280]{2,1,0:T(8,128)(2,1)S(1)} %get-tuple-element.32), channel_id=1, source_target_pairs={{0,4},{4,0},{8,12},{12,8},{1,5},{5,1},{9,13},{13,9},{2,6},{6,2},{1... | collective-permute-start | bytes 245768 | tf_op jit(solution)/shard_map/ppermute | solution.py:833
  7.3 9.0 %collective-permute-start.3 = (bf16[2,16,1280]{2,1,0:T(8,128)(2,1)S(1)}, bf16[2,16,1280]{2,1,0:T(8,128)(2,1)S(1)}, u32[]{:S(2)}, u32[]{:S(2)}) collective-permute-start(bf16[2,16,1280]{2,1,0:T(8,128)(2,1)S(1)} %get-tuple-element.33), channel_id=1, source_target_pairs={{4,8},{8,4},{5,9},{9,5},{6,10},{10,6},{7,11},{11,7},{20,24},{24,20... | collective-permute-start | bytes 245768 | tf_op jit(solution)/shard_map/ppermute | solution.py:834
  11.9 3.7 %collective-permute-start.4 = (f32[8,256]{1,0:T(8,128)S(1)}, f32[8,256]{1,0:T(8,128)S(1)}, u32[]{:S(2)}, u32[]{:S(2)}) collective-permute-start(f32[8,256]{1,0:T(8,128)S(1)} %get-tuple-element.37.refs_3_), channel_id=1, source_target_pairs={{0,16},{16,0},{1,17},{17,1},{2,18},{18,2},{3,19},{19,3},{4,20},{20... | collective-permute-start | bytes 24584 | tf_op jit(solution)/shard_map/ppermute | solution.py:819
  20.8 4.3 %collective-permute-start.5 = (bf16[2,128,128]{2,1,0:T(8,128)(2,1)S(1)}, bf16[2,128,128]{2,1,0:T(8,128)(2,1)S(1)}, u32[]{:S(2)}, u32[]{:S(2)}) collective-permute-start(bf16[2,128,128]{2,1,0:T(8,128)(2,1)S(1)} %get-tuple-element.52), channel_id=1, source_target_pairs={{0,16},{16,0},{1,17},{17,1},{2,18},{18,2},{3,19},{19,3},{4,20},{20... | collective-permute-start | bytes 196616 | tf_op jit(solution)/shard_map/ppermute | solution.py:885

commit v3 on v2

--- a/solution.py
+++ b/solution.py
@@ -162,7 +162,7 @@
 SEG = 4 * EDGE
 FIELDS = 3 + TAPS
 VMEM_LIMIT = 24 * 1024 * 1024
-COVER_FLOPS = 400_000_000
+COVER_FLOPS = 2_000_000_000
 
 
 def tables_of(slots):
@@ -288,7 +288,7 @@
     return out.astype(BF16)
 
 
-def phasors(rate, first, delta, count, low, high, store):
+def phasors(rate, first, delta, count, low, high, lead, cells, turns, store):
     n = rate.shape[1]
     r8 = iota((8, n), 0)
     small = rate * (r8.astype(F32) * delta)
@@ -297,21 +297,29 @@
     so, co = sincos(other)
     cu, su = co[1:2], so[1:2]
     ck, sk = jnp.broadcast_to(co[0:1], (8, n)), jnp.broadcast_to(so[0:1], (8, n))
-    re = cs * cu - ss * su
-    im = ss * cu + cs * su
-    for j in range(count):
-        ids = r8 + 8 * j
-        keep = jnp.logical_and(ids >= low, ids < high)
-        store(j, jnp.where(keep, re, 0.0), jnp.where(keep, im, 0.0))
-        if j + 1 < count:
-            re, im = re * ck - im * sk, im * ck + re * sk
+    base_re = cs * cu - ss * su
+    base_im = ss * cu + cs * su
+    for at, turn in enumerate(turns):
+        re, im = base_re, base_im
+        if turn is not None:
+            ct, st = turn
+            re, im = re * ct - im * st, im * ct + re * st
+        for j in range(count):
+            if 8 * j < lead or 8 * j + 8 > lead + cells:
+                ids = r8 + 8 * j
+                keep = jnp.logical_and(ids >= low, ids < high)
+                store(at, j, jnp.where(keep, re, 0.0), jnp.where(keep, im, 0.0))
+            else:
+                store(at, j, re, im)
+            if j + 1 < count:
+                re, im = re * ck - im * sk, im * ck + re * sk
 
 
 def range_place(cells, lv, full):
     lead = (EDGE - HALO * (lv + 1)) if lv < LEVELS - 1 else 0
     at = lax.axis_index("rng") * cells - lead
     first = at.astype(F32) / full - 0.5
-    return first, -at, full - at
+    return first, -at, full - at, lead
 
 
 def rows_of(cells, lv):
@@ -326,7 +334,7 @@
             xt[x, :, s * beams : (s + 1) * beams] = turned(sub[s, x])
 
 
-def main_tables_kernel(slots, full, p_ref, bo, ro, bt, rf, pr, w1, w2, v1, v2, o2, e_refs, th):
+def main_tables_kernel(slots, full, p_ref, bo, ro, bt, rf, pr, w1, w2, v1, v2, o2, f_refs):
     row, _ = tables_of(slots)
     total = 2 * slots
     beams = p_ref.shape[1]
@@ -398,25 +406,26 @@
             o2[t, 0:1, outs] = (ro[lv, own, h : h + 1, cols] + HALO).astype(F32)
             o2[t, 1:2, outs] = rf[lv, own, h : h + 1, cols]
 
+    at = row["b", 0, 0, 0]
+    sin_all, cos_all = sincos(p_ref[at : at + slots * (LEVELS - 1) * 2, :])
     for lv in range(LEVELS):
-        first, low, high = range_place(cells, lv, full)
-        count = (rows_of(cells, lv) if lv < LEVELS - 1 else cells) // 8
+        first, low, high, lead = range_place(cells, lv, full)
+        count = (cells + 2 * lead) // 8
         for c in range(2 if lv < LEVELS - 1 else 1):
+            turns = [None]
             if lv < LEVELS - 1:
                 at = row["r", lv, c]
                 rate = p_ref[at : at + 1, :]
+                spots = [row["b", s, lv, c] - row["b", 0, 0, 0] for s in range(slots)]
+                turns = [(cos_all[k : k + 1], sin_all[k : k + 1]) for k in spots]
             else:
                 rate = jnp.where(own == 0, pr[lv, 0:1, :], pr[lv, 1:2, :])
 
-            def store(j, re, im):
-                e_refs[lv][c, 0, 8 * j : 8 * j + 8, :] = re
-                e_refs[lv][c, 1, 8 * j : 8 * j + 8, :] = im
-
-            phasors(rate, first, 1.0 / full, count, low, high, store)
-    at = row["b", 0, 0, 0]
-    n = slots * (LEVELS - 1) * 2
-    base = p_ref[at : at + n, :]
-    th[1], th[0] = sincos(base)
+            def store(g, j, re, im):
+                f_refs[lv][c, g, 0, 8 * j : 8 * j + 8, :] = re
+                f_refs[lv][c, g, 1, 8 * j : 8 * j + 8, :] = im
+
+            phasors(rate, first, 1.0 / full, count, low, high, lead, cells, turns, store)
 
 
 def strip_kernel(slots, got_a, got_b, sub, xt, strip, out_c, out_d, nat):
@@ -466,7 +475,7 @@
         send(out_d, out_c)
 
 
-def strip_tables_kernel(slots, full, got_a, got_b, p_ref, ws, es_refs, ths, os_, seg, halo):
+def strip_tables_kernel(slots, full, got_a, got_b, p_ref, ws, fs_refs, os_, seg, halo):
     row, rows = tables_of(slots)
     total = 2 * slots
     cells = LANES
@@ -517,7 +526,7 @@
         return jnp.where(j < 2 * EDGE, beams - EDGE + j, j - 3 * EDGE)
 
     for lv in range(LEVELS - 1):
-        first, low, high = range_place(cells, lv, full)
+        first, low, high, lead = range_place(cells, lv, full)
         for c in range(2):
             for t in range(beams // LANES):
                 cols = slice(t * LANES, (t + 1) * LANES)
@@ -535,15 +544,21 @@
                 lag = jnp.where(i_row // SEG == wanted, lag, -1)
                 ws[lv, c, :, cols] = band(lag, field[3:])
                 halo[2, at * 2 + t : at * 2 + t + 1, :] = pick(row["b", s0, lv, c], row["b", s1, lv, c])
-            rate = jnp.concatenate([pick(row["r", lv, c], row["r", lv, c])] * (beams // LANES), 1)
-
-            def store(j, re, im):
-                es_refs[lv][c, 0, 8 * j : 8 * j + 8, :] = re
-                es_refs[lv][c, 1, 8 * j : 8 * j + 8, :] = im
-
-            phasors(rate[:, :LANES], first, 1.0 / full, rows_of(cells, lv) // 8, low, high, store)
-    angles = halo[2, : 2 * 2 * (LEVELS - 1)]
-    ths[1], ths[0] = sincos(angles)
+    tiles = beams // LANES
+    sin_all, cos_all = sincos(halo[2, : 2 * tiles * (LEVELS - 1)])
+    for lv in range(LEVELS - 1):
+        first, low, high, lead = range_place(cells, lv, full)
+        for c in range(2):
+            rate = pick(row["r", lv, c], row["r", lv, c])
+            at = (lv * 2 + c) * tiles
+            turns = [(cos_all[at + t : at + t + 1], sin_all[at + t : at + t + 1]) for t in range(tiles)]
+
+            def store(t, j, re, im):
+                cols = slice(t * LANES, (t + 1) * LANES)
+                fs_refs[lv][c, 0, 8 * j : 8 * j + 8, cols] = re
+                fs_refs[lv][c, 1, 8 * j : 8 * j + 8, cols] = im
+
+            phasors(rate, first, 1.0 / full, (cells + 2 * lead) // 8, low, high, lead, cells, turns, store)
 
 
 def turn_tables(slots, base_ref, got_base, fp, th2):
@@ -595,13 +610,13 @@
     return new if held is None else [jnp.concatenate([a, b], 0) for a, b in zip(held, new)]
 
 
-def level_step(slots, total, cells, lv, x_in, out, inter, w1, w2, ws, e_main, e_strip, th, ths, o_main, os_, row):
+def level_step(slots, total, cells, lv, x_in, out, inter, w1, w2, ws, f_main, f_strip, o_main, os_, row):
     rows_in = x_in.shape[1]
     beams = slots * SEG
     need_rows = cells + 2 * (EDGE - HALO * (lv + 1))
-    groups = slots + 1
-    for g in range(groups):
-        buf = inter[g % 2]
+    order = [slots] + list(range(0, slots, 2)) + list(range(1, slots, 2))
+    for turn, g in enumerate(order):
+        buf = inter[turn % 2]
         for c in range(2):
             if g < slots:
                 k = child_of(lv, g, c, total)
@@ -620,17 +635,14 @@
                     buf[c, x, t, :rows_in, :] = val[x * rows_in : (x + 1) * rows_in, t * LANES : (t + 1) * LANES]
         for t in range(beams // LANES):
             cols = slice(t * LANES, (t + 1) * LANES)
-            sets, turn = [], []
+            sets = []
             for c in range(2):
                 if g < slots:
                     at = row["p", lv, c, half_of(lv, g, total), 0]
                     sets.append(shift_setup(o_main[at + 1 : at + 2, cols], o_main[at + 2 : at + 3, cols], 0))
-                    at = (g * (LEVELS - 1) + lv) * 2 + c
-                    turn.append([jnp.broadcast_to(th[q, at : at + 1, cols], (8, LANES))[None] for q in range(2)])
                 else:
                     at = lv * 2 + c
                     sets.append(shift_setup(os_[at, 0:1, cols], os_[at, 1:2, cols], 0))
-                    turn.append([jnp.broadcast_to(ths[q, at * 2 + t : at * 2 + t + 1, :], (8, LANES))[None] for q in range(2)])
             held = [[None, None], [None, None]]
             step = 4
             done = 0
@@ -647,12 +659,12 @@
                         seqs = joined(held[c][x], spun(sets[c], v))
                         held[c][x] = [seq[n : n + 1] for seq in seqs]
                         moved.append(mixed(sets[c], seqs, n, False))
-                    e = e_main if g < slots else e_strip
-                    ecols = cols if g < slots else slice(0, LANES)
-                    ec = e[c, 0, 8 * done : 8 * (done + n), ecols].reshape(n, 8, LANES)
-                    es = e[c, 1, 8 * done : 8 * (done + n), ecols].reshape(n, 8, LANES)
-                    tc, ts = turn[c]
-                    fc, fs = ec * tc - es * ts, es * tc + ec * ts
+                    spot = slice(8 * done, 8 * (done + n))
+                    if g < slots:
+                        fc, fs = f_main[c, g, 0, spot, cols], f_main[c, g, 1, spot, cols]
+                    else:
+                        fc, fs = f_strip[c, 0, spot, cols], f_strip[c, 1, spot, cols]
+                    fc, fs = fc.reshape(n, 8, LANES), fs.reshape(n, 8, LANES)
                     re = fc * moved[0] - fs * moved[1]
                     im = fs * moved[0] + fc * moved[1]
                     acc_re = re if acc_re is None else acc_re + re
@@ -666,7 +678,7 @@
 def last_step(slots, cells, hf, x_in, v1, v2, o2, th2, e2, buf, put):
     rows_in = x_in.shape[1]
     beams = slots * SEG
-    for q in range(slots):
+    for q in list(range(0, slots, 2)) + list(range(1, slots, 2)):
         lhs = x_in[:, :, q * beams : (q + 1) * beams].reshape(2 * rows_in, beams)
         tile = slots * beams + q * SEG // LANES * LANES
         lhs2 = x_in[:, :, tile : tile + LANES].reshape(2 * rows_in, LANES)
@@ -715,13 +727,13 @@
             sum_re = moved[0] if sum_re is None else sum_re + moved[0]
             sum_im = moved[1] if sum_im is None else sum_im + moved[1]
         at = pl.ds(pl.multiple_of(hf * LANES, LANES), LANES)
-        ec = e2[0, 0, 8 * done : 8 * (done + n), at].reshape(n, 8, LANES)
-        es = e2[0, 1, 8 * done : 8 * (done + n), at].reshape(n, 8, LANES)
+        ec = e2[0, 0, 0, 8 * done : 8 * (done + n), at].reshape(n, 8, LANES)
+        es = e2[0, 0, 1, 8 * done : 8 * (done + n), at].reshape(n, 8, LANES)
         put(done, n, ec * sum_re - es * sum_im, es * sum_re + ec * sum_im)
         done += n
 
 
-def levels_kernel(slots, xt, strip, got_c, got_d, w1, w2, ws, v1, v2, o2, e0, e1, e2, es0, es1, th, ths, os_, th2, p_ref, out, x2, x0, x1, inter0, inter1, buf, flat):
+def levels_kernel(slots, xt, strip, got_c, got_d, w1, w2, ws, v1, v2, o2, e0, e1, e2, es0, es1, os_, th2, p_ref, out, x2, x0, x1, inter0, inter1, buf, flat):
     row, _ = tables_of(slots)
     total = 2 * slots
     cells = xt.shape[1]
@@ -745,8 +757,8 @@
         place(got_d, got_c)
 
     inter = (inter0, inter1)
-    level_step(slots, total, cells, 0, x0, x1, inter, w1, w2, ws, e0, es0, th, ths, p_ref, os_, row)
-    level_step(slots, total, cells, 1, x1, x2, inter, w1, w2, ws, e1, es1, th, ths, p_ref, os_, row)
+    level_step(slots, total, cells, 0, x0, x1, inter, w1, w2, ws, e0, es0, p_ref, os_, row)
+    level_step(slots, total, cells, 1, x1, x2, inter, w1, w2, ws, e1, es1, p_ref, os_, row)
     hf = 1 - lax.axis_index("aper")
 
     def put(done, n, re, im):
@@ -804,7 +816,6 @@
     m = (rows // 8 + LANES // EDGE - 1) // (LANES // EDGE) * 8
     msg = slots * 2 * EDGE + 2 * m
     lv_rows = [rows_of(cells, lv) for lv in range(LEVELS - 1)]
-    n_th = slots * (LEVELS - 1) * 2
     tiles = beams // LANES
     subimages, beam_offsets, range_offsets, beam_taps, range_frac, _, phase_rate, final_phase = args
     (blank,) = call(blank_kernel, [((8, LANES), F32)], (), flops=COVER_FLOPS)
@@ -835,9 +846,9 @@
 
     def main_tables(*refs):
         ins, outs = refs[:6], refs[6:]
-        main_tables_kernel(slots, full, *ins, *outs[:5], outs[5 : 5 + LEVELS], outs[5 + LEVELS])
-
-    w1, w2, v1, v2, o2, e0, e1, e2, th = call(
+        main_tables_kernel(slots, full, *ins, *outs[:5], outs[5:])
+
+    w1, w2, v1, v2, o2, e0, e1, e2 = call(
         main_tables,
         [
             ((LEVELS - 1, 2, 2, beams, beams), BF16),
@@ -846,22 +857,22 @@
             ((tiles, LANES // SEG, LANES, beams), BF16),
             ((tiles, 8, beams), F32),
         ]
-        + [((2, 2, r, beams), F32) for r in lv_rows]
-        + [((1, 2, cells, beams), F32), ((2, n_th, beams), F32)],
+        + [((2, slots, 2, r, beams), F32) for r in lv_rows]
+        + [((1, 1, 2, cells, beams), F32)],
         (params, beam_offsets, range_offsets, beam_taps, range_frac, phase_rate),
         flops=20_000_000,
     )
 
     def strip_tables(*refs):
         ins, outs, more = refs[:3], refs[6:], refs[3:6]
-        strip_tables_kernel(slots, full, *ins, outs[0], outs[1:LEVELS], *outs[LEVELS : LEVELS + 2], *outs[LEVELS + 3 :])
-        turn_tables(slots, *more, outs[LEVELS + 2])
-
-    ws, es0, es1, ths, os_, th2 = call(
+        strip_tables_kernel(slots, full, *ins, outs[0], outs[1:LEVELS], outs[LEVELS], *outs[LEVELS + 2 :])
+        turn_tables(slots, *more, outs[LEVELS + 1])
+
+    ws, es0, es1, os_, th2 = call(
         strip_tables,
         [((LEVELS - 1, 2, beams, beams), BF16)]
-        + [((2, 2, r, LANES), F32) for r in lv_rows]
-        + [((2, 4 * (LEVELS - 1), LANES), F32), ((2 * (LEVELS - 1), 8, beams), F32), ((2, tiles, slots, beams), F32)],
+        + [((2, 2, r, beams), F32) for r in lv_rows]
+        + [((2 * (LEVELS - 1), 8, beams), F32), ((2, tiles, slots, beams), F32)],
         (got_a, got_b, params, bases, got_base, final_phase),
         scratch=[((rows, LANES), F32), ((3, max(m, 8), LANES), F32)],
         flops=20_000_000,
@@ -871,7 +882,7 @@
     sent, x2 = call(
         functools.partial(levels_kernel, slots),
         [((2, LANES, cells), BF16), ((2, lv_rows[1], wide), BF16)],
-        (xt, strip, got_c, got_d, w1, w2, ws, v1, v2, o2, e0, e1, e2, es0, es1, th, ths, os_, th2, params),
+        (xt, strip, got_c, got_d, w1, w2, ws, v1, v2, o2, e0, e1, e2, es0, es1, os_, th2, params),
         scratch=[
             ((2, x_rows, wide), BF16),
             ((2, lv_rows[0], wide), BF16),

time: 25.9 us -> 25.1 us (0.969)
  Pallas kernels: 7.42 us -> 6.92 us
  waiting for transfers between devices: 5.73 us -> 5.33 us
    pallas_call x8, Pallas kernels: 7.42 us -> 6.92 us  [call(): pl.pallas_call(kernel, out_shape=[jax.ShapeDtypeStruct(s, d) for s, d in...]
    ppermute x1, waiting for transfers between devices: 1.03 us -> 0.67 us  [fast_body(): got_base = lax.ppermute(bases, 'aper', swap_even('aper'))]
  transfers between devices with their start and end apart: 6 -> 6, of which waited for: 3 -> 3; matrix products, arithmetic and copies ran while one was open for 0% -> 0% of each run, Pallas kernels for 10% -> 12%
where the time goes in v3:
time: 25.1 us; the launch traced here: 24.9 us
  starting transfers between devices  10.8 us (43%)
  Pallas kernels  6.92 us (28%)
  waiting for transfers between devices  5.33 us (21%)
  local copies, waits for them, and re-layouts  1 us (4%)
  other arithmetic  0.67 us (3%)
    pallas_call x8, Pallas kernels, call(): pl.pallas_call(kernel, out_shape=[jax.ShapeDtypeStruct(s, d) for s, d in...  6.92 us
    ppermute x1, starting transfers between devices, fast_body(): got_d = lax.ppermute(out_d, 'rng', swap_odd('rng'))  4.6 us
    ppermute x1, waiting for transfers between devices, fast_body(): got_b = lax.ppermute(out_b, 'ang', swap_odd('ang'))  2.59 us
    ppermute x1, starting transfers between devices, fast_body(): got_b = lax.ppermute(out_b, 'ang', swap_odd('ang'))  2.5 us
    ppermute x1, waiting for transfers between devices, fast_body(): got = lax.ppermute(sent, 'aper', swap_even('aper'))  2.06 us
    ppermute x1, starting transfers between devices, fast_body(): got = lax.ppermute(sent, 'aper', swap_even('aper'))  1.56 us
    ppermute x1, starting transfers between devices, fast_body(): got_base = lax.ppermute(bases, 'aper', swap_even('aper'))  1.56 us
    unnamed x16, local copies, waits for them, and re-layouts  1 us
  transfers between devices with their start and end apart: 6, of which 3 were waited for; matrix products, arithmetic and copies ran while one was open for 0% of the time, Pallas kernels for 12%

profile of v3, /device:TPU:12, one launch (start us, length us, event | category | flops | bytes accessed | tf_op | source)
XLA Modules:
  0.0 24.9 jit_solution(330827856676656779)
XLA Ops:
  0.0 0.0 copy-start
  0.0 0.0 copy-start.5
  0.0 0.0 copy-start.6
  0.0 0.0 copy-start.4
  0.0 0.0 copy-start.1
  0.0 0.0 copy-start.3
  0.0 0.0 copy-start.2
  0.0 0.0 copy-start.7
  0.1 1.0 %copy-done = bf16[4,2,256,128]{3,2,1,0:T(8,128)(2,1)S(1)} copy-done((bf16[4,2,256,128]{3,2,1,0:T(8,128)(2,1)S(1)}, bf16[4,2,256,128]{3,2,1,0:T(8,128)(2,1)}, u32[]{:S(2)}) %copy-start) | copy-done | bytes 524312
  1.0 0.0 copy-done.5
  1.0 0.0 copy-done.6
  1.0 0.0 copy-done.4
  1.1 0.0 copy-done.1
  1.1 0.0 copy-done.3
  1.1 0.0 copy-done.2
  1.1 0.0 copy-done.7
  1.1 0.1 shard_map.84
  1.2 0.1 collective-permute-start
  1.3 2.5 %collective-permute-start.1 = (bf16[160,128]{1,0:T(8,128)(2,1)S(1)}, bf16[160,128]{1,0:T(8,128)(2,1)S(1)}, u32[]{:S(2)}, u32[]{:S(2)}) collective-permute-start(bf16[160,128]{1,0:T(8,128)(2,1)S(1)} %get-tuple-element.28), channel_id=1, source_target_pairs={{1,2},{2,1},{5,6},{6,5},{9,10},{10,9},{13,14},{14,13},{17,18},{18,... | collective-permute-start | bytes 122888 | tf_op jit(solution)/shard_map/ppermute | solution.py:829
  3.8 0.2 shard_map.82.xt
  4.0 0.0 collective-permute-done.got_a.refs_0_
  4.0 2.6 %collective-permute-done.1.got_b.refs_1_ = bf16[160,128]{1,0:T(8,128)(2,1)S(1)} collective-permute-done((bf16[160,128]{1,0:T(8,128)(2,1)S(1)}, bf16[160,128]{1,0:T(8,128)(2,1)S(1)}, u32[]{:S(2)}, u32[]{:S(2)}) %collective-permute-start.1) | collective-permute-done | bytes 40992 | tf_op jit(solution)/shard_map/ppermute | solution.py:829
  6.6 0.1 shard_map.85
  6.8 0.5 %collective-permute-start.2 = (bf16[2,16,1280]{2,1,0:T(8,128)(2,1)S(1)}, bf16[2,16,1280]{2,1,0:T(8,128)(2,1)S(1)}, u32[]{:S(2)}, u32[]{:S(2)}) collective-permute-start(bf16[2,16,1280]{2,1,0:T(8,128)(2,1)S(1)} %get-tuple-element.30), channel_id=1, source_target_pairs={{0,4},{4,0},{8,12},{12,8},{1,5},{5,1},{9,13},{13,9},{2,6},{6,2},{1... | collective-permute-start | bytes 245768 | tf_op jit(solution)/shard_map/ppermute | solution.py:844
  7.3 4.6 %collective-permute-start.3 = (bf16[2,16,1280]{2,1,0:T(8,128)(2,1)S(1)}, bf16[2,16,1280]{2,1,0:T(8,128)(2,1)S(1)}, u32[]{:S(2)}, u32[]{:S(2)}) collective-permute-start(bf16[2,16,1280]{2,1,0:T(8,128)(2,1)S(1)} %get-tuple-element.31), channel_id=1, source_target_pairs={{4,8},{8,4},{5,9},{9,5},{6,10},{10,6},{7,11},{11,7},{20,24},{24,20... | collective-permute-start | bytes 245768 | tf_op jit(solution)/shard_map/ppermute | solution.py:845
  11.9 1.6 %collective-permute-start.4 = (f32[8,256]{1,0:T(8,128)S(1)}, f32[8,256]{1,0:T(8,128)S(1)}, u32[]{:S(2)}, u32[]{:S(2)}) collective-permute-start(f32[8,256]{1,0:T(8,128)S(1)} %get-tuple-element.35.refs_3_), channel_id=1, source_target_pairs={{0,16},{16,0},{1,17},{17,1},{2,18},{18,2},{3,19},{19,3},{4,20},{20... | collective-permute-start | bytes 24584 | tf_op jit(solution)/shard_map/ppermute | solution.py:830
  13.4 1.5 %shard_map.86 = (bf16[2,2,2,256,256]{4,3,2,1,0:T(8,128)(2,1)S(1)}, bf16[2,2,4,128,256]{4,3,2,1,0:T(8,128)(2,1)S(1)}, bf16[2,256,256]{2,1,0:T(8,128)(2,1)S(1)}, b...) custom-call(f32[80,256]{1,0:T(8,128)S(1)} %get-tuple-element.32.refs, ...), custom_call_target="tpu_custom_call" | custom-call | flops 20000000 | tf_op jit(solution)/shard_map/pallas_call | solution.py:801
  14.9 0.7 %collective-permute-done.4.refs_4_ = f32[8,256]{1,0:T(8,128)S(1)} collective-permute-done((f32[8,256]{1,0:T(8,128)S(1)}, f32[8,256]{1,0:T(8,128)S(1)}, u32[]{:S(2)}, u32[]{:S(2)}) %collective-permute-start.4) | collective-permute-done | bytes 8224 | tf_op jit(solution)/shard_map/ppermute | solution.py:830
  15.6 0.7 %shard_map.87 = (bf16[2,2,256,256]{3,2,1,0:T(8,128)(2,1)S(1)}, f32[2,2,160,256]{3,2,1,0:T(8,128)S(1)}, f32[2,2,144,256]{3,2,1,0:T(8,128)S(1)}, f32[4,8,256]{2,1,0:T(8,128)S(1)}, f32[2,2,4,256]{3,2,1,0:T(4,128)S(1)}) custom-call(bf16[160,128]{1,0:T(8,128)(2,1)S(1)} %collective-permute-done.got_a.refs_0_, ...), custom_call_target="tpu_custom_call" | custom-call | flops 20000000 | tf_op jit(solution)/shard_map/pallas_call | solution.py:801
  16.3 0.0 collective-permute-done.2.got_c
  16.3 0.0 collective-permute-done.3.got_d
  16.3 3.6 %shard_map.88 = (bf16[2,128,128]{2,1,0:T(8,128)(2,1)S(1)}, bf16[2,144,1280]{2,1,0:T(8,128)(2,1)S(1)}) custom-call(bf16[2,128,1024]{2,1,0:T(8,128)(2,1)S(1)} %shard_map.82.xt, bf16[2,128,256]{2,1,0:T(8,128)(2,1)S(1)} %get-tuple-element.29.strip, bf16[2,16,1280]{2,1,0:T(8,128)(2,1)S(1)} %collective-permute-done.2.got_c, ...), custom_call_target="tpu_custom_call" | custom-call | flops 200000000 | tf_op jit(solution)/shard_map/pallas_call | solution.py:801
  19.9 1.6 %collective-permute-start.5 = (bf16[2,128,128]{2,1,0:T(8,128)(2,1)S(1)}, bf16[2,128,128]{2,1,0:T(8,128)(2,1)S(1)}, u32[]{:S(2)}, u32[]{:S(2)}) collective-permute-start(bf16[2,128,128]{2,1,0:T(8,128)(2,1)S(1)} %get-tuple-element.48), channel_id=1, source_target_pairs={{0,16},{16,0},{1,17},{17,1},{2,18},{18,2},{3,19},{19,3},{4,20},{20... | collective-permute-start | bytes 196616 | tf_op jit(solution)/shard_map/ppermute | solution.py:896
  21.5 0.7 %shard_map.89 = f32[2,128,128]{2,1,0:T(8,128)S(1)} custom-call(bf16[2,144,1280]{2,1,0:T(8,128)(2,1)S(1)} %get-tuple-element.47.x2, bf16[2,256,256]{2,1,0:T(8,128)(2,1)S(1)} %get-tuple-element.37.v1, bf16[2,2,128,256]{3,2,1,0:T(8,128)(2,1)S(1)} %get-tuple-element.38.v2, f32[2,8,256]{2,1,0:T(8,128)S(1)} %get-tuple-element.39.o2, ...), custom_call_target="tpu_custom_call" | custom-call | flops 20000000 | tf_op jit(solution)/shard_map/pallas_call | solution.py:801
  22.2 2.1 %collective-permute-done.5 = bf16[2,128,128]{2,1,0:T(8,128)(2,1)S(1)} collective-permute-done((bf16[2,128,128]{2,1,0:T(8,128)(2,1)S(1)}, bf16[2,128,128]{2,1,0:T(8,128)(2,1)S(1)}, u32[]{:S(2)}, u32[]{:S(2)}) %collective-permute-start.5) | collective-permute-done | bytes 65568 | tf_op jit(solution)/shard_map/ppermute | solution.py:896
  24.2 0.7 %add_bitcast_fusion = f32[2,1,128,128]{3,2,1,0:T(8,128)} fusion(f32[2,128,128]{2,1,0:T(8,128)S(1)} %shard_map.89, bf16[2,128,128]{2,1,0:T(8,128)(2,1)S(1)} %collective-permute-done.5), kind=kLoop, calls=%fused_computation | loop fusion | flops 65536 | bytes 327680 | tf_op jit(solution)/shard_map/broadcast_in_dim | solution.py:904
  (1 shorter events, 0.0 us)
Async XLA Ops:
  0.0 1.0 %copy-start = (bf16[4,2,256,128]{3,2,1,0:T(8,128)(2,1)S(1)}, bf16[4,2,256,128]{3,2,1,0:T(8,128)(2,1)}, u32[]{:S(2)}) copy-start(bf16[4,2,256,128]{3,2,1,0:T(8,128)(2,1)} %sub.5) | copy-start | bytes 1572868
  0.0 1.0 %copy-start.5 = (f32[8,256]{1,0:T(8,128)S(1)}, f32[8,256]{1,0:T(8,128)}, u32[]{:S(2)}) copy-start(f32[8,256]{1,0:T(8,128)} %refs_5_.3) | copy-start | bytes 24580
  0.0 1.0 %copy-start.6 = (f32[3,2,256]{2,1,0:T(2,128)S(1)}, f32[3,2,256]{2,1,0:T(2,128)}, u32[]{:S(2)}) copy-start(f32[3,2,256]{2,1,0:T(2,128)} %refs_5_.2) | copy-start | bytes 18436
  0.0 1.0 %copy-start.4 = (f32[3,2,2,256]{3,2,1,0:T(2,128)S(1)}, f32[3,2,2,256]{3,2,1,0:T(2,128)}, u32[]{:S(2)}) copy-start(f32[3,2,2,256]{3,2,1,0:T(2,128)} %refs_4_.1) | copy-start | bytes 36868
  0.0 1.0 %copy-start.1 = (bf16[3,2,2,4,256]{4,3,2,1,0:T(4,128)(2,1)S(1)}, bf16[3,2,2,4,256]{4,3,2,1,0:T(4,128)(2,1)}, u32[]{:S(2)}) copy-start(bf16[3,2,2,4,256]{4,3,2,1,0:T(4,128)(2,1)} %refs_3_.1) | copy-start | bytes 73732
  0.0 1.0 %copy-start.3 = (s32[3,2,2,256]{3,2,1,0:T(2,128)S(1)}, s32[3,2,2,256]{3,2,1,0:T(2,128)}, u32[]{:S(2)}) copy-start(s32[3,2,2,256]{3,2,1,0:T(2,128)} %refs_2_.1) | copy-start | bytes 36868
  0.0 1.0 %copy-start.2 = (s32[3,2,2,256]{3,2,1,0:T(2,128)S(1)}, s32[3,2,2,256]{3,2,1,0:T(2,128)}, u32[]{:S(2)}) copy-start(s32[3,2,2,256]{3,2,1,0:T(2,128)} %refs_1_.1) | copy-start | bytes 36868
  0.0 1.0 %copy-start.7 = (f32[4,3,2,256]{3,2,1,0:T(2,128)S(1)}, f32[4,3,2,256]{3,2,1,0:T(2,128)}, u32[]{:S(2)}) copy-start(f32[4,3,2,256]{3,2,1,0:T(2,128)} %pb.1) | copy-start | bytes 73732
  1.2 2.8 %collective-permute-start = (bf16[160,128]{1,0:T(8,128)(2,1)S(1)}, bf16[160,128]{1,0:T(8,128)(2,1)S(1)}, u32[]{:S(2)}, u32[]{:S(2)}) collective-permute-start(bf16[160,128]{1,0:T(8,128)(2,1)S(1)} %get-tuple-element.27), channel_id=1, source_target_pairs={{0,1},{1,0},{2,3},{3,2},{4,5},{5,4},{6,7},{7,6},{8,9},{9,8},{10,11... | collective-permute-start | bytes 122888 | tf_op jit(solution)/shard_map/ppermute | solution.py:828
  1.3 5.3 %collective-permute-start.1 = (bf16[160,128]{1,0:T(8,128)(2,1)S(1)}, bf16[160,128]{1,0:T(8,128)(2,1)S(1)}, u32[]{:S(2)}, u32[]{:S(2)}) collective-permute-start(bf16[160,128]{1,0:T(8,128)(2,1)S(1)} %get-tuple-element.28), channel_id=1, source_target_pairs={{1,2},{2,1},{5,6},{6,5},{9,10},{10,9},{13,14},{14,13},{17,18},{18,... | collective-permute-start | bytes 122888 | tf_op jit(solution)/shard_map/ppermute | solution.py:829
  6.8 9.5 %collective-permute-start.2 = (bf16[2,16,1280]{2,1,0:T(8,128)(2,1)S(1)}, bf16[2,16,1280]{2,1,0:T(8,128)(2,1)S(1)}, u32[]{:S(2)}, u32[]{:S(2)}) collective-permute-start(bf16[2,16,1280]{2,1,0:T(8,128)(2,1)S(1)} %get-tuple-element.30), channel_id=1, source_target_pairs={{0,4},{4,0},{8,12},{12,8},{1,5},{5,1},{9,13},{13,9},{2,6},{6,2},{1... | collective-permute-start | bytes 245768 | tf_op jit(solution)/shard_map/ppermute | solution.py:844
  7.3 9.0 %collective-permute-start.3 = (bf16[2,16,1280]{2,1,0:T(8,128)(2,1)S(1)}, bf16[2,16,1280]{2,1,0:T(8,128)(2,1)S(1)}, u32[]{:S(2)}, u32[]{:S(2)}) collective-permute-start(bf16[2,16,1280]{2,1,0:T(8,128)(2,1)S(1)} %get-tuple-element.31), channel_id=1, source_target_pairs={{4,8},{8,4},{5,9},{9,5},{6,10},{10,6},{7,11},{11,7},{20,24},{24,20... | collective-permute-start | bytes 245768 | tf_op jit(solution)/shard_map/ppermute | solution.py:845
  11.9 3.7 %collective-permute-start.4 = (f32[8,256]{1,0:T(8,128)S(1)}, f32[8,256]{1,0:T(8,128)S(1)}, u32[]{:S(2)}, u32[]{:S(2)}) collective-permute-start(f32[8,256]{1,0:T(8,128)S(1)} %get-tuple-element.35.refs_3_), channel_id=1, source_target_pairs={{0,16},{16,0},{1,17},{17,1},{2,18},{18,2},{3,19},{19,3},{4,20},{20... | collective-permute-start | bytes 24584 | tf_op jit(solution)/shard_map/ppermute | solution.py:830
  19.9 4.3 %collective-permute-start.5 = (bf16[2,128,128]{2,1,0:T(8,128)(2,1)S(1)}, bf16[2,128,128]{2,1,0:T(8,128)(2,1)S(1)}, u32[]{:S(2)}, u32[]{:S(2)}) collective-permute-start(bf16[2,128,128]{2,1,0:T(8,128)(2,1)S(1)} %get-tuple-element.48), channel_id=1, source_target_pairs={{0,16},{16,0},{1,17},{17,1},{2,18},{18,2},{3,19},{19,3},{4,20},{20... | collective-permute-start | bytes 196616 | tf_op jit(solution)/shard_map/ppermute | solution.py:896

commit v4 on v3

--- a/solution.py
+++ b/solution.py
@@ -610,10 +610,9 @@
     return new if held is None else [jnp.concatenate([a, b], 0) for a, b in zip(held, new)]
 
 
-def level_step(slots, total, cells, lv, x_in, out, inter, w1, w2, ws, f_main, f_strip, o_main, os_, row):
-    rows_in = x_in.shape[1]
+def level_step(slots, total, lv, x_in, spans, tile_at, out, inter, w1, w2, ws, f_main, f_strip, o_main, os_, row):
     beams = slots * SEG
-    need_rows = cells + 2 * (EDGE - HALO * (lv + 1))
+    rows_in = x_in(0, LANES).shape[1]
     order = [slots] + list(range(0, slots, 2)) + list(range(1, slots, 2))
     for turn, g in enumerate(order):
         buf = inter[turn % 2]
@@ -621,14 +620,14 @@
             if g < slots:
                 k = child_of(lv, g, c, total)
                 h = half_of(lv, g, total)
-                lhs = x_in[:, :, k * beams : (k + 1) * beams].reshape(2 * rows_in, beams)
+                lhs = x_in(k * beams, beams).reshape(2 * rows_in, beams)
                 tile = slots * beams + k * SEG // LANES * LANES
-                lhs2 = x_in[:, :, tile : tile + LANES].reshape(2 * rows_in, LANES)
+                lhs2 = x_in(tile, LANES).reshape(2 * rows_in, LANES)
                 val = jnp.dot(lhs, w1[lv, c, h], preferred_element_type=F32) + jnp.dot(
                     lhs2, w2[lv, c, g], preferred_element_type=F32
                 )
             else:
-                lhs = x_in[:, :, slots * beams :].reshape(2 * rows_in, beams)
+                lhs = x_in(slots * beams, beams).reshape(2 * rows_in, beams)
                 val = jnp.dot(lhs, ws[lv, c], preferred_element_type=F32)
             for x in range(2):
                 for t in range(beams // LANES):
@@ -643,36 +642,36 @@
                 else:
                     at = lv * 2 + c
                     sets.append(shift_setup(os_[at, 0:1, cols], os_[at, 1:2, cols], 0))
-            held = [[None, None], [None, None]]
-            step = 4
-            done = 0
-            n_out = need_rows // 8
-            while done < n_out:
-                n = min(step, n_out - done)
-                acc_re = acc_im = None
-                for c in range(2):
-                    moved = []
-                    for x in range(2):
-                        lo = 0 if done == 0 else done + 1
-                        hi = done + n + 1
-                        v = buf[c, x, t, 8 * lo : 8 * hi, :].reshape(hi - lo, 8, LANES)
-                        seqs = joined(held[c][x], spun(sets[c], v))
-                        held[c][x] = [seq[n : n + 1] for seq in seqs]
-                        moved.append(mixed(sets[c], seqs, n, False))
-                    spot = slice(8 * done, 8 * (done + n))
-                    if g < slots:
-                        fc, fs = f_main[c, g, 0, spot, cols], f_main[c, g, 1, spot, cols]
-                    else:
-                        fc, fs = f_strip[c, 0, spot, cols], f_strip[c, 1, spot, cols]
-                    fc, fs = fc.reshape(n, 8, LANES), fs.reshape(n, 8, LANES)
-                    re = fc * moved[0] - fs * moved[1]
-                    im = fs * moved[0] + fc * moved[1]
-                    acc_re = re if acc_re is None else acc_re + re
-                    acc_im = im if acc_im is None else acc_im + im
-                ocols = slice(g * beams + t * LANES, g * beams + (t + 1) * LANES)
-                out[0, 8 * done : 8 * (done + n), ocols] = acc_re.reshape(8 * n, LANES).astype(BF16)
-                out[1, 8 * done : 8 * (done + n), ocols] = acc_im.reshape(8 * n, LANES).astype(BF16)
-                done += n
+            for t0, t1 in spans:
+                held = [[None, None], [None, None]]
+                step = 4
+                done = t0
+                while done < t1:
+                    n = min(step, t1 - done)
+                    acc_re = acc_im = None
+                    for c in range(2):
+                        moved = []
+                        for x in range(2):
+                            lo = done if done == t0 else done + 1
+                            hi = done + n + 1
+                            v = buf[c, x, t, 8 * tile_at(lo) : 8 * (tile_at(hi - 1) + 1), :].reshape(hi - lo, 8, LANES)
+                            seqs = joined(held[c][x], spun(sets[c], v))
+                            held[c][x] = [seq[n : n + 1] for seq in seqs]
+                            moved.append(mixed(sets[c], seqs, n, False))
+                        spot = slice(8 * done, 8 * (done + n))
+                        if g < slots:
+                            fc, fs = f_main[c, g, 0, spot, cols], f_main[c, g, 1, spot, cols]
+                        else:
+                            fc, fs = f_strip[c, 0, spot, cols], f_strip[c, 1, spot, cols]
+                        fc, fs = fc.reshape(n, 8, LANES), fs.reshape(n, 8, LANES)
+                        re = fc * moved[0] - fs * moved[1]
+                        im = fs * moved[0] + fc * moved[1]
+                        acc_re = re if acc_re is None else acc_re + re
+                        acc_im = im if acc_im is None else acc_im + im
+                    ocols = slice(g * beams + t * LANES, g * beams + (t + 1) * LANES)
+                    out[0, 8 * done : 8 * (done + n), ocols] = acc_re.reshape(8 * n, LANES).astype(BF16)
+                    out[1, 8 * done : 8 * (done + n), ocols] = acc_im.reshape(8 * n, LANES).astype(BF16)
+                    done += n
 
 
 def last_step(slots, cells, hf, x_in, v1, v2, o2, th2, e2, buf, put):
@@ -733,20 +732,38 @@
         done += n
 
 
-def levels_kernel(slots, xt, strip, got_c, got_d, w1, w2, ws, v1, v2, o2, e0, e1, e2, es0, es1, os_, th2, p_ref, out, x2, x0, x1, inter0, inter1, buf, flat):
+def inner_rows(cells):
+    return 2 * EDGE // 16, cells // 8
+
+
+def interior_kernel(slots, xt, strip, w1, w2, ws, e0, es0, os_, p_ref, x1, inter0, inter1):
+    row, _ = tables_of(slots)
+    mains = xt.shape[2]
+    low, top = inner_rows(xt.shape[1])
+
+    def get(lane, width):
+        return xt[:, :, lane : lane + width] if lane < mains else strip[:, :, lane - mains : lane - mains + width]
+
+    level_step(slots, 2 * slots, 0, get, [(low, top)], lambda v: v - low, x1, (inter0, inter1), w1, w2, ws, e0, es0, p_ref, os_, row)
+
+
+def levels_kernel(slots, xt, strip, got_c, got_d, inner, w1, w2, ws, v1, v2, o2, e0, e1, e2, es0, es1, os_, th2, p_ref, out, x2, x0, x1, inter0, inter1, buf, flat):
     row, _ = tables_of(slots)
     total = 2 * slots
     cells = xt.shape[1]
     mains = xt.shape[2]
+    low, top = inner_rows(cells)
     for x in range(2):
-        x0[x, EDGE : EDGE + cells, :mains] = xt[x]
-        x0[x, EDGE : EDGE + cells, mains:] = strip[x]
+        for at, spot in ((EDGE, slice(0, EDGE)), (2 * EDGE, slice(cells - EDGE, cells))):
+            x0[x, at : at + EDGE, :mains] = xt[x, spot]
+            x0[x, at : at + EDGE, mains:] = strip[x, spot]
+        x1[x, 8 * low : 8 * top] = inner[x, 8 * low : 8 * top]
     even = lax.axis_index("rng") % 2 == 0
 
     def place(right, left):
         for x in range(2):
             x0[x, :EDGE, :] = left[x]
-            x0[x, EDGE + cells :, :] = right[x]
+            x0[x, 3 * EDGE :, :] = right[x]
 
     @pl.when(even)
     def _():
@@ -757,8 +774,10 @@
         place(got_d, got_c)
 
     inter = (inter0, inter1)
-    level_step(slots, total, cells, 0, x0, x1, inter, w1, w2, ws, e0, es0, p_ref, os_, row)
-    level_step(slots, total, cells, 1, x1, x2, inter, w1, w2, ws, e1, es1, p_ref, os_, row)
+    edge_tiles = EDGE // 4
+    spans = [(0, low), (top, (cells + 2 * (EDGE - HALO)) // 8)]
+    level_step(slots, total, 0, lambda lane, width: x0[:, :, lane : lane + width], spans, lambda v: v if v < edge_tiles else v - (cells + 2 * EDGE) // 8 + 2 * edge_tiles, x1, inter, w1, w2, ws, e0, es0, p_ref, os_, row)
+    level_step(slots, total, 1, lambda lane, width: x1[:, :, lane : lane + width], [(0, x2.shape[1] // 8)], lambda v: v, x2, inter, w1, w2, ws, e1, es1, p_ref, os_, row)
     hf = 1 - lax.axis_index("aper")
 
     def put(done, n, re, im):
@@ -828,29 +847,16 @@
     got_a = lax.ppermute(out_a, "ang", swap_even("ang"))
     got_b = lax.ppermute(out_b, "ang", swap_odd("ang"))
     got_base = lax.ppermute(bases, "aper", swap_even("aper"))
-    (xt,) = call(
-        functools.partial(turn_mains_kernel, slots),
-        [((2, cells, slots * beams), BF16)],
-        (subimages,),
-        flops=1_000_000,
-    )
-    strip, out_c, out_d = call(
-        functools.partial(strip_kernel, slots),
-        [((2, cells, beams), BF16)] + [((2, EDGE, (slots + 1) * beams), BF16)] * 2,
-        (got_a, got_b, subimages, xt),
-        scratch=[((2, beams, cells), BF16)],
-        flops=1000,
-    )
-    got_c = lax.ppermute(out_c, "rng", swap_even("rng"))
-    got_d = lax.ppermute(out_d, "rng", swap_odd("rng"))
 
     def main_tables(*refs):
-        ins, outs = refs[:6], refs[6:]
+        ins, xt, outs = refs[1:7], refs[7], refs[8:]
+        turn_mains_kernel(slots, refs[0], xt)
         main_tables_kernel(slots, full, *ins, *outs[:5], outs[5:])
 
-    w1, w2, v1, v2, o2, e0, e1, e2 = call(
+    xt, w1, w2, v1, v2, o2, e0, e1, e2 = call(
         main_tables,
         [
+            ((2, cells, slots * beams), BF16),
             ((LEVELS - 1, 2, 2, beams, beams), BF16),
             ((LEVELS - 1, 2, slots, LANES, beams), BF16),
             ((tiles, beams, beams), BF16),
@@ -859,9 +865,19 @@
         ]
         + [((2, slots, 2, r, beams), F32) for r in lv_rows]
         + [((1, 1, 2, cells, beams), F32)],
-        (params, beam_offsets, range_offsets, beam_taps, range_frac, phase_rate),
+        (subimages, params, beam_offsets, range_offsets, beam_taps, range_frac, phase_rate),
         flops=20_000_000,
     )
+
+    strip, out_c, out_d = call(
+        functools.partial(strip_kernel, slots),
+        [((2, cells, beams), BF16)] + [((2, EDGE, (slots + 1) * beams), BF16)] * 2,
+        (got_a, got_b, subimages, xt),
+        scratch=[((2, beams, cells), BF16)],
+        flops=1000,
+    )
+    got_c = lax.ppermute(out_c, "rng", swap_even("rng"))
+    got_d = lax.ppermute(out_d, "rng", swap_odd("rng"))
 
     def strip_tables(*refs):
         ins, outs, more = refs[:3], refs[6:], refs[3:6]
@@ -878,13 +894,20 @@
         flops=20_000_000,
     )
     wide = (slots + 1) * beams
+    (inner,) = call(
+        functools.partial(interior_kernel, slots),
+        [((2, lv_rows[0], wide), BF16)],
+        (xt, strip, w1, w2, ws, e0, es0, os_, params),
+        scratch=[((2, 2, tiles, cells, LANES), F32)] * 2,
+        flops=100_000_000,
+    )
     x_rows = cells + 2 * EDGE
     sent, x2 = call(
         functools.partial(levels_kernel, slots),
         [((2, LANES, cells), BF16), ((2, lv_rows[1], wide), BF16)],
-        (xt, strip, got_c, got_d, w1, w2, ws, v1, v2, o2, e0, e1, e2, es0, es1, os_, th2, params),
+        (xt, strip, got_c, got_d, inner, w1, w2, ws, v1, v2, o2, e0, e1, e2, es0, es1, os_, th2, params),
         scratch=[
-            ((2, x_rows, wide), BF16),
+            ((2, 4 * EDGE, wide), BF16),
             ((2, lv_rows[0], wide), BF16),
             ((2, 2, tiles, x_rows, LANES), F32),
             ((2, 2, tiles, x_rows, LANES), F32),

time: 25.1 us -> 25.4 us (1.012)
  Pallas kernels: 6.92 us -> 7.24 us
    ppermute x1, waiting for transfers between devices: 0.67 us -> 2.16 us  [fast_body(): got_base = lax.ppermute(bases, 'aper', swap_even('aper'))]
    ppermute x1, waiting for transfers between devices: 2.59 us -> 1.11 us  [fast_body(): got_b = lax.ppermute(out_b, 'ang', swap_odd('ang'))]
    pallas_call x8, Pallas kernels: 6.92 us -> 7.24 us  [call(): pl.pallas_call(kernel, out_shape=[jax.ShapeDtypeStruct(s, d) for s, d in...]
  transfers between devices with their start and end apart: 6 -> 6, of which waited for: 3 -> 3; matrix products, arithmetic and copies ran while one was open for 0% -> 0% of each run, Pallas kernels for 12% -> 17%
where the time goes in v4:
time: 25.4 us; the launch traced here: 25.2 us
  starting transfers between devices  10.8 us (43%)
  Pallas kernels  7.24 us (29%)
  waiting for transfers between devices  5.33 us (21%)
  local copies, waits for them, and re-layouts  1 us (4%)
  other arithmetic  0.67 us (3%)
    pallas_call x8, Pallas kernels, call(): pl.pallas_call(kernel, out_shape=[jax.ShapeDtypeStruct(s, d) for s, d in...  7.24 us
    ppermute x1, starting transfers between devices, fast_body(): got_d = lax.ppermute(out_d, 'rng', swap_odd('rng'))  4.6 us
    ppermute x1, starting transfers between devices, fast_body(): got_b = lax.ppermute(out_b, 'ang', swap_odd('ang'))  2.5 us
    ppermute x1, waiting for transfers between devices, fast_body(): got_base = lax.ppermute(bases, 'aper', swap_even('aper'))  2.16 us
    ppermute x1, waiting for transfers between devices, fast_body(): got = lax.ppermute(sent, 'aper', swap_even('aper'))  2.06 us
    ppermute x1, starting transfers between devices, fast_body(): got = lax.ppermute(sent, 'aper', swap_even('aper'))  1.57 us
    ppermute x1, starting transfers between devices, fast_body(): got_base = lax.ppermute(bases, 'aper', swap_even('aper'))  1.56 us
    ppermute x1, waiting for transfers between devices, fast_body(): got_b = lax.ppermute(out_b, 'ang', swap_odd('ang'))  1.11 us
  transfers between devices with their start and end apart: 6, of which 3 were waited for; matrix products, arithmetic and copies ran while one was open for 0% of the time, Pallas kernels for 17%

profile of v4, /device:TPU:12, one launch (start us, length us, event | category | flops | bytes accessed | tf_op | source)
XLA Modules:
  0.0 25.2 jit_solution(12714598154791302814)
XLA Ops:
  0.0 0.0 copy-start
  0.0 0.0 copy-start.5
  0.0 0.0 copy-start.6
  0.0 0.0 copy-start.4
  0.0 0.0 copy-start.1
  0.0 0.0 copy-start.3
  0.0 0.0 copy-start.2
  0.0 0.0 copy-start.7
  0.1 1.0 %copy-done = bf16[4,2,256,128]{3,2,1,0:T(8,128)(2,1)S(1)} copy-done((bf16[4,2,256,128]{3,2,1,0:T(8,128)(2,1)S(1)}, bf16[4,2,256,128]{3,2,1,0:T(8,128)(2,1)}, u32[]{:S(2)}) %copy-start) | copy-done | bytes 524312
  1.0 0.0 copy-done.5
  1.0 0.0 copy-done.6
  1.0 0.0 copy-done.4
  1.1 0.0 copy-done.1
  1.1 0.0 copy-done.3
  1.1 0.0 copy-done.2
  1.1 0.0 copy-done.7
  1.1 0.1 shard_map.83
  1.2 0.1 collective-permute-start
  1.3 2.5 %collective-permute-start.1 = (bf16[160,128]{1,0:T(8,128)(2,1)S(1)}, bf16[160,128]{1,0:T(8,128)(2,1)S(1)}, u32[]{:S(2)}, u32[]{:S(2)}) collective-permute-start(bf16[160,128]{1,0:T(8,128)(2,1)S(1)} %get-tuple-element.31), channel_id=1, source_target_pairs={{1,2},{2,1},{5,6},{6,5},{9,10},{10,9},{13,14},{14,13},{17,18},{18,... | collective-permute-start | bytes 122888 | tf_op jit(solution)/shard_map/ppermute | solution.py:848
  3.8 1.7 %shard_map.84 = (bf16[2,128,1024]{2,1,0:T(8,128)(2,1)S(1)}, bf16[2,2,2,256,256]{4,3,2,1,0:T(8,128)(2,1)S(1)}, bf16[2,2,4,128,256]{4,3,2,1,0:T(8,128)(2,1)S(1)}, ...) custom-call(bf16[4,2,256,128]{3,2,1,0:T(8,128)(2,1)S(1)} %copy-done,, ...), custom_call_target="tpu_custom_call" | custom-call | flops 20000000 | tf_op jit(solution)/shard_map/pallas_call | solution.py:820
  5.5 0.0 collective-permute-done.got_a.refs_0_
  5.5 1.1 %collective-permute-done.1.got_b.refs_1_ = bf16[160,128]{1,0:T(8,128)(2,1)S(1)} collective-permute-done((bf16[160,128]{1,0:T(8,128)(2,1)S(1)}, bf16[160,128]{1,0:T(8,128)(2,1)S(1)}, u32[]{:S(2)}, u32[]{:S(2)}) %collective-permute-start.1) | collective-permute-done | bytes 40992 | tf_op jit(solution)/shard_map/ppermute | solution.py:848
  6.6 0.1 shard_map.85
  6.8 0.5 %collective-permute-start.2 = (bf16[2,16,1280]{2,1,0:T(8,128)(2,1)S(1)}, bf16[2,16,1280]{2,1,0:T(8,128)(2,1)S(1)}, u32[]{:S(2)}, u32[]{:S(2)}) collective-permute-start(bf16[2,16,1280]{2,1,0:T(8,128)(2,1)S(1)} %get-tuple-element.33), channel_id=1, source_target_pairs={{0,4},{4,0},{8,12},{12,8},{1,5},{5,1},{9,13},{13,9},{2,6},{6,2},{1... | collective-permute-start | bytes 245768 | tf_op jit(solution)/shard_map/ppermute | solution.py:879
  7.3 4.6 %collective-permute-start.3 = (bf16[2,16,1280]{2,1,0:T(8,128)(2,1)S(1)}, bf16[2,16,1280]{2,1,0:T(8,128)(2,1)S(1)}, u32[]{:S(2)}, u32[]{:S(2)}) collective-permute-start(bf16[2,16,1280]{2,1,0:T(8,128)(2,1)S(1)} %get-tuple-element.34), channel_id=1, source_target_pairs={{4,8},{8,4},{5,9},{9,5},{6,10},{10,6},{7,11},{11,7},{20,24},{24,20... | collective-permute-start | bytes 245768 | tf_op jit(solution)/shard_map/ppermute | solution.py:880
  11.9 1.6 %collective-permute-start.4 = (f32[8,256]{1,0:T(8,128)S(1)}, f32[8,256]{1,0:T(8,128)S(1)}, u32[]{:S(2)}, u32[]{:S(2)}) collective-permute-start(f32[8,256]{1,0:T(8,128)S(1)} %get-tuple-element.37.refs_3_), channel_id=1, source_target_pairs={{0,16},{16,0},{1,17},{17,1},{2,18},{18,2},{3,19},{19,3},{4,20},{20... | collective-permute-start | bytes 24584 | tf_op jit(solution)/shard_map/ppermute | solution.py:849
  13.4 2.2 %collective-permute-done.4.refs_4_ = f32[8,256]{1,0:T(8,128)S(1)} collective-permute-done((f32[8,256]{1,0:T(8,128)S(1)}, f32[8,256]{1,0:T(8,128)S(1)}, u32[]{:S(2)}, u32[]{:S(2)}) %collective-permute-start.4) | collective-permute-done | bytes 8224 | tf_op jit(solution)/shard_map/ppermute | solution.py:849
  15.6 0.7 %shard_map.86 = (bf16[2,2,256,256]{3,2,1,0:T(8,128)(2,1)S(1)}, f32[2,2,160,256]{3,2,1,0:T(8,128)S(1)}, f32[2,2,144,256]{3,2,1,0:T(8,128)S(1)}, f32[4,8,256]{2,1,0:T(8,128)S(1)}, f32[2,2,4,256]{3,2,1,0:T(4,128)S(1)}) custom-call(bf16[160,128]{1,0:T(8,128)(2,1)S(1)} %collective-permute-done.got_a.refs_0_, ...), custom_call_target="tpu_custom_call" | custom-call | flops 20000000 | tf_op jit(solution)/shard_map/pallas_call | solution.py:820
  16.3 1.3 %shard_map.87.inner = bf16[2,160,1280]{2,1,0:T(8,128)(2,1)S(1)} custom-call(bf16[2,128,1024]{2,1,0:T(8,128)(2,1)S(1)} %get-tuple-element.29.xt, bf16[2,128,256]{2,1,0:T(8,128)(2,1)S(1)} %get-tuple-element.32.strip, bf16[2,2,2,256,256]{4,3,2,1,0:T(8,128)(2,1)S(1)} %get-tuple-element.35.w1, bf16[2,2,4,128,256]{4,3,2,1,0:T(8,128)(2,1)S(1)} %get-tuple-element.36.w2, ...), custom_call_target="tpu_custom_call" | custom-call | flops 100000000 | tf_op jit(solution)/shard_map/pallas_call | solution.py:820
  17.6 0.0 collective-permute-done.2.got_c
  17.6 0.0 collective-permute-done.3.got_d
  17.6 2.6 %shard_map.88 = (bf16[2,128,128]{2,1,0:T(8,128)(2,1)S(1)}, bf16[2,144,1280]{2,1,0:T(8,128)(2,1)S(1)}) custom-call(bf16[2,128,1024]{2,1,0:T(8,128)(2,1)S(1)} %get-tuple-element.29.xt, bf16[2,128,256]{2,1,0:T(8,128)(2,1)S(1)} %get-tuple-element.32.strip, bf16[2,16,1280]{2,1,0:T(8,128)(2,1)S(1)} %collective-permute-done.2.got_c, ...), custom_call_target="tpu_custom_call" | custom-call | flops 200000000 | tf_op jit(solution)/shard_map/pallas_call | solution.py:820
  20.2 1.6 %collective-permute-start.5 = (bf16[2,128,128]{2,1,0:T(8,128)(2,1)S(1)}, bf16[2,128,128]{2,1,0:T(8,128)(2,1)S(1)}, u32[]{:S(2)}, u32[]{:S(2)}) collective-permute-start(bf16[2,128,128]{2,1,0:T(8,128)(2,1)S(1)} %get-tuple-element.50), channel_id=1, source_target_pairs={{0,16},{16,0},{1,17},{17,1},{2,18},{18,2},{3,19},{19,3},{4,20},{20... | collective-permute-start | bytes 196616 | tf_op jit(solution)/shard_map/ppermute | solution.py:919
  21.8 0.7 %shard_map.89 = f32[2,128,128]{2,1,0:T(8,128)S(1)} custom-call(bf16[2,144,1280]{2,1,0:T(8,128)(2,1)S(1)} %get-tuple-element.49.x2, bf16[2,256,256]{2,1,0:T(8,128)(2,1)S(1)} %get-tuple-element.42.v1, bf16[2,2,128,256]{3,2,1,0:T(8,128)(2,1)S(1)} %get-tuple-element.43.v2, f32[2,8,256]{2,1,0:T(8,128)S(1)} %get-tuple-element.44.o2, ...), custom_call_target="tpu_custom_call" | custom-call | flops 20000000 | tf_op jit(solution)/shard_map/pallas_call | solution.py:820
  22.5 2.1 %collective-permute-done.5 = bf16[2,128,128]{2,1,0:T(8,128)(2,1)S(1)} collective-permute-done((bf16[2,128,128]{2,1,0:T(8,128)(2,1)S(1)}, bf16[2,128,128]{2,1,0:T(8,128)(2,1)S(1)}, u32[]{:S(2)}, u32[]{:S(2)}) %collective-permute-start.5) | collective-permute-done | bytes 65568 | tf_op jit(solution)/shard_map/ppermute | solution.py:919
  24.6 0.7 %add_bitcast_fusion = f32[2,1,128,128]{3,2,1,0:T(8,128)} fusion(f32[2,128,128]{2,1,0:T(8,128)S(1)} %shard_map.89, bf16[2,128,128]{2,1,0:T(8,128)(2,1)S(1)} %collective-permute-done.5), kind=kLoop, calls=%fused_computation | loop fusion | flops 65536 | bytes 327680 | tf_op jit(solution)/shard_map/broadcast_in_dim | solution.py:927
  (1 shorter events, 0.0 us)
Async XLA Ops:
  0.0 1.0 %copy-start = (bf16[4,2,256,128]{3,2,1,0:T(8,128)(2,1)S(1)}, bf16[4,2,256,128]{3,2,1,0:T(8,128)(2,1)}, u32[]{:S(2)}) copy-start(bf16[4,2,256,128]{3,2,1,0:T(8,128)(2,1)} %sub.3) | copy-start | bytes 1572868
  0.0 1.0 %copy-start.5 = (f32[8,256]{1,0:T(8,128)S(1)}, f32[8,256]{1,0:T(8,128)}, u32[]{:S(2)}) copy-start(f32[8,256]{1,0:T(8,128)} %refs_5_.3) | copy-start | bytes 24580
  0.0 1.0 %copy-start.6 = (f32[3,2,256]{2,1,0:T(2,128)S(1)}, f32[3,2,256]{2,1,0:T(2,128)}, u32[]{:S(2)}) copy-start(f32[3,2,256]{2,1,0:T(2,128)} %refs_6_.1) | copy-start | bytes 18436
  0.0 1.0 %copy-start.4 = (f32[3,2,2,256]{3,2,1,0:T(2,128)S(1)}, f32[3,2,2,256]{3,2,1,0:T(2,128)}, u32[]{:S(2)}) copy-start(f32[3,2,2,256]{3,2,1,0:T(2,128)} %refs_5_.2) | copy-start | bytes 36868
  0.0 1.0 %copy-start.1 = (bf16[3,2,2,4,256]{4,3,2,1,0:T(4,128)(2,1)S(1)}, bf16[3,2,2,4,256]{4,3,2,1,0:T(4,128)(2,1)}, u32[]{:S(2)}) copy-start(bf16[3,2,2,4,256]{4,3,2,1,0:T(4,128)(2,1)} %refs_4_.1) | copy-start | bytes 73732
  0.0 1.0 %copy-start.3 = (s32[3,2,2,256]{3,2,1,0:T(2,128)S(1)}, s32[3,2,2,256]{3,2,1,0:T(2,128)}, u32[]{:S(2)}) copy-start(s32[3,2,2,256]{3,2,1,0:T(2,128)} %refs_3_.1) | copy-start | bytes 36868
  0.0 1.0 %copy-start.2 = (s32[3,2,2,256]{3,2,1,0:T(2,128)S(1)}, s32[3,2,2,256]{3,2,1,0:T(2,128)}, u32[]{:S(2)}) copy-start(s32[3,2,2,256]{3,2,1,0:T(2,128)} %refs_2_.1) | copy-start | bytes 36868
  0.0 1.0 %copy-start.7 = (f32[4,3,2,256]{3,2,1,0:T(2,128)S(1)}, f32[4,3,2,256]{3,2,1,0:T(2,128)}, u32[]{:S(2)}) copy-start(f32[4,3,2,256]{3,2,1,0:T(2,128)} %pb.1) | copy-start | bytes 73732
  1.2 4.3 %collective-permute-start = (bf16[160,128]{1,0:T(8,128)(2,1)S(1)}, bf16[160,128]{1,0:T(8,128)(2,1)S(1)}, u32[]{:S(2)}, u32[]{:S(2)}) collective-permute-start(bf16[160,128]{1,0:T(8,128)(2,1)S(1)} %get-tuple-element.30), channel_id=1, source_target_pairs={{0,1},{1,0},{2,3},{3,2},{4,5},{5,4},{6,7},{7,6},{8,9},{9,8},{10,11... | collective-permute-start | bytes 122888 | tf_op jit(solution)/shard_map/ppermute | solution.py:847
  1.3 5.3 %collective-permute-start.1 = (bf16[160,128]{1,0:T(8,128)(2,1)S(1)}, bf16[160,128]{1,0:T(8,128)(2,1)S(1)}, u32[]{:S(2)}, u32[]{:S(2)}) collective-permute-start(bf16[160,128]{1,0:T(8,128)(2,1)S(1)} %get-tuple-element.31), channel_id=1, source_target_pairs={{1,2},{2,1},{5,6},{6,5},{9,10},{10,9},{13,14},{14,13},{17,18},{18,... | collective-permute-start | bytes 122888 | tf_op jit(solution)/shard_map/ppermute | solution.py:848
  6.8 10.9 %collective-permute-start.2 = (bf16[2,16,1280]{2,1,0:T(8,128)(2,1)S(1)}, bf16[2,16,1280]{2,1,0:T(8,128)(2,1)S(1)}, u32[]{:S(2)}, u32[]{:S(2)}) collective-permute-start(bf16[2,16,1280]{2,1,0:T(8,128)(2,1)S(1)} %get-tuple-element.33), channel_id=1, source_target_pairs={{0,4},{4,0},{8,12},{12,8},{1,5},{5,1},{9,13},{13,9},{2,6},{6,2},{1... | collective-permute-start | bytes 245768 | tf_op jit(solution)/shard_map/ppermute | solution.py:879
  7.3 10.4 %collective-permute-start.3 = (bf16[2,16,1280]{2,1,0:T(8,128)(2,1)S(1)}, bf16[2,16,1280]{2,1,0:T(8,128)(2,1)S(1)}, u32[]{:S(2)}, u32[]{:S(2)}) collective-permute-start(bf16[2,16,1280]{2,1,0:T(8,128)(2,1)S(1)} %get-tuple-element.34), channel_id=1, source_target_pairs={{4,8},{8,4},{5,9},{9,5},{6,10},{10,6},{7,11},{11,7},{20,24},{24,20... | collective-permute-start | bytes 245768 | tf_op jit(solution)/shard_map/ppermute | solution.py:880
  11.9 3.7 %collective-permute-start.4 = (f32[8,256]{1,0:T(8,128)S(1)}, f32[8,256]{1,0:T(8,128)S(1)}, u32[]{:S(2)}, u32[]{:S(2)}) collective-permute-start(f32[8,256]{1,0:T(8,128)S(1)} %get-tuple-element.37.refs_3_), channel_id=1, source_target_pairs={{0,16},{16,0},{1,17},{17,1},{2,18},{18,2},{3,19},{19,3},{4,20},{20... | collective-permute-start | bytes 24584 | tf_op jit(solution)/shard_map/ppermute | solution.py:849
  20.2 4.3 %collective-permute-start.5 = (bf16[2,128,128]{2,1,0:T(8,128)(2,1)S(1)}, bf16[2,128,128]{2,1,0:T(8,128)(2,1)S(1)}, u32[]{:S(2)}, u32[]{:S(2)}) collective-permute-start(bf16[2,128,128]{2,1,0:T(8,128)(2,1)S(1)} %get-tuple-element.50), channel_id=1, source_target_pairs={{0,16},{16,0},{1,17},{17,1},{2,18},{18,2},{3,19},{19,3},{4,20},{20... | collective-permute-start | bytes 196616 | tf_op jit(solution)/shard_map/ppermute | solution.py:919

commit v5 on v4

--- a/solution.py
+++ b/solution.py
@@ -158,7 +158,8 @@
 F32 = jnp.float32
 BF16 = jnp.bfloat16
 LANES = 128
-EDGE = -(-HALO * LEVELS // 16) * 16
+REACH = HALO * LEVELS
+EDGE = -(-REACH // 16) * 16
 SEG = 4 * EDGE
 FIELDS = 3 + TAPS
 VMEM_LIMIT = 24 * 1024 * 1024
@@ -459,10 +460,11 @@
 
     def send(first, last):
         for x in range(2):
-            first[x, :, :mains] = xt[x, cells - EDGE :, :]
-            first[x, :, mains:] = strip[x, cells - EDGE :, :]
-            last[x, :, :mains] = xt[x, :EDGE, :]
-            last[x, :, mains:] = strip[x, :EDGE, :]
+            spot = slice(x * REACH, (x + 1) * REACH)
+            first[spot, :mains] = xt[x, cells - REACH :, :]
+            first[spot, mains:] = strip[x, cells - REACH :, :]
+            last[spot, :mains] = xt[x, :REACH, :]
+            last[spot, mains:] = strip[x, :REACH, :]
 
     even_r = lax.axis_index("rng") % 2 == 0
 
@@ -736,7 +738,7 @@
     return 2 * EDGE // 16, cells // 8
 
 
-def interior_kernel(slots, xt, strip, w1, w2, ws, e0, es0, os_, p_ref, x1, inter0, inter1):
+def interior_kernel(slots, xt, strip, w1, w2, ws, e0, es0, e1, es1, os_, p_ref, x1, x2, inter0, inter1):
     row, _ = tables_of(slots)
     mains = xt.shape[2]
     low, top = inner_rows(xt.shape[1])
@@ -746,8 +748,13 @@
 
     level_step(slots, 2 * slots, 0, get, [(low, top)], lambda v: v - low, x1, (inter0, inter1), w1, w2, ws, e0, es0, p_ref, os_, row)
 
-
-def levels_kernel(slots, xt, strip, got_c, got_d, inner, w1, w2, ws, v1, v2, o2, e0, e1, e2, es0, es1, os_, th2, p_ref, out, x2, x0, x1, inter0, inter1, buf, flat):
+    def again(lane, width):
+        return x1[:, 8 * low : 8 * top, lane : lane + width]
+
+    level_step(slots, 2 * slots, 1, again, [(low, top - 2)], lambda v: v - low, x2, (inter0, inter1), w1, w2, ws, e1, es1, p_ref, os_, row)
+
+
+def levels_kernel(slots, xt, strip, got_c, got_d, inner, inner2, w1, w2, ws, v1, v2, o2, e0, e1, e2, es0, es1, os_, th2, p_ref, out, x2, x0, x1, inter0, inter1, buf, flat):
     row, _ = tables_of(slots)
     total = 2 * slots
     cells = xt.shape[1]
@@ -757,13 +764,18 @@
         for at, spot in ((EDGE, slice(0, EDGE)), (2 * EDGE, slice(cells - EDGE, cells))):
             x0[x, at : at + EDGE, :mains] = xt[x, spot]
             x0[x, at : at + EDGE, mains:] = strip[x, spot]
-        x1[x, 8 * low : 8 * top] = inner[x, 8 * low : 8 * top]
+        x1[x, 8 * low : 8 * low + 16] = inner[x, 8 * low : 8 * low + 16]
+        x1[x, 8 * top - 16 : 8 * top] = inner[x, 8 * top - 16 : 8 * top]
+        x2[x, 8 * low : 8 * top - 16] = inner2[x, 8 * low : 8 * top - 16]
+        for at in (0, 3 * EDGE):
+            x0[x, at : at + EDGE, :] = jnp.zeros((EDGE, x0.shape[2]), BF16)
     even = lax.axis_index("rng") % 2 == 0
 
     def place(right, left):
         for x in range(2):
-            x0[x, :EDGE, :] = left[x]
-            x0[x, 3 * EDGE :, :] = right[x]
+            spot = slice(x * REACH, (x + 1) * REACH)
+            x0[x, EDGE - REACH : EDGE, :] = left[spot]
+            x0[x, 3 * EDGE : 3 * EDGE + REACH, :] = right[spot]
 
     @pl.when(even)
     def _():
@@ -777,7 +789,14 @@
     edge_tiles = EDGE // 4
     spans = [(0, low), (top, (cells + 2 * (EDGE - HALO)) // 8)]
     level_step(slots, total, 0, lambda lane, width: x0[:, :, lane : lane + width], spans, lambda v: v if v < edge_tiles else v - (cells + 2 * EDGE) // 8 + 2 * edge_tiles, x1, inter, w1, w2, ws, e0, es0, p_ref, os_, row)
-    level_step(slots, total, 1, lambda lane, width: x1[:, :, lane : lane + width], [(0, x2.shape[1] // 8)], lambda v: v, x2, inter, w1, w2, ws, e1, es1, p_ref, os_, row)
+    first, last = 8 * low + 16, 8 * top - 16
+
+    def ends(lane, width):
+        lanes = slice(lane, lane + width)
+        return jnp.concatenate([x1[:, :first, lanes], x1[:, last:, lanes]], 1)
+
+    spans = [(0, low), (top - 2, x2.shape[1] // 8)]
+    level_step(slots, total, 1, ends, spans, lambda v: v if v < first // 8 else v - (last - first) // 8, x2, inter, w1, w2, ws, e1, es1, p_ref, os_, row)
     hf = 1 - lax.axis_index("aper")
 
     def put(done, n, re, im):
@@ -871,7 +890,7 @@
 
     strip, out_c, out_d = call(
         functools.partial(strip_kernel, slots),
-        [((2, cells, beams), BF16)] + [((2, EDGE, (slots + 1) * beams), BF16)] * 2,
+        [((2, cells, beams), BF16)] + [((2 * REACH, (slots + 1) * beams), BF16)] * 2,
         (got_a, got_b, subimages, xt),
         scratch=[((2, beams, cells), BF16)],
         flops=1000,
@@ -894,10 +913,10 @@
         flops=20_000_000,
     )
     wide = (slots + 1) * beams
-    (inner,) = call(
+    inner, inner2 = call(
         functools.partial(interior_kernel, slots),
-        [((2, lv_rows[0], wide), BF16)],
-        (xt, strip, w1, w2, ws, e0, es0, os_, params),
+        [((2, lv_rows[0], wide), BF16), ((2, lv_rows[1], wide), BF16)],
+        (xt, strip, w1, w2, ws, e0, es0, e1, es1, os_, params),
         scratch=[((2, 2, tiles, cells, LANES), F32)] * 2,
         flops=100_000_000,
     )
@@ -905,7 +924,7 @@
     sent, x2 = call(
         functools.partial(levels_kernel, slots),
         [((2, LANES, cells), BF16), ((2, lv_rows[1], wide), BF16)],
-        (xt, strip, got_c, got_d, inner, w1, w2, ws, v1, v2, o2, e0, e1, e2, es0, es1, os_, th2, params),
+        (xt, strip, got_c, got_d, inner, inner2, w1, w2, ws, v1, v2, o2, e0, e1, e2, es0, es1, os_, th2, params),
         scratch=[
             ((2, 4 * EDGE, wide), BF16),
             ((2, lv_rows[0], wide), BF16),

time: 25.4 us -> 25.8 us (1.016)
  Pallas kernels: 7.24 us -> 7.7 us
    pallas_call x8, Pallas kernels: 7.24 us -> 7.7 us  [call(): pl.pallas_call(kernel, out_shape=[jax.ShapeDtypeStruct(s, d) for s, d in...]
  transfers between devices with their start and end apart: 6 -> 6, of which waited for: 3 -> 3; matrix products, arithmetic and copies ran while one was open for 0% -> 0% of each run, Pallas kernels for 17% -> 22%
where the time goes in v5:
time: 25.8 us; the launch traced here: 25.7 us
  starting transfers between devices  10.8 us (42%)
  Pallas kernels  7.7 us (30%)
  waiting for transfers between devices  5.34 us (21%)
  local copies, waits for them, and re-layouts  1 us (4%)
  other arithmetic  0.67 us (3%)
    pallas_call x8, Pallas kernels, call(): pl.pallas_call(kernel, out_shape=[jax.ShapeDtypeStruct(s, d) for s, d in...  7.7 us
    ppermute x1, starting transfers between devices, fast_body(): got_d = lax.ppermute(out_d, 'rng', swap_odd('rng'))  4.61 us
    ppermute x1, starting transfers between devices, fast_body(): got_b = lax.ppermute(out_b, 'ang', swap_odd('ang'))  2.5 us
    ppermute x1, waiting for transfers between devices, fast_body(): got_base = lax.ppermute(bases, 'aper', swap_even('aper'))  2.16 us
    ppermute x1, waiting for transfers between devices, fast_body(): got = lax.ppermute(sent, 'aper', swap_even('aper'))  2.06 us
    ppermute x1, starting transfers between devices, fast_body(): got = lax.ppermute(sent, 'aper', swap_even('aper'))  1.56 us
    ppermute x1, starting transfers between devices, fast_body(): got_base = lax.ppermute(bases, 'aper', swap_even('aper'))  1.56 us
    ppermute x1, waiting for transfers between devices, fast_body(): got_b = lax.ppermute(out_b, 'ang', swap_odd('ang'))  1.11 us
  transfers between devices with their start and end apart: 6, of which 3 were waited for; matrix products, arithmetic and copies ran while one was open for 0% of the time, Pallas kernels for 22%

profile of v5, /device:TPU:12, one launch (start us, length us, event | category | flops | bytes accessed | tf_op | source)
XLA Modules:
  0.0 25.7 jit_solution(7289887920496957700)
XLA Ops:
  0.0 0.0 copy-start
  0.0 0.0 copy-start.5
  0.0 0.0 copy-start.6
  0.0 0.0 copy-start.4
  0.0 0.0 copy-start.1
  0.0 0.0 copy-start.3
  0.0 0.0 copy-start.2
  0.0 0.0 copy-start.7
  0.1 1.0 %copy-done = bf16[4,2,256,128]{3,2,1,0:T(8,128)(2,1)S(1)} copy-done((bf16[4,2,256,128]{3,2,1,0:T(8,128)(2,1)S(1)}, bf16[4,2,256,128]{3,2,1,0:T(8,128)(2,1)}, u32[]{:S(2)}) %copy-start) | copy-done | bytes 524312
  1.0 0.0 copy-done.5
  1.0 0.0 copy-done.6
  1.0 0.0 copy-done.4
  1.1 0.0 copy-done.1
  1.1 0.0 copy-done.3
  1.1 0.0 copy-done.2
  1.1 0.0 copy-done.7
  1.1 0.1 shard_map.83
  1.2 0.1 collective-permute-start
  1.3 2.5 %collective-permute-start.1 = (bf16[160,128]{1,0:T(8,128)(2,1)S(1)}, bf16[160,128]{1,0:T(8,128)(2,1)S(1)}, u32[]{:S(2)}, u32[]{:S(2)}) collective-permute-start(bf16[160,128]{1,0:T(8,128)(2,1)S(1)} %get-tuple-element.33), channel_id=1, source_target_pairs={{1,2},{2,1},{5,6},{6,5},{9,10},{10,9},{13,14},{14,13},{17,18},{18,... | collective-permute-start | bytes 122888 | tf_op jit(solution)/shard_map/ppermute | solution.py:867
  3.8 1.7 %shard_map.84 = (bf16[2,128,1024]{2,1,0:T(8,128)(2,1)S(1)}, bf16[2,2,2,256,256]{4,3,2,1,0:T(8,128)(2,1)S(1)}, bf16[2,2,4,128,256]{4,3,2,1,0:T(8,128)(2,1)S(1)}, ...) custom-call(bf16[4,2,256,128]{3,2,1,0:T(8,128)(2,1)S(1)} %copy-done,, ...), custom_call_target="tpu_custom_call" | custom-call | flops 20000000 | tf_op jit(solution)/shard_map/pallas_call | solution.py:839
  5.5 0.0 collective-permute-done.got_a.refs_0_
  5.5 1.1 %collective-permute-done.1.got_b.refs_1_ = bf16[160,128]{1,0:T(8,128)(2,1)S(1)} collective-permute-done((bf16[160,128]{1,0:T(8,128)(2,1)S(1)}, bf16[160,128]{1,0:T(8,128)(2,1)S(1)}, u32[]{:S(2)}, u32[]{:S(2)}) %collective-permute-start.1) | collective-permute-done | bytes 40992 | tf_op jit(solution)/shard_map/ppermute | solution.py:867
  6.6 0.1 shard_map.85
  6.8 0.5 %collective-permute-start.2 = (bf16[24,1280]{1,0:T(8,128)(2,1)S(1)}, bf16[24,1280]{1,0:T(8,128)(2,1)S(1)}, u32[]{:S(2)}, u32[]{:S(2)}) collective-permute-start(bf16[24,1280]{1,0:T(8,128)(2,1)S(1)} %get-tuple-element.35), channel_id=1, source_target_pairs={{0,4},{4,0},{8,12},{12,8},{1,5},{5,1},{9,13},{13,9},{2,6},{6,2},{1... | collective-permute-start | bytes 184328 | tf_op jit(solution)/shard_map/ppermute | solution.py:898
  7.3 4.6 %collective-permute-start.3 = (bf16[24,1280]{1,0:T(8,128)(2,1)S(1)}, bf16[24,1280]{1,0:T(8,128)(2,1)S(1)}, u32[]{:S(2)}, u32[]{:S(2)}) collective-permute-start(bf16[24,1280]{1,0:T(8,128)(2,1)S(1)} %get-tuple-element.36), channel_id=1, source_target_pairs={{4,8},{8,4},{5,9},{9,5},{6,10},{10,6},{7,11},{11,7},{20,24},{24,20... | collective-permute-start | bytes 184328 | tf_op jit(solution)/shard_map/ppermute | solution.py:899
  11.9 1.6 %collective-permute-start.4 = (f32[8,256]{1,0:T(8,128)S(1)}, f32[8,256]{1,0:T(8,128)S(1)}, u32[]{:S(2)}, u32[]{:S(2)}) collective-permute-start(f32[8,256]{1,0:T(8,128)S(1)} %get-tuple-element.39.refs_3_), channel_id=1, source_target_pairs={{0,16},{16,0},{1,17},{17,1},{2,18},{18,2},{3,19},{19,3},{4,20},{20... | collective-permute-start | bytes 24584 | tf_op jit(solution)/shard_map/ppermute | solution.py:868
  13.4 2.2 %collective-permute-done.4.refs_4_ = f32[8,256]{1,0:T(8,128)S(1)} collective-permute-done((f32[8,256]{1,0:T(8,128)S(1)}, f32[8,256]{1,0:T(8,128)S(1)}, u32[]{:S(2)}, u32[]{:S(2)}) %collective-permute-start.4) | collective-permute-done | bytes 8224 | tf_op jit(solution)/shard_map/ppermute | solution.py:868
  15.6 0.7 %shard_map.86 = (bf16[2,2,256,256]{3,2,1,0:T(8,128)(2,1)S(1)}, f32[2,2,160,256]{3,2,1,0:T(8,128)S(1)}, f32[2,2,144,256]{3,2,1,0:T(8,128)S(1)}, f32[4,8,256]{2,1,0:T(8,128)S(1)}, f32[2,2,4,256]{3,2,1,0:T(4,128)S(1)}) custom-call(bf16[160,128]{1,0:T(8,128)(2,1)S(1)} %collective-permute-done.got_a.refs_0_, ...), custom_call_target="tpu_custom_call" | custom-call | flops 20000000 | tf_op jit(solution)/shard_map/pallas_call | solution.py:839
  16.3 2.5 %shard_map.87 = (bf16[2,160,1280]{2,1,0:T(8,128)(2,1)S(1)}, bf16[2,144,1280]{2,1,0:T(8,128)(2,1)S(1)}) custom-call(bf16[2,128,1024]{2,1,0:T(8,128)(2,1)S(1)} %get-tuple-element.31.xt, bf16[2,128,256]{2,1,0:T(8,128)(2,1)S(1)} %get-tuple-element.34.strip, bf16[2,2,2,256,256]{4,3,2,1,0:T(8,128)(2,1)S(1)} %get-tuple-element.37.w1, ...), custom_call_target="tpu_custom_call" | custom-call | flops 100000000 | tf_op jit(solution)/shard_map/pallas_call | solution.py:839
  18.8 0.0 collective-permute-done.2.got_c
  18.8 0.0 collective-permute-done.3.got_d
  18.8 1.9 %shard_map.88 = (bf16[2,128,128]{2,1,0:T(8,128)(2,1)S(1)}, bf16[2,144,1280]{2,1,0:T(8,128)(2,1)S(1)}) custom-call(bf16[2,128,1024]{2,1,0:T(8,128)(2,1)S(1)} %get-tuple-element.31.xt, bf16[2,128,256]{2,1,0:T(8,128)(2,1)S(1)} %get-tuple-element.34.strip, bf16[24,1280]{1,0:T(8,128)(2,1)S(1)} %collective-permute-done.2.got_c, ...), custom_call_target="tpu_custom_call" | custom-call | flops 200000000 | tf_op jit(solution)/shard_map/pallas_call | solution.py:839
  20.7 1.6 %collective-permute-start.5 = (bf16[2,128,128]{2,1,0:T(8,128)(2,1)S(1)}, bf16[2,128,128]{2,1,0:T(8,128)(2,1)S(1)}, u32[]{:S(2)}, u32[]{:S(2)}) collective-permute-start(bf16[2,128,128]{2,1,0:T(8,128)(2,1)S(1)} %get-tuple-element.54), channel_id=1, source_target_pairs={{0,16},{16,0},{1,17},{17,1},{2,18},{18,2},{3,19},{19,3},{4,20},{20... | collective-permute-start | bytes 196616 | tf_op jit(solution)/shard_map/ppermute | solution.py:938
  22.2 0.7 %shard_map.89 = f32[2,128,128]{2,1,0:T(8,128)S(1)} custom-call(bf16[2,144,1280]{2,1,0:T(8,128)(2,1)S(1)} %get-tuple-element.53.x2, bf16[2,256,256]{2,1,0:T(8,128)(2,1)S(1)} %get-tuple-element.48.v1, bf16[2,2,128,256]{3,2,1,0:T(8,128)(2,1)S(1)} %get-tuple-element.49.v2, f32[2,8,256]{2,1,0:T(8,128)S(1)} %get-tuple-element.50.o2, ...), custom_call_target="tpu_custom_call" | custom-call | flops 20000000 | tf_op jit(solution)/shard_map/pallas_call | solution.py:839
  23.0 2.1 %collective-permute-done.5 = bf16[2,128,128]{2,1,0:T(8,128)(2,1)S(1)} collective-permute-done((bf16[2,128,128]{2,1,0:T(8,128)(2,1)S(1)}, bf16[2,128,128]{2,1,0:T(8,128)(2,1)S(1)}, u32[]{:S(2)}, u32[]{:S(2)}) %collective-permute-start.5) | collective-permute-done | bytes 65568 | tf_op jit(solution)/shard_map/ppermute | solution.py:938
  25.0 0.7 %add_bitcast_fusion = f32[2,1,128,128]{3,2,1,0:T(8,128)} fusion(f32[2,128,128]{2,1,0:T(8,128)S(1)} %shard_map.89, bf16[2,128,128]{2,1,0:T(8,128)(2,1)S(1)} %collective-permute-done.5), kind=kLoop, calls=%fused_computation | loop fusion | flops 65536 | bytes 327680 | tf_op jit(solution)/shard_map/broadcast_in_dim | solution.py:946
  (1 shorter events, 0.0 us)
Async XLA Ops:
  0.0 1.0 %copy-start = (bf16[4,2,256,128]{3,2,1,0:T(8,128)(2,1)S(1)}, bf16[4,2,256,128]{3,2,1,0:T(8,128)(2,1)}, u32[]{:S(2)}) copy-start(bf16[4,2,256,128]{3,2,1,0:T(8,128)(2,1)} %sub.3) | copy-start | bytes 1572868
  0.0 1.0 %copy-start.5 = (f32[8,256]{1,0:T(8,128)S(1)}, f32[8,256]{1,0:T(8,128)}, u32[]{:S(2)}) copy-start(f32[8,256]{1,0:T(8,128)} %refs_5_.3) | copy-start | bytes 24580
  0.0 1.0 %copy-start.6 = (f32[3,2,256]{2,1,0:T(2,128)S(1)}, f32[3,2,256]{2,1,0:T(2,128)}, u32[]{:S(2)}) copy-start(f32[3,2,256]{2,1,0:T(2,128)} %refs_6_.1) | copy-start | bytes 18436
  0.0 1.0 %copy-start.4 = (f32[3,2,2,256]{3,2,1,0:T(2,128)S(1)}, f32[3,2,2,256]{3,2,1,0:T(2,128)}, u32[]{:S(2)}) copy-start(f32[3,2,2,256]{3,2,1,0:T(2,128)} %refs_5_.2) | copy-start | bytes 36868
  0.0 1.0 %copy-start.1 = (bf16[3,2,2,4,256]{4,3,2,1,0:T(4,128)(2,1)S(1)}, bf16[3,2,2,4,256]{4,3,2,1,0:T(4,128)(2,1)}, u32[]{:S(2)}) copy-start(bf16[3,2,2,4,256]{4,3,2,1,0:T(4,128)(2,1)} %refs_4_.1) | copy-start | bytes 73732
  0.0 1.0 %copy-start.3 = (s32[3,2,2,256]{3,2,1,0:T(2,128)S(1)}, s32[3,2,2,256]{3,2,1,0:T(2,128)}, u32[]{:S(2)}) copy-start(s32[3,2,2,256]{3,2,1,0:T(2,128)} %refs_3_.1) | copy-start | bytes 36868
  0.0 1.0 %copy-start.2 = (s32[3,2,2,256]{3,2,1,0:T(2,128)S(1)}, s32[3,2,2,256]{3,2,1,0:T(2,128)}, u32[]{:S(2)}) copy-start(s32[3,2,2,256]{3,2,1,0:T(2,128)} %refs_2_.1) | copy-start | bytes 36868
  0.0 1.0 %copy-start.7 = (f32[4,3,2,256]{3,2,1,0:T(2,128)S(1)}, f32[4,3,2,256]{3,2,1,0:T(2,128)}, u32[]{:S(2)}) copy-start(f32[4,3,2,256]{3,2,1,0:T(2,128)} %pb.1) | copy-start | bytes 73732
  1.2 4.3 %collective-permute-start = (bf16[160,128]{1,0:T(8,128)(2,1)S(1)}, bf16[160,128]{1,0:T(8,128)(2,1)S(1)}, u32[]{:S(2)}, u32[]{:S(2)}) collective-permute-start(bf16[160,128]{1,0:T(8,128)(2,1)S(1)} %get-tuple-element.32), channel_id=1, source_target_pairs={{0,1},{1,0},{2,3},{3,2},{4,5},{5,4},{6,7},{7,6},{8,9},{9,8},{10,11... | collective-permute-start | bytes 122888 | tf_op jit(solution)/shard_map/ppermute | solution.py:866
  1.3 5.3 %collective-permute-start.1 = (bf16[160,128]{1,0:T(8,128)(2,1)S(1)}, bf16[160,128]{1,0:T(8,128)(2,1)S(1)}, u32[]{:S(2)}, u32[]{:S(2)}) collective-permute-start(bf16[160,128]{1,0:T(8,128)(2,1)S(1)} %get-tuple-element.33), channel_id=1, source_target_pairs={{1,2},{2,1},{5,6},{6,5},{9,10},{10,9},{13,14},{14,13},{17,18},{18,... | collective-permute-start | bytes 122888 | tf_op jit(solution)/shard_map/ppermute | solution.py:867
  6.8 12.0 %collective-permute-start.2 = (bf16[24,1280]{1,0:T(8,128)(2,1)S(1)}, bf16[24,1280]{1,0:T(8,128)(2,1)S(1)}, u32[]{:S(2)}, u32[]{:S(2)}) collective-permute-start(bf16[24,1280]{1,0:T(8,128)(2,1)S(1)} %get-tuple-element.35), channel_id=1, source_target_pairs={{0,4},{4,0},{8,12},{12,8},{1,5},{5,1},{9,13},{13,9},{2,6},{6,2},{1... | collective-permute-start | bytes 184328 | tf_op jit(solution)/shard_map/ppermute | solution.py:898
  7.3 11.5 %collective-permute-start.3 = (bf16[24,1280]{1,0:T(8,128)(2,1)S(1)}, bf16[24,1280]{1,0:T(8,128)(2,1)S(1)}, u32[]{:S(2)}, u32[]{:S(2)}) collective-permute-start(bf16[24,1280]{1,0:T(8,128)(2,1)S(1)} %get-tuple-element.36), channel_id=1, source_target_pairs={{4,8},{8,4},{5,9},{9,5},{6,10},{10,6},{7,11},{11,7},{20,24},{24,20... | collective-permute-start | bytes 184328 | tf_op jit(solution)/shard_map/ppermute | solution.py:899
  11.9 3.7 %collective-permute-start.4 = (f32[8,256]{1,0:T(8,128)S(1)}, f32[8,256]{1,0:T(8,128)S(1)}, u32[]{:S(2)}, u32[]{:S(2)}) collective-permute-start(f32[8,256]{1,0:T(8,128)S(1)} %get-tuple-element.39.refs_3_), channel_id=1, source_target_pairs={{0,16},{16,0},{1,17},{17,1},{2,18},{18,2},{3,19},{19,3},{4,20},{20... | collective-permute-start | bytes 24584 | tf_op jit(solution)/shard_map/ppermute | solution.py:868
  20.7 4.3 %collective-permute-start.5 = (bf16[2,128,128]{2,1,0:T(8,128)(2,1)S(1)}, bf16[2,128,128]{2,1,0:T(8,128)(2,1)S(1)}, u32[]{:S(2)}, u32[]{:S(2)}) collective-permute-start(bf16[2,128,128]{2,1,0:T(8,128)(2,1)S(1)} %get-tuple-element.54), channel_id=1, source_target_pairs={{0,16},{16,0},{1,17},{17,1},{2,18},{18,2},{3,19},{19,3},{4,20},{20... | collective-permute-start | bytes 196616 | tf_op jit(solution)/shard_map/ppermute | solution.py:938
